TPU v7x, 32 devices: a whole 2x2x4 slice. The times are simulated.
32 devices in a mesh: lat: 4 (over x, core), lon: 8 (over z, y).
Axes of the slice: x: 2, y: 2, z: 4, core: 2. Of those that a mesh axis runs over, the one named last changes fastest.
Arguments:
- zonal_wind: float32 [16, 32, 2048], P(None, 'lat', 'lon'), may hold values from -0.45 to 0.45
- merid_wind: float32 [16, 32, 2048], P(None, 'lat', 'lon'), may hold values from -0.45 to 0.45
- operator_rows: float32 [8, 64], replicated, may hold values from -1.5 to 1.5
- innovation: float32 [131072], P(('lat', 'lon')), may hold values from -6 to 6
- error_weight: float32 [131072], P(('lat', 'lon')), may hold values from 0.25 to 4
- interp_weight: float32 [4, 131072], P(None, ('lat', 'lon')), may hold values from 0.05 to 1
- obs_slot: int32 [4, 131072], P(None, ('lat', 'lon')), may hold values from 0 to 2047
- block_count: int32 [1024], P(('lat', 'lon')), may hold values from 1 to 128
- block_type: int32 [1024], P(('lat', 'lon')), may hold values from 0 to 7
- block_window: int32 [1024], P(('lat', 'lon')), may hold values from 0 to 2
- send_cols: int32 [32, 2048], P(('lat', 'lon')), may hold values from 0 to 2047
Outputs:
- increment: float32 [4, 16, 32, 2048], P(None, None, 'lat', 'lon')
- residual: float32 [4, 16, 32, 2048], P(None, None, 'lat', 'lon')
Inputs may be any that keep to these rules, and one draw needn't show every extreme that they name: `obs_slot`: an index into the 2048 slots that the observation's own device receives: slot s * 64 + q comes from device s. `send_cols`: entry r * 64 + q of device s's row is a local cell of device s, row-major over 8 x 256, sent to slot q of device r. `block_count`: rows of a block at or past its count are padding and observe nothing.
All inputs are finite; a program needn't handle non-finite values.
Results may differ from a plain program's by a relative error of at most 0.00025.
Values sent between devices are 32-bit elements; how exact they have to be, the bound alone decides.
No kernel may reach another device: no remote copies, remote signals or barrier semaphores. Data moves between devices by JAX's collectives and lax.ppermute only.
A program may use at most 128 MiB of HBM per device.

v0:
```python
import jax
import jax.numpy as jnp
from jax import lax
from jax.sharding import PartitionSpec as P

TYPES = 8
WIN = 3
STEP_WIN = 2
ITERS = 2
BLOCK_ROWS = 128


HIGH = lax.Precision.HIGHEST


def padded(cells, sides, width, closed):
    for axis, dim in sides:
        count = lax.axis_size(axis)
        ends = count if closed else count - 1
        head = lax.slice_in_dim(cells, 0, width, axis=dim)
        tail = lax.slice_in_dim(cells, cells.shape[dim] - width, cells.shape[dim], axis=dim)
        cells = jnp.concatenate(
            [
                lax.ppermute(tail, axis, [(i, (i + 1) % count) for i in range(ends)]),
                cells,
                lax.ppermute(head, axis, [((i + 1) % count, i) for i in range(ends)]),
            ],
            axis=dim,
        )
    return cells


def extend(field, width):
    widened = padded(field, (("lon", 3),), width, True)
    return padded(widened, (("lat", 2),), width, False)


def squares(residual):
    return lax.psum(jnp.sum(residual * residual), ("lat", "lon"))


def advance(field, margin, adjoint, winds, valid_rows):
    keep_rate, from_west, from_east, from_south, from_north = winds
    lat_out = keep_rate.shape[1] - 4 + 2 * margin - 2
    lon_out = keep_rate.shape[2] - 4 + 2 * margin - 2
    offset = 3 - margin

    def wind(array, shift_lat, shift_lon):
        return array[
            :,
            offset + shift_lat : offset + shift_lat + lat_out,
            offset + shift_lon : offset + shift_lon + lon_out,
        ]

    def cur(shift_lat, shift_lon):
        return field[
            :, :, 1 + shift_lat : 1 + shift_lat + lat_out, 1 + shift_lon : 1 + shift_lon + lon_out
        ]

    if adjoint:
        result = (
            wind(keep_rate, 0, 0) * cur(0, 0)
            + wind(from_west, 0, 1) * cur(0, 1)
            - wind(from_east, 0, -1) * cur(0, -1)
            + wind(from_south, 1, 0) * cur(1, 0)
            - wind(from_north, -1, 0) * cur(-1, 0)
        )
    else:
        result = (
            wind(keep_rate, 0, 0) * cur(0, 0)
            + wind(from_west, 0, 0) * cur(0, -1)
            - wind(from_east, 0, 0) * cur(0, 1)
            + wind(from_south, 0, 0) * cur(-1, 0)
            - wind(from_north, 0, 0) * cur(1, 0)
        )
    mask = valid_rows[offset : offset + lat_out][:, None]
    return result * mask


def shards(
    zonal_wind,
    merid_wind,
    operator_rows,
    innovation,
    error_weight,
    interp_weight,
    obs_slot,
    block_count,
    block_type,
    block_window,
    send_cols,
):
    levels, lat_cells, lon_cells = zonal_wind.shape
    channels = operator_rows.shape[1]
    layers = channels // levels
    cells = lat_cells * lon_cells
    recv = send_cols.shape[1]
    blocks = block_count.shape[0]
    rows = innovation.shape[0]
    send_row = send_cols[0]
    total_rows = lax.axis_size("lat") * lat_cells
    wind_rims = extend(jnp.stack([zonal_wind, merid_wind]), 2)
    keep_ext = 1.0 - jnp.abs(wind_rims[0]) - jnp.abs(wind_rims[1])
    winds = (
        keep_ext,
        jnp.maximum(wind_rims[0], 0.0),
        jnp.minimum(wind_rims[0], 0.0),
        jnp.maximum(wind_rims[1], 0.0),
        jnp.minimum(wind_rims[1], 0.0),
    )
    global_rows = lax.axis_index("lat") * lat_cells - 2 + jnp.arange(lat_cells + 4, dtype=jnp.int32)
    valid_rows = ((global_rows >= 0) & (global_rows < total_rows)).astype(jnp.float32)
    live = (jnp.arange(BLOCK_ROWS, dtype=jnp.int32)[None, :] < block_count[:, None]).reshape(rows)
    weight_live = error_weight * live.astype(jnp.float32)
    row_type = jnp.broadcast_to(block_type[:, None], (blocks, BLOCK_ROWS)).reshape(rows)
    row_window = jnp.broadcast_to(block_window[:, None], (blocks, BLOCK_ROWS)).reshape(rows)
    flat_index = (row_window * TYPES + row_type)[None, :] * recv + obs_slot

    def run_steps(field, count, adjoint):
        for _ in range(count):
            field = advance(extend(field, 1), 1, adjoint, winds, valid_rows)
        return field

    def forward_model(field):
        states = [field]
        for _ in range(WIN - 1):
            field = run_steps(field, STEP_WIN, False)
            states.append(field)
        return states

    def adjoint_model(weighted):
        terms = (interp_weight * weighted[None, :]).reshape(-1)
        summed = jax.ops.segment_sum(
            terms, flat_index.reshape(-1), num_segments=WIN * TYPES * recv
        ).reshape(WIN, TYPES, recv)
        typed_back = lax.all_to_all(
            summed.reshape(WIN * TYPES, recv),
            ("lat", "lon"),
            split_axis=1,
            concat_axis=1,
            tiled=True,
        ).reshape(WIN, TYPES, recv)
        returned = jnp.einsum("tc,wts->wcs", operator_rows, typed_back, precision=HIGH)
        forcing = [
            jnp.zeros((channels, cells), jnp.float32)
            .at[:, send_row]
            .add(returned[window])
            .reshape(layers, levels, lat_cells, lon_cells)
            for window in range(WIN)
        ]
        field = forcing[WIN - 1]
        for window in range(WIN - 2, -1, -1):
            field = run_steps(field, STEP_WIN, True)
            field = field + forcing[window]
        return field

    right = adjoint_model(weight_live * innovation)
    increment = jnp.zeros_like(right)
    residual = right
    direction = right
    norm_now = squares(residual)
    for _ in range(ITERS):
        observe_states = forward_model(direction)
        picked = jnp.stack(
            [jnp.take(state.reshape(channels, cells), send_row, axis=1) for state in observe_states]
        )
        typed = jnp.einsum("tc,wcs->wts", operator_rows, picked, precision=HIGH)
        images = lax.all_to_all(
            typed.reshape(WIN * TYPES, recv),
            ("lat", "lon"),
            split_axis=1,
            concat_axis=1,
            tiled=True,
        )
        values = images.reshape(-1)[flat_index]
        image = direction + adjoint_model(weight_live * jnp.sum(interp_weight * values, axis=0))
        alpha = norm_now / lax.psum(jnp.sum(direction * image), ("lat", "lon"))
        increment = increment + alpha * direction
        residual = residual - alpha * image
        norm_next = squares(residual)
        direction = residual + norm_next / norm_now * direction
        norm_now = norm_next
    return (increment, residual)


def solution(mesh):
    return jax.shard_map(
        shards,
        mesh=mesh,
        in_specs=(
            P(None, "lat", "lon"),
            P(None, "lat", "lon"),
            P(),
            P(("lat", "lon")),
            P(("lat", "lon")),
            P(None, ("lat", "lon")),
            P(None, ("lat", "lon")),
            P(("lat", "lon")),
            P(("lat", "lon")),
            P(("lat", "lon")),
            P(("lat", "lon"), None),
        ),
        out_specs=(P(None, None, "lat", "lon"), P(None, None, "lat", "lon")),
        check_vma=False,
    )
```

profile of v0, /device:TPU:1, one launch (start us, length us, event | category | flops | bytes accessed | tf_op | source)
XLA Modules:
  0.0 1315.7 jit_solution(2563698290402520018)
XLA Ops:
  4.1 86.5 %scatter_custom_fusion = f32[49152]{0:T(1024)S(1)} fusion(s32[16384]{0:T(1024)S(1)} %bitcast.263, f32[16384]{0:T(1024)S(1)} %bitcast.266, f32[]{:T(128)} %constant.18.clone.1), kind=kCustom, calls=%fused_computation.503 | custom fusion | flops 16384 | bytes 196612 | tf_op jit(solution)/shard_map/scatter-add | solution.py:133
  126.5 11.7 scatter_custom_fusion.1
  182.3 12.1 scatter_custom_fusion.2
  241.2 12.1 scatter_custom_fusion.3
  345.0 7.6 gather_fusion.2
  357.3 7.6 gather_fusion.3
  369.7 7.6 gather_fusion.4
  384.3 8.4 all-to-all-done.1
  394.2 90.5 %gather_fusion = f32[16384]{0:T(1024)S(1)} fusion(f32[49152]{0:T(1024)S(1)} %reshape.188, s32[16384]{0:T(1024)S(1)} %broadcast_clamp_fusion), kind=kCustom, calls=%fused_computation.6 | custom fusion | bytes 196608 | tf_op jit(solution)/shard_map/gather | solution.py:175
  485.0 86.9 %scatter_custom_fusion.4 = f32[49152]{0:T(1024)S(1)} fusion(s32[16384]{0:T(1024)} %bitcast.264, f32[16384]{0:T(1024)S(1)} %bitcast.268, f32[]{:T(128)} %constant.18.clone.1), kind=kCustom, calls=%fused_computation.501 | custom fusion | flops 16384 | bytes 197120 | tf_op jit(solution)/shard_map/scatter-add | solution.py:133
  572.5 11.4 all_to_all.45
  590.5 12.1 scatter_custom_fusion.5
  607.4 8.1 collective-permute-done.37
  630.4 7.6 collective-permute-done.41
  648.7 12.1 scatter_custom_fusion.6
  709.0 12.1 scatter_custom_fusion.7
  726.0 37.0 %all-reduce = (f32[]{:T(128)}, f32[]{:T(128)}) all-reduce(f32[]{:T(128)} %get-tuple-element.4, f32[]{:T(128)} %get-tuple-element.3), channel_id=1, replica_groups=mesh['lat'=4,'lon'=8] {'lat','lon'}, use_global_device_ids=true, to_apply=%region_5.0 | all-reduce | flops 2 | bytes 16 | tf_op jit(solution)/shard_map/psum | solution.py:39
  765.1 41.5 %psum.30 = f32[]{:T(128)} all-reduce(f32[]{:T(128)} %multiply_reduce_fusion.1), channel_id=1, replica_groups=mesh['lat'=4,'lon'=8] {'lat','lon'}, use_global_device_ids=true, to_apply=%region_14.16 | all-reduce | flops 1 | bytes 8 | tf_op jit(solution)/shard_map/psum | solution.py:39
  812.4 7.7 collective-permute-done.52
  898.5 7.6 gather_fusion.5
  910.8 7.6 gather_fusion.6
  923.3 7.6 gather_fusion.7
  934.3 11.1 all_to_all.46
  946.9 90.5 %gather_fusion.1 = f32[16384]{0:T(1024)S(1)} fusion(f32[49152]{0:T(1024)S(1)} %reshape.197, s32[16384]{0:T(1024)S(1)} %copy-done.53), kind=kCustom, calls=%fused_computation.7 | custom fusion | bytes 196608 | tf_op jit(solution)/shard_map/gather | solution.py:175
  1037.7 86.7 %scatter_custom_fusion.8 = f32[49152]{0:T(1024)S(1)} fusion(s32[16384]{0:T(1024)} %bitcast.265, f32[16384]{0:T(1024)S(1)} %bitcast.267, f32[]{:T(128)} %constant.18.clone.1), kind=kCustom, calls=%fused_computation.499 | custom fusion | flops 16384 | bytes 197120 | tf_op jit(solution)/shard_map/scatter-add | solution.py:133
  1125.0 11.6 all_to_all.47
  1142.0 12.1 scatter_custom_fusion.9
  1158.9 8.1 collective-permute-done.69
  1182.0 7.6 collective-permute-done.73
  1200.2 12.8 scatter_custom_fusion.10
  1258.2 12.8 scatter_custom_fusion.11
  1275.5 37.4 %psum.31 = f32[]{:T(128)} all-reduce(f32[]{:T(128)} %get-tuple-element.7), channel_id=1, replica_groups=mesh['lat'=4,'lon'=8] {'lat','lon'}, use_global_device_ids=true, to_apply=%region_21.23 | all-reduce | flops 1 | bytes 8 | tf_op jit(solution)/shard_map/psum | solution.py:177
  (481 shorter events, 514.1 us)
Async XLA Ops:
  91.8 29.9 %all-to-all-start = ((f32[32,1,1536]{2,1,0:T(1,128)}), f32[32,1,1536]{2,1,0:T(1,128)S(1)}, u32[]{:S(2)}, u32[]{:S(2)}) async-start(f32[32,1,1536]{2,1,0:T(1,128)} %reshape.413), calls=%async_computation | async-start | bytes 393216 | tf_op jit(solution)/shard_map/all_to_all | solution.py:136
  159.6 14.0 %collective-permute-start.8 = (f32[4,16,8,1]{3,2,1,0:T(8,128)S(1)}, f32[4,16,8,1]{3,2,1,0:T(8,128)S(1)}, u32[]{:S(2)}, u32[]{:S(2)}) collective-permute-start(f32[4,16,8,1]{3,2,1,0:T(8,128)S(1)} %get-tuple-element.103), channel_id=1, source_target_pairs={{1,0},{2,1},{3,2},{4,3},{5,4},{6,5},{7,6},{0,7},{9,8},{10,9},{11,1... | collective-permute-start | bytes 6152 | tf_op jit(solution)/shard_map/ppermute | solution.py:26
  174.9 20.0 %collective-permute-start.10 = (f32[4,16,1,258]{3,2,1,0:T(1,128)}, f32[4,16,1,258]{3,2,1,0:T(1,128)S(1)}, u32[]{:S(2)}, u32[]{:S(2)}) collective-permute-start(f32[4,16,1,258]{3,2,1,0:T(1,128)} %get-tuple-element.55), channel_id=1, source_target_pairs={{8,0},{16,8},{24,16},{9,1},{17,9},{25,17},{10,2},{18,10},{26,18},{... | collective-permute-start | bytes 198152 | tf_op jit(solution)/shard_map/ppermute | solution.py:26
  177.0 17.9 %collective-permute-start.11 = (f32[4,16,1,258]{3,2,1,0:T(1,128)}, f32[4,16,1,258]{3,2,1,0:T(1,128)S(1)}, u32[]{:S(2)}, u32[]{:S(2)}) collective-permute-start(f32[4,16,1,258]{3,2,1,0:T(1,128)} %get-tuple-element.56), channel_id=1, source_target_pairs={{0,8},{8,16},{16,24},{1,9},{9,17},{17,25},{2,10},{10,18},{18,26},{... | collective-permute-start | bytes 198152 | tf_op jit(solution)/shard_map/ppermute | solution.py:24
  197.2 13.2 %collective-permute-start.12 = (f32[4,16,8,1]{3,2,1,0:T(8,128)S(1)}, f32[4,16,8,1]{3,2,1,0:T(8,128)S(1)}, u32[]{:S(2)}, u32[]{:S(2)}) collective-permute-start(f32[4,16,8,1]{3,2,1,0:T(8,128)S(1)} %get-tuple-element.101), channel_id=1, source_target_pairs={{1,0},{2,1},{3,2},{4,3},{5,4},{6,5},{7,6},{0,7},{9,8},{10,9},{11,1... | collective-permute-start | bytes 6152 | tf_op jit(solution)/shard_map/ppermute | solution.py:26
  219.2 13.7 %collective-permute-start.16 = (f32[4,16,8,1]{3,2,1,0:T(8,128)S(1)}, f32[4,16,8,1]{3,2,1,0:T(8,128)S(1)}, u32[]{:S(2)}, u32[]{:S(2)}) collective-permute-start(f32[4,16,8,1]{3,2,1,0:T(8,128)S(1)} %get-tuple-element.99), channel_id=1, source_target_pairs={{1,0},{2,1},{3,2},{4,3},{5,4},{6,5},{7,6},{0,7},{9,8},{10,9},{11,1... | collective-permute-start | bytes 6152 | tf_op jit(solution)/shard_map/ppermute | solution.py:26
  234.2 19.5 %collective-permute-start.18 = (f32[4,16,1,258]{3,2,1,0:T(1,128)}, f32[4,16,1,258]{3,2,1,0:T(1,128)S(1)}, u32[]{:S(2)}, u32[]{:S(2)}) collective-permute-start(f32[4,16,1,258]{3,2,1,0:T(1,128)} %get-tuple-element.51), channel_id=1, source_target_pairs={{8,0},{16,8},{24,16},{9,1},{17,9},{25,17},{10,2},{18,10},{26,18},{... | collective-permute-start | bytes 198152 | tf_op jit(solution)/shard_map/ppermute | solution.py:26
  236.1 17.6 %collective-permute-start.19 = (f32[4,16,1,258]{3,2,1,0:T(1,128)}, f32[4,16,1,258]{3,2,1,0:T(1,128)S(1)}, u32[]{:S(2)}, u32[]{:S(2)}) collective-permute-start(f32[4,16,1,258]{3,2,1,0:T(1,128)} %get-tuple-element.52), channel_id=1, source_target_pairs={{0,8},{8,16},{16,24},{1,9},{9,17},{17,25},{2,10},{10,18},{18,26},{... | collective-permute-start | bytes 198152 | tf_op jit(solution)/shard_map/ppermute | solution.py:24
  256.0 13.1 collective-permute-start.21
  278.8 13.0 collective-permute-start.25
  323.1 12.8 collective-permute-start.33
  336.5 30.9 %collective-permute-start.34 = (f32[4,16,1,258]{3,2,1,0:T(1,128)S(1)}, f32[4,16,1,258]{3,2,1,0:T(1,128)}, u32[]{:S(2)}, u32[]{:S(2)}) collective-permute-start(f32[4,16,1,258]{3,2,1,0:T(1,128)S(1)} %get-tuple-element.43), channel_id=1, source_target_pairs={{0,8},{8,16},{16,24},{1,9},{9,17},{17,25},{2,10},{10,18},{18,26},{... | collective-permute-start | bytes 198152 | tf_op jit(solution)/shard_map/ppermute | solution.py:24
  338.4 28.9 %collective-permute-start.35 = (f32[4,16,1,258]{3,2,1,0:T(1,128)S(1)}, f32[4,16,1,258]{3,2,1,0:T(1,128)}, u32[]{:S(2)}, u32[]{:S(2)}) collective-permute-start(f32[4,16,1,258]{3,2,1,0:T(1,128)S(1)} %get-tuple-element.44), channel_id=1, source_target_pairs={{8,0},{16,8},{24,16},{9,1},{17,9},{25,17},{10,2},{18,10},{26,18},{... | collective-permute-start | bytes 198152 | tf_op jit(solution)/shard_map/ppermute | solution.py:26
  604.6 12.8 collective-permute-start.36
  626.6 13.9 %collective-permute-start.40 = (f32[4,16,8,1]{3,2,1,0:T(8,128)S(1)}, f32[4,16,8,1]{3,2,1,0:T(8,128)S(1)}, u32[]{:S(2)}, u32[]{:S(2)}) collective-permute-start(f32[4,16,8,1]{3,2,1,0:T(8,128)S(1)} %get-tuple-element.87), channel_id=1, source_target_pairs={{1,0},{2,1},{3,2},{4,3},{5,4},{6,5},{7,6},{0,7},{9,8},{10,9},{11,1... | collective-permute-start | bytes 6152 | tf_op jit(solution)/shard_map/ppermute | solution.py:26
  641.7 21.3 %collective-permute-start.42 = (f32[4,16,1,258]{3,2,1,0:T(1,128)}, f32[4,16,1,258]{3,2,1,0:T(1,128)S(1)}, u32[]{:S(2)}, u32[]{:S(2)}) collective-permute-start(f32[4,16,1,258]{3,2,1,0:T(1,128)} %get-tuple-element.39), channel_id=1, source_target_pairs={{8,0},{16,8},{24,16},{9,1},{17,9},{25,17},{10,2},{18,10},{26,18},{... | collective-permute-start | bytes 198152 | tf_op jit(solution)/shard_map/ppermute | solution.py:26
  644.1 19.0 %collective-permute-start.43 = (f32[4,16,1,258]{3,2,1,0:T(1,128)}, f32[4,16,1,258]{3,2,1,0:T(1,128)S(1)}, u32[]{:S(2)}, u32[]{:S(2)}) collective-permute-start(f32[4,16,1,258]{3,2,1,0:T(1,128)} %get-tuple-element.40), channel_id=1, source_target_pairs={{0,8},{8,16},{16,24},{1,9},{9,17},{17,25},{2,10},{10,18},{18,26},{... | collective-permute-start | bytes 198152 | tf_op jit(solution)/shard_map/ppermute | solution.py:24
  665.5 13.8 %collective-permute-start.44 = (f32[4,16,8,1]{3,2,1,0:T(8,128)S(1)}, f32[4,16,8,1]{3,2,1,0:T(8,128)S(1)}, u32[]{:S(2)}, u32[]{:S(2)}) collective-permute-start(f32[4,16,8,1]{3,2,1,0:T(8,128)S(1)} %get-tuple-element.85), channel_id=1, source_target_pairs={{1,0},{2,1},{3,2},{4,3},{5,4},{6,5},{7,6},{0,7},{9,8},{10,9},{11,1... | collective-permute-start | bytes 6152 | tf_op jit(solution)/shard_map/ppermute | solution.py:26
  688.1 12.6 collective-permute-start.48
  702.0 21.3 %collective-permute-start.50 = (f32[4,16,1,258]{3,2,1,0:T(1,128)}, f32[4,16,1,258]{3,2,1,0:T(1,128)S(1)}, u32[]{:S(2)}, u32[]{:S(2)}) collective-permute-start(f32[4,16,1,258]{3,2,1,0:T(1,128)} %get-tuple-element.35), channel_id=1, source_target_pairs={{8,0},{16,8},{24,16},{9,1},{17,9},{25,17},{10,2},{18,10},{26,18},{... | collective-permute-start | bytes 198152 | tf_op jit(solution)/shard_map/ppermute | solution.py:26
  703.9 19.4 %collective-permute-start.51 = (f32[4,16,1,258]{3,2,1,0:T(1,128)}, f32[4,16,1,258]{3,2,1,0:T(1,128)S(1)}, u32[]{:S(2)}, u32[]{:S(2)}) collective-permute-start(f32[4,16,1,258]{3,2,1,0:T(1,128)} %get-tuple-element.36), channel_id=1, source_target_pairs={{0,8},{8,16},{16,24},{1,9},{9,17},{17,25},{2,10},{10,18},{18,26},{... | collective-permute-start | bytes 198152 | tf_op jit(solution)/shard_map/ppermute | solution.py:24
  877.1 12.8 collective-permute-start.65
  891.2 29.7 %collective-permute-start.66 = (f32[4,16,1,258]{3,2,1,0:T(1,128)}, f32[4,16,1,258]{3,2,1,0:T(1,128)}, u32[]{:S(2)}, u32[]{:S(2)}) collective-permute-start(f32[4,16,1,258]{3,2,1,0:T(1,128)} %get-tuple-element.27), channel_id=1, source_target_pairs={{0,8},{8,16},{16,24},{1,9},{9,17},{17,25},{2,10},{10,18},{18,26},{... | collective-permute-start | bytes 198152 | tf_op jit(solution)/shard_map/ppermute | solution.py:24
  893.1 27.8 %collective-permute-start.67 = (f32[4,16,1,258]{3,2,1,0:T(1,128)}, f32[4,16,1,258]{3,2,1,0:T(1,128)}, u32[]{:S(2)}, u32[]{:S(2)}) collective-permute-start(f32[4,16,1,258]{3,2,1,0:T(1,128)} %get-tuple-element.28), channel_id=1, source_target_pairs={{8,0},{16,8},{24,16},{9,1},{17,9},{25,17},{10,2},{18,10},{26,18},{... | collective-permute-start | bytes 198152 | tf_op jit(solution)/shard_map/ppermute | solution.py:26
  1156.1 12.8 collective-permute-start.68
  1178.1 13.9 %collective-permute-start.72 = (f32[4,16,8,1]{3,2,1,0:T(8,128)S(1)}, f32[4,16,8,1]{3,2,1,0:T(8,128)S(1)}, u32[]{:S(2)}, u32[]{:S(2)}) collective-permute-start(f32[4,16,8,1]{3,2,1,0:T(8,128)S(1)} %get-tuple-element.71), channel_id=1, source_target_pairs={{1,0},{2,1},{3,2},{4,3},{5,4},{6,5},{7,6},{0,7},{9,8},{10,9},{11,1... | collective-permute-start | bytes 6152 | tf_op jit(solution)/shard_map/ppermute | solution.py:26
  1193.2 21.4 %collective-permute-start.74 = (f32[4,16,1,258]{3,2,1,0:T(1,128)}, f32[4,16,1,258]{3,2,1,0:T(1,128)S(1)}, u32[]{:S(2)}, u32[]{:S(2)}) collective-permute-start(f32[4,16,1,258]{3,2,1,0:T(1,128)} %get-tuple-element.23), channel_id=1, source_target_pairs={{8,0},{16,8},{24,16},{9,1},{17,9},{25,17},{10,2},{18,10},{26,18},{... | collective-permute-start | bytes 198152 | tf_op jit(solution)/shard_map/ppermute | solution.py:26
  1195.6 19.1 %collective-permute-start.75 = (f32[4,16,1,258]{3,2,1,0:T(1,128)}, f32[4,16,1,258]{3,2,1,0:T(1,128)S(1)}, u32[]{:S(2)}, u32[]{:S(2)}) collective-permute-start(f32[4,16,1,258]{3,2,1,0:T(1,128)} %get-tuple-element.24), channel_id=1, source_target_pairs={{0,8},{8,16},{16,24},{1,9},{9,17},{17,25},{2,10},{10,18},{18,26},{... | collective-permute-start | bytes 198152 | tf_op jit(solution)/shard_map/ppermute | solution.py:24
  1215.8 13.4 %collective-permute-start.76 = (f32[4,16,8,1]{3,2,1,0:T(8,128)S(1)}, f32[4,16,8,1]{3,2,1,0:T(8,128)S(1)}, u32[]{:S(2)}, u32[]{:S(2)}) collective-permute-start(f32[4,16,8,1]{3,2,1,0:T(8,128)S(1)} %get-tuple-element.69), channel_id=1, source_target_pairs={{1,0},{2,1},{3,2},{4,3},{5,4},{6,5},{7,6},{0,7},{9,8},{10,9},{11,1... | collective-permute-start | bytes 6152 | tf_op jit(solution)/shard_map/ppermute | solution.py:26
  1238.0 12.6 collective-permute-start.80
  1251.3 21.4 %collective-permute-start.82 = (f32[4,16,1,258]{3,2,1,0:T(1,128)S(1)}, f32[4,16,1,258]{3,2,1,0:T(1,128)S(1)}, u32[]{:S(2)}, u32[]{:S(2)}) collective-permute-start(f32[4,16,1,258]{3,2,1,0:T(1,128)S(1)} %get-tuple-element.19), channel_id=1, source_target_pairs={{8,0},{16,8},{24,16},{9,1},{17,9},{25,17},{10,2},{18,10},{26,18},{... | collective-permute-start | bytes 198152 | tf_op jit(solution)/shard_map/ppermute | solution.py:26
  1253.2 19.5 %collective-permute-start.83 = (f32[4,16,1,258]{3,2,1,0:T(1,128)S(1)}, f32[4,16,1,258]{3,2,1,0:T(1,128)S(1)}, u32[]{:S(2)}, u32[]{:S(2)}) collective-permute-start(f32[4,16,1,258]{3,2,1,0:T(1,128)S(1)} %get-tuple-element.20), channel_id=1, source_target_pairs={{0,8},{8,16},{16,24},{1,9},{9,17},{17,25},{2,10},{10,18},{18,26},{... | collective-permute-start | bytes 198152 | tf_op jit(solution)/shard_map/ppermute | solution.py:24
  (119 other events, 4818.5 us)
where the time goes:
time: 1330 us; the launch traced here: 1320 us
  other arithmetic  426 us (32%)
  local copies, waits for them, and re-layouts  288 us (22%)
  waiting for transfers between devices  228 us (17%)
  starting transfers between devices  211 us (16%)
  blocking collectives  150 us (11%)
    scatter-add x3, other arithmetic, adjoint_model(): jax.ops.segment_sum(terms, flat_index.reshape(-1), num_segments=WIN * TYP...  260 us
    gather x4, local copies, waits for them, and re-layouts, shards(): values = images.reshape(-1)[flat_index]  181 us
    ppermute x42, waiting for transfers between devices, padded(): lax.ppermute(tail, axis, [(i, (i + 1) % count) for i in range(ends)])  141 us
    ppermute x42, starting transfers between devices, padded(): lax.ppermute(head, axis, [((i + 1) % count, i) for i in range(ends)])  132 us
    scatter-add x9, other arithmetic, adjoint_model(): forcing = [jnp.zeros((channels, cells), jnp.float32).at[:, send_row].add(...  110 us
    psum x2, blocking collectives, squares(): return lax.psum(jnp.sum(residual * residual), ('lat', 'lon'))  78.5 us
    ppermute x42, waiting for transfers between devices, padded(): lax.ppermute(head, axis, [((i + 1) % count, i) for i in range(ends)])  78.1 us
    ppermute x42, starting transfers between devices, padded(): lax.ppermute(tail, axis, [(i, (i + 1) % count) for i in range(ends)])  69.2 us
  transfers between devices with their start and end apart: 86, of which 60 were waited for; matrix products, arithmetic and copies ran while one was open for 11% of the time, Pallas kernels for 0%

commit v1 on v0

v1 whole, which is shorter than its diff:
```python
import functools

import jax
import jax.numpy as jnp
from jax import lax
from jax.experimental import pallas as pl
from jax.experimental.pallas import tpu as pltpu
from jax.sharding import PartitionSpec as P

WIN = 3
STEP_WIN = 2
ITERS = 2
BLOCK_ROWS = 128
LANES = 128
SUB = 8
REACH = STEP_WIN * (WIN - 1)
HALO = 2 * REACH
AXES = ("lat", "lon")
F32 = jnp.float32
BF16 = jnp.bfloat16
NT = (((1,), (1,)), ((), ()))


def log2(n):
    assert n & (n - 1) == 0
    return n.bit_length() - 1


def iota(shape, dim):
    return lax.broadcasted_iota(jnp.int32, shape, dim)


def halves(x):
    top = x.astype(BF16).astype(F32)
    return top, x - top


def dot(a, b):
    return jnp.dot(a, b, preferred_element_type=F32)


class Packing:
    def __init__(self, devices, recv):
        self.devices = devices
        self.recv = recv
        self.slots = recv // devices
        assert self.slots <= LANES and recv % LANES == 0
        self.per = LANES // self.slots
        self.tiles = WIN // self.per + 1
        self.rows = self.tiles * SUB
        self.spare_tile, self.spare_group = WIN // self.per, WIN % self.per
        self.group_bits = log2(self.slots)

    def group(self, shape):
        return iota(shape, len(shape) - 1) >> self.group_bits

    def spare(self, row):
        lane = iota(row.shape, 1)
        first = lane == self.spare_group * self.slots
        return jnp.sum(jnp.where(first, row, 0.0), axis=1, keepdims=True)

    def write(self, out_ref, typed, spare, tile):
        group = self.group((SUB, LANES))
        for d in range(self.per):
            device = tile * self.per + d
            for part in range(self.tiles):
                chunk = jnp.zeros((SUB, LANES), F32)
                for g in range(self.per):
                    w = part * self.per + g
                    if w < WIN:
                        piece = turn(typed[w], (g - d) * self.slots)
                    elif w == WIN:
                        piece = spare
                    else:
                        continue
                    chunk = jnp.where(group == g, piece, chunk)
                at = (device * self.tiles + part) * SUB
                out_ref[at : at + SUB, :] = chunk

    def read(self, ref, w, tile):
        group = self.group((SUB, LANES))
        part, g = w // self.per, w % self.per
        found = jnp.zeros((SUB, LANES), F32)
        for d in range(self.per):
            at = ((tile * self.per + d) * self.tiles + part) * SUB
            piece = turn(ref[at : at + SUB, :], (d - g) * self.slots)
            found = jnp.where(group == d, piece, found)
        return found


def turn(x, shift):
    shift %= x.shape[-1]
    return pltpu.roll(x, shift, len(x.shape) - 1) if shift else x


def observe_kernel(pack, mode, count_ref, type_ref, window_ref, *refs):
    if mode == "right":
        slot_ref, weight_ref, error_ref, value_ref, out_ref, total = refs
    else:
        if mode == "start":
            recv_ref, slot_ref, weight_ref, error_ref = refs[:4]
            refs = refs[4:]
        else:
            recv_ref, slot_ref, weight_ref, error_ref, value_ref, before_ref = refs[:6]
            refs = refs[6:]
        out_ref, observed_ref, scalar_ref, total, table = refs
    points = slot_ref.shape[0]
    blocks = error_ref.shape[0]
    devices = pack.devices
    wide = points * BLOCK_ROWS
    spare = pack.spare_tile * SUB
    total[...] = jnp.zeros_like(total)
    if mode != "right":
        for j in range(pack.rows):
            table[j] = recv_ref[pl.ds(j, devices, stride=pack.rows), :]
        norm = pack.spare(jnp.sum(table[spare], axis=0, keepdims=True))
        if mode == "start":
            ratio, square = jnp.zeros_like(norm), norm
        else:
            cross = pack.spare(jnp.sum(table[spare + 1], axis=0, keepdims=True))
            ratio = norm / before_ref[0:1, 0:1]
            square = norm + 2.0 * ratio * cross + ratio * ratio * before_ref[2:3, 0:1]
        row = iota((SUB, LANES), 0)
        scalar_ref[...] = jnp.where(row == 0, norm, jnp.where(row == 1, ratio, square))

    def one(b, energy):
        window = window_ref[b]
        j = (window >> log2(pack.per)) * SUB + type_ref[b]
        shift = (window & (pack.per - 1)) * pack.slots
        lanes = pl.ds(pl.multiple_of(b * BLOCK_ROWS, BLOCK_ROWS), BLOCK_ROWS)
        slot = slot_ref[:, lanes]
        weight = weight_ref[:, lanes]
        device = slot >> pack.group_bits
        lane = (slot & (pack.slots - 1)) + shift
        ids = iota((LANES, BLOCK_ROWS), 0)
        pick = jnp.concatenate(
            [jnp.where(ids == lane[k : k + 1, :], 1.0, 0.0) for k in range(points)], axis=1
        ).astype(BF16)
        device = jnp.concatenate([device[k : k + 1, :] for k in range(points)], axis=1)
        weight = jnp.concatenate([weight[k : k + 1, :] for k in range(points)], axis=1)
        owner = iota((devices, wide), 0) == device
        if mode == "right":
            value = value_ref[pl.ds(b, 1), :]
        else:
            top, rest = halves(table[j])
            both = dot(jnp.concatenate([top, rest], axis=0).astype(BF16), pick)
            both = both[:devices] + both[devices:]
            found = jnp.sum(jnp.where(owner, both, 0.0), axis=0, keepdims=True) * weight
            value = found[:, :BLOCK_ROWS]
            for k in range(1, points):
                value = value + found[:, k * BLOCK_ROWS : (k + 1) * BLOCK_ROWS]
            if mode == "next":
                value = value + ratio * value_ref[pl.ds(b, 1), :]
            observed_ref[pl.ds(b, 1), :] = value
        live = iota((1, BLOCK_ROWS), 1) < count_ref[b]
        weighted = jnp.where(live, error_ref[pl.ds(b, 1), :], 0.0) * value
        spread = jnp.concatenate([weighted] * points, axis=1) * weight
        top, rest = halves(jnp.where(owner, spread, 0.0))
        both = lax.dot_general(
            jnp.concatenate([top, rest], axis=0).astype(BF16),
            pick,
            NT,
            preferred_element_type=F32,
        )
        total[j] += both[:devices] + both[devices:]
        return energy + weighted * value

    energy = lax.fori_loop(0, blocks, one, jnp.zeros((1, BLOCK_ROWS), F32), unroll=4)
    energy = jnp.sum(energy, axis=1, keepdims=True)
    for j in range(pack.rows):
        chunk = total[j]
        if j == spare:
            chunk = jnp.where(pack.group((devices, LANES)) == pack.spare_group, energy, chunk)
        out_ref[pl.ds(j, devices, stride=pack.rows), :] = chunk


def collect_kernel(pack, lat_cells, with_winds, *refs):
    if with_winds:
        recv_ref, send_ref, zonal_ref, merid_ref = refs[:4]
        refs = refs[4:]
    else:
        recv_ref, send_ref = refs[:2]
        refs = refs[2:]
    main_ref, west_ref, east_ref, scalar_ref = refs[:4]
    lon_cells = main_ref.shape[2]
    cols = lon_cells // LANES
    tiles = pack.recv // LANES
    send = send_ref[...]
    pick = jnp.where(iota((LANES, pack.recv), 0) == (send & (LANES - 1)), 1.0, 0.0).astype(BF16)
    high = send >> log2(LANES)
    strips = {}

    def note(slab, left, right):
        at = slab * HALO
        q, s = at // LANES, at % LANES
        lane = iota((SUB, LANES), 1)
        inside = (lane >= s) & (lane < s + HALO)
        west, east = strips.get(q, (jnp.zeros((SUB, LANES), F32),) * 2)
        west = jnp.where(inside, turn(left, s), west)
        east = jnp.where(inside, turn(right, s - (LANES - HALO)), east)
        strips[q] = (west, east)

    for w in range(WIN):
        typed = jnp.concatenate([pack.read(recv_ref, w, t) for t in range(tiles)], axis=1)
        masked = []
        for part in halves(typed):
            masked += [
                jnp.where(high == h, part, 0.0) for h in range(lat_cells * cols)
            ]
        both = lax.dot_general(
            jnp.concatenate(masked, axis=0).astype(BF16), pick, NT, preferred_element_type=F32
        )
        count = lat_cells * cols * SUB
        forcing = both[:count] + both[count:]
        for row in range(lat_cells):
            slab = w * lat_cells + row
            pieces = [
                forcing[(row * cols + c) * SUB : (row * cols + c + 1) * SUB] for c in range(cols)
            ]
            for c in range(cols):
                main_ref[slab, :, c * LANES : (c + 1) * LANES] = pieces[c]
            note(slab, pieces[0], pieces[-1])
    if with_winds:
        slab = WIN * lat_cells
        levels = zonal_ref.shape[0] // lat_cells
        held = refs[4:]
        for ref in (zonal_ref, merid_ref):
            for c in range(cols):
                held[c][...] = ref[:, c * LANES : (c + 1) * LANES]
            for row in range(lat_cells):
                for part in range(levels // SUB):
                    at = pl.ds(part * SUB * lat_cells + row, SUB, stride=lat_cells)
                    pieces = [held[c][at, :] for c in range(cols)]
                    for c in range(cols):
                        main_ref[slab, :, c * LANES : (c + 1) * LANES] = pieces[c]
                    note(slab, pieces[0], pieces[-1])
                    slab += 1
    for q in range(west_ref.shape[1] // LANES):
        west, east = strips[q]
        west_ref[:, q * LANES : (q + 1) * LANES] = west
        east_ref[:, q * LANES : (q + 1) * LANES] = east
    row = recv_ref[pl.ds(pack.spare_tile * SUB, pack.devices, stride=pack.rows), :]
    energy = pack.spare(jnp.sum(row, axis=0, keepdims=True))
    scalar_ref[...] = jnp.broadcast_to(energy, scalar_ref.shape)


def model_kernel(pack, mode, dims, edge_ref, *refs):
    layers, levels, lat_cells, lon_cells = dims
    channels = layers * levels
    rows = lat_cells + 2 * HALO
    cols = lon_cells // LANES
    width = lon_cells + LANES
    refs = list(refs)

    def take(count):
        got = refs[:count]
        del refs[:count]
        return got

    mains = take(3)
    strips = [take(2), take(2), take(2)]
    into_ref, back_ref = take(2)
    if mode != "right":
        (winds,) = take(1)
        energy_ref, scalar_ref, residual_ref = take(3)
    if mode == "last":
        (energy0_ref, scalar0_ref, first_ref) = take(3)
        increment_out, residual_out = take(2)
    else:
        (send_ref,) = take(1)
        out_ref, state_out = take(2)
        if mode == "right":
            (winds,) = take(1)
        (picked,) = take(1)
    fields = take(2)
    forced, coef = take(2)
    ends = refs

    lane = iota((SUB, LANES), 1)

    def assemble(slab, block):
        main = mains[block]
        east, west = strips[block]
        q, s = slab * HALO // LANES, slab * HALO % LANES
        right = turn(east[:, q * LANES : (q + 1) * LANES], -s)
        left = turn(west[:, q * LANES : (q + 1) * LANES], LANES - HALO - s)
        edge = jnp.where(lane < HALO, right, jnp.where(lane >= LANES - HALO, left, 0.0))
        return jnp.concatenate([main[slab], edge], axis=1)

    def source(e):
        at = e - HALO
        if at < 0:
            return 0, lat_cells + at
        if at < lat_cells:
            return 1, at
        return 2, at - lat_cells

    for w in range(WIN):
        trim = STEP_WIN * (WIN - 1 - w)
        for e in range(trim, rows - trim):
            block, row = source(e)
            forced[w, e] = assemble(w * lat_cells + row, block)
    if mode == "right":
        for which in range(2):
            for e in range(rows):
                block, row = source(e)
                for part in range(levels // SUB):
                    slab = WIN * lat_cells + (which * lat_cells + row) * (levels // SUB) + part
                    winds[which, e, part * SUB : (part + 1) * SUB, :] = assemble(slab, block)

    def prepare(e, carry):
        u, v = winds[0, e], winds[1, e]
        coef[0, e] = 1.0 - jnp.abs(u) - jnp.abs(v)
        coef[1, e] = jnp.maximum(u, 0.0)
        coef[2, e] = jnp.maximum(-u, 0.0)
        coef[3, e] = jnp.maximum(v, 0.0)
        coef[4, e] = jnp.maximum(-v, 0.0)
        return carry

    lax.fori_loop(0, rows, prepare, 0)

    into = into_ref[...]
    top, rest = halves(into)
    into = jnp.where(iota(into.shape, 1) < 2 * SUB, top, rest).astype(BF16)

    def force(w, e):
        top, rest = halves(forced[w, e])
        return dot(into, jnp.concatenate([top, rest, top, rest], axis=0).astype(BF16))

    def pieces(part):
        level = slice(part * SUB, (part + 1) * SUB)
        return level, [
            slice(v * levels + part * SUB, v * levels + (part + 1) * SUB) for v in range(layers)
        ]

    def adjoint(field, e, put, extra=None):
        for part in range(levels // SUB):
            level, chans = pieces(part)
            keep, west, east = coef[0, e, level], coef[1, e, level], coef[2, e, level]
            south, north = coef[3, e + 1, level], coef[4, e - 1, level]
            for chan in chans:
                here = field[e, chan]
                result = (
                    keep * here
                    + turn(west * here, -1)
                    + turn(east * here, 1)
                    + south * field[e + 1, chan]
                    + north * field[e - 1, chan]
                )
                if extra is not None:
                    result = result + extra[chan]
                put(chan, result)

    def tangent(field, e, put):
        for part in range(levels // SUB):
            level, chans = pieces(part)
            keep, west, east = coef[0, e, level], coef[1, e, level], coef[2, e, level]
            south, north = coef[3, e, level], coef[4, e, level]
            for chan in chans:
                here = field[e, chan]
                put(
                    chan,
                    keep * here
                    + west * turn(here, 1)
                    + east * turn(here, -1)
                    + south * field[e - 1, chan]
                    + north * field[e + 1, chan],
                )

    def put_in(field, e):
        def put(chan, value):
            field[e, chan] = value

        return put

    def begin(e, carry):
        fields[0][e] = force(WIN - 1, e)
        return carry

    lax.fori_loop(0, rows, begin, 0)
    now = 0
    for step in range(1, REACH):
        old, new = fields[now], fields[1 - now]
        w = WIN - 1 - step // STEP_WIN if step % STEP_WIN == 0 else None

        def body(e, carry, old=old, new=new, w=w):
            extra = None if w is None else force(w, e)
            adjoint(old, e, put_in(new, e), extra)
            return carry

        lax.fori_loop(step, rows - step, body, 0)
        now = 1 - now
    old, new = fields[now], fields[1 - now]

    if mode != "right":
        alpha = scalar_ref[0:1, 0:1] / (scalar_ref[2:3, 0:1] + energy_ref[0:1, 0:1])
        ratio = scalar_ref[1:2, 0:1]
    if mode == "last":
        alpha0 = scalar0_ref[0:1, 0:1] / (scalar0_ref[2:3, 0:1] + energy0_ref[0:1, 0:1])

        def finish(row, carry):
            e = row + HALO

            def put(chan, value):
                at = pl.ds(chan.start * lat_cells + row, SUB, stride=lat_cells)
                for c in range(cols):
                    part = slice(c * LANES, (c + 1) * LANES)
                    residual = residual_ref[row + REACH, chan, part]
                    first = first_ref[row + REACH, chan, part]
                    direction = residual + ratio * first
                    image = direction + value[:, part]
                    ends[c][at, :] = alpha0 * first + alpha * direction
                    ends[cols + c][at, :] = residual - alpha * image

            adjoint(old, e, put, force(0, e))
            return carry

        lax.fori_loop(0, lat_cells, finish, 0)
        for c in range(cols):
            part = slice(c * LANES, (c + 1) * LANES)
            increment_out[:, part] = ends[c][...]
            residual_out[:, part] = ends[cols + c][...]
        return

    def update(e, sums):
        valid = jnp.where(e < HALO, edge_ref[0], jnp.where(e >= HALO + lat_cells, edge_ref[1], 1))
        scale = valid.astype(F32)
        inside = jnp.where((e >= HALO) & (e < HALO + lat_cells), 1, 0).astype(F32)
        at = e - REACH
        sums = list(sums)

        def put(chan, value):
            value = value * scale
            if mode != "right":
                before = residual_ref[at, chan]
                value = before - alpha * (before + value)
            state_out[at, chan] = value
            new[e, chan] = value
            kept = value[:, :lon_cells] * inside
            sums[0] = sums[0] + kept * value[:, :lon_cells]
            if mode != "right":
                sums[1] = sums[1] + kept * before[:, :lon_cells]

        adjoint(old, e, put, force(0, e))
        return tuple(sums)

    zero = jnp.zeros((SUB, lon_cells), F32)
    sums = (zero,) if mode == "right" else (zero, zero)
    sums = lax.fori_loop(REACH, rows - REACH, update, sums)
    sums = [jnp.sum(jnp.sum(s, axis=1, keepdims=True), axis=0, keepdims=True) for s in sums]
    now = 1 - now

    back = back_ref[...]
    top, rest = halves(back)
    back = jnp.where(iota(back.shape, 0) < SUB, top, rest).astype(BF16)

    def look(field, w):
        def body(row, carry):
            top, rest = halves(field[row + HALO, :, :lon_cells])
            both = dot(back, jnp.concatenate([top, rest], axis=0).astype(BF16))
            typed = both[:SUB] + both[SUB:]
            for c in range(cols):
                at = pl.multiple_of(((w * lat_cells + row) * cols + c) * SUB, SUB)
                picked[pl.ds(at, SUB), :] = typed[:, c * LANES : (c + 1) * LANES]
            return carry

        lax.fori_loop(0, lat_cells, body, 0)

    look(fields[now], 0)
    for step in range(1, REACH + 1):
        old, new = fields[now], fields[1 - now]

        def body(e, carry, old=old, new=new):
            tangent(old, e, put_in(new, e))
            return carry

        lax.fori_loop(REACH + step, rows - REACH - step, body, 0)
        now = 1 - now
        if step % STEP_WIN == 0:
            look(fields[now], step // STEP_WIN)

    row = iota((SUB, LANES), 0)
    spare = jnp.where(row == 0, sums[0], 0.0)
    if mode != "right":
        spare = jnp.where(row == 1, sums[1], spare)
    top, rest = halves(picked[...])
    values = jnp.concatenate([top, rest], axis=1).astype(BF16)
    chunk = 2 * LANES
    parts = lat_cells * cols
    for c in range(pack.recv // chunk):
        send = send_ref[:, c * chunk : (c + 1) * chunk]
        pick = jnp.where(iota((LANES, chunk), 0) == (send & (LANES - 1)), 1.0, 0.0)
        pick = jnp.concatenate([pick, pick], axis=0).astype(BF16)
        high = send >> log2(LANES)
        every = dot(values, pick)
        typed = []
        for w in range(WIN):
            found = jnp.zeros((SUB, chunk), F32)
            for h in range(parts):
                at = (w * parts + h) * SUB
                found = jnp.where(high == h, every[at : at + SUB], found)
            typed.append(found)
        for t in range(chunk // LANES):
            lanes = slice(t * LANES, (t + 1) * LANES)
            pack.write(out_ref, [x[:, lanes] for x in typed], spare, c * (chunk // LANES) + t)


def call(kernel, out_shapes, args, scalars, scratch, limit=40):
    specs = [pl.BlockSpec(memory_space=pltpu.SMEM)] * scalars
    specs += [pl.BlockSpec(memory_space=pltpu.VMEM)] * (len(args) - scalars)
    return pl.pallas_call(
        kernel,
        out_shape=[jax.ShapeDtypeStruct(s, F32) for s in out_shapes],
        in_specs=specs,
        out_specs=[pl.BlockSpec(memory_space=pltpu.VMEM)] * len(out_shapes),
        scratch_shapes=[pltpu.VMEM(s, F32) for s in scratch],
        compiler_params=pltpu.CompilerParams(vmem_limit_bytes=limit << 20),
    )(*args)


def shards(
    zonal_wind,
    merid_wind,
    operator_rows,
    innovation,
    error_weight,
    interp_weight,
    obs_slot,
    block_count,
    block_type,
    block_window,
    send_cols,
):
    levels, lat_cells, lon_cells = zonal_wind.shape
    types, channels = operator_rows.shape
    layers = channels // levels
    n_lat, n_lon = lax.axis_size("lat"), lax.axis_size("lon")
    recv = send_cols.shape[1]
    blocks = block_count.shape[0]
    pack = Packing(n_lat * n_lon, recv)
    assert types == SUB and lat_cells >= HALO and lon_cells % LANES == 0
    dims = (layers, levels, lat_cells, lon_cells)
    rows, width = lat_cells + 2 * HALO, lon_cells + LANES
    chunks = (pack.devices * pack.rows, LANES)
    block_args = [block_count, block_type, block_window]
    rows_of = lambda x: x.reshape(blocks, BLOCK_ROWS)
    error = rows_of(error_weight)
    total = (pack.rows, pack.devices, LANES)
    band = lax.axis_index("lat")
    edges = jnp.stack([band > 0, band < n_lat - 1]).astype(jnp.int32)
    into = jnp.tile(operator_rows.T, (1, 4))
    back = jnp.tile(operator_rows, (2, 2))

    def exchange(x):
        x = x.reshape(pack.devices, pack.rows, LANES)
        x = lax.all_to_all(x, AXES, split_axis=0, concat_axis=0, tiled=True)
        return x.reshape(chunks)

    def send(x, up, right):
        pairs = [
            (i * n_lon + j, (i + up) * n_lon + (j + right) % n_lon)
            for i in range(n_lat)
            for j in range(n_lon)
            if 0 <= i + up < n_lat
        ]
        return lax.ppermute(x, AXES, pairs)

    def collect(received, with_winds):
        slabs = WIN * lat_cells
        args = [received, send_cols]
        if with_winds:
            slabs += 2 * lat_cells * (levels // SUB)
            args += [x.reshape(levels * lat_cells, lon_cells) for x in (zonal_wind, merid_wind)]
        strip = (SUB, -(-slabs * HALO // LANES) * LANES)
        main, west, east, energy = call(
            functools.partial(collect_kernel, pack, lat_cells, with_winds),
            [(slabs, SUB, lon_cells), strip, strip, (SUB, LANES)],
            args,
            0,
            [(levels * lat_cells, LANES)] * (lon_cells // LANES) if with_winds else [],
        )
        mains = [send(main, 1, 0), main, send(main, -1, 0)]
        strips = []
        for up in (1, 0, -1):
            strips += [send(west, up, -1), send(east, up, 1)]
        return mains + strips, energy

    def model(mode, halos, extra):
        ends = (channels * lat_cells, lon_cells)
        state = (lat_cells + 2 * REACH, channels, width)
        outs = [ends, ends] if mode == "last" else [chunks, state]
        scratch = [(rows, channels, width)] * 2
        scratch += [(WIN, rows, SUB, width), (5, rows, levels, width)]
        if mode == "right":
            outs += [(2, rows, levels, width)]
        if mode == "last":
            scratch += [(ends[0], LANES)] * (2 * lon_cells // LANES)
        if mode != "last":
            scratch = [(WIN * lat_cells * lon_cells // LANES * SUB, LANES)] + scratch
        return call(
            functools.partial(model_kernel, pack, mode, dims),
            outs,
            [edges, *halos, into, back, *extra],
            1,
            scratch,
        )

    def observe(mode, received, extra):
        outs, scratch = [chunks], [total]
        if mode != "right":
            outs += [(blocks, BLOCK_ROWS), (SUB, LANES)]
            scratch += [total]
        return call(
            functools.partial(observe_kernel, pack, mode),
            outs,
            block_args + received + [obs_slot, interp_weight, error] + extra,
            3,
            scratch,
        )

    assert ITERS == 2
    (chunk,) = observe("right", [], [rows_of(innovation)])
    halos, _ = collect(exchange(chunk), True)
    chunk, right, winds = model("right", halos, [send_cols])
    chunk, seen, scalar0 = observe("start", [exchange(chunk)], [])
    halos, energy0 = collect(exchange(chunk), False)
    chunk, residual = model("next", halos, [winds, energy0, scalar0, right, send_cols])
    chunk, seen, scalar1 = observe("next", [exchange(chunk)], [seen, scalar0])
    halos, energy1 = collect(exchange(chunk), False)
    ends = model(
        "last", halos, [winds, energy1, scalar1, residual, energy0, scalar0, right]
    )
    return tuple(x.reshape(layers, levels, lat_cells, lon_cells) for x in ends)


def solution(mesh):
    return jax.shard_map(
        shards,
        mesh=mesh,
        in_specs=(
            P(None, "lat", "lon"),
            P(None, "lat", "lon"),
            P(),
            P(("lat", "lon")),
            P(("lat", "lon")),
            P(None, ("lat", "lon")),
            P(None, ("lat", "lon")),
            P(("lat", "lon")),
            P(("lat", "lon")),
            P(("lat", "lon")),
            P(("lat", "lon"), None),
        ),
        out_specs=(P(None, None, "lat", "lon"), P(None, None, "lat", "lon")),
        check_vma=False,
    )
```

time: 1330 us -> 244 us (0.18)
  other arithmetic: 426 us -> 0.08 us
  local copies, waits for them, and re-layouts: 288 us -> 8.48 us
  waiting for transfers between devices: 228 us -> 7.86 us
  starting transfers between devices: 211 us -> 64.5 us
  Pallas kernels: 0 us -> 86.5 us
  blocking collectives: 150 us -> 72.7 us
    scatter-add x12 -> x0, other arithmetic: 370 us -> none  [the longest x3 260 us: adjoint_model(): jax.ops.segment_sum(terms, flat_index.reshape(-1), num_segments=WIN * TYP...]
    gather x16 -> x0, local copies, waits for them, and re-layouts: 240 us -> none  [the longest x4 181 us: shards(): values = images.reshape(-1)[flat_index]]
    ppermute x84 -> x24, waiting for transfers between devices: 219 us -> 7.86 us  [send(): return lax.ppermute(x, AXES, pairs)]
    ppermute x84 -> x24, starting transfers between devices: 201 us -> 64.5 us  [send(): return lax.ppermute(x, AXES, pairs)]
    psum x3 -> x0, blocking collectives: 116 us -> none  [the longest x2 78.5 us: squares(): return lax.psum(jnp.sum(residual * residual), ('lat', 'lon'))]
    pallas_call x0 -> x9, Pallas kernels: none -> 86.5 us  [call(): pl.pallas_call(kernel, out_shape=[jax.ShapeDtypeStruct(s, F32) for s in o...]
    all_to_all x3 -> x5, blocking collectives: 34.2 us -> 72.7 us  [exchange(): x = lax.all_to_all(x, AXES, split_axis=0, concat_axis=0, tiled=True)]
    slice x22 -> x0, other arithmetic: 16.6 us -> none  [the longest x12 10.7 us: padded(): head = lax.slice_in_dim(cells, 0, width, axis=dim)]
  transfers between devices with their start and end apart: 86 -> 24, of which waited for: 60 -> 6; matrix products, arithmetic and copies ran while one was open for 11% -> 0% of each run, Pallas kernels for 0% -> 0%
where the time goes in v1:
time: 244 us; the launch traced here: 241 us
  Pallas kernels  86.5 us (35%)
  blocking collectives  72.7 us (30%)
  starting transfers between devices  64.5 us (26%)
  local copies, waits for them, and re-layouts  8.48 us (3%)
  waiting for transfers between devices  7.86 us (3%)
    pallas_call x9, Pallas kernels, call(): pl.pallas_call(kernel, out_shape=[jax.ShapeDtypeStruct(s, F32) for s in o...  86.5 us
    all_to_all x5, blocking collectives, exchange(): x = lax.all_to_all(x, AXES, split_axis=0, concat_axis=0, tiled=True)  72.7 us
    ppermute x24, starting transfers between devices, send(): return lax.ppermute(x, AXES, pairs)  64.5 us
    ppermute x24, waiting for transfers between devices, send(): return lax.ppermute(x, AXES, pairs)  7.86 us
    unnamed x36, local copies, waits for them, and re-layouts  7.62 us
  transfers between devices with their start and end apart: 24, of which 6 were waited for; matrix products, arithmetic and copies ran while one was open for 0% of the time, Pallas kernels for 0%

profile of v1, /device:TPU:1, one launch (start us, length us, event | category | flops | bytes accessed | tf_op | source)
XLA Modules:
  0.0 241.0 jit_solution(12386759626791270969)
XLA Ops:
  5.7 3.1 %shard_map.122 = f32[512,128]{1,0:T(8,128)S(1)} custom-call(s32[32]{0:T(128)S(1)} %copy-done.11, s32[32]{0:T(128)S(1)} %copy-done.13, s32[32]{0:T(128)S(1)} %copy-done.15, s32[4,4096]{1,0:T(4,128)S(1)} %copy-done, f32[4,4096]{1,0:T(4,128)S(1)} %copy-done.2, f32[32,128]{1,0:T(8,128)S(1)} %bitcast.31, f32[32,128]{1,0:T(8,128)S(1)} %bitcast.36), custom_call_target="tpu_custom_call" | custom-call | tf_op jit(solution)/shard_map/pallas_call | solution.py:511
  8.9 17.0 %all_to_all.25 = f32[32,16,128]{2,1,0:T(8,128)S(1)} all-to-all(f32[32,16,128]{2,1,0:T(8,128)S(1)} %bitcast.26), channel_id=1, replica_groups=mesh['lat'=4,'lon'=8] {'lat','lon'}, dimensions={0} | all-to-all | bytes 524288 | tf_op jit(solution)/shard_map/all_to_all | solution.py:556
  28.5 1.6 shard_map.123
  30.1 2.5 %collective-permute-start.1 = (f32[56,8,256]{2,1,0:T(8,128)S(1)}, f32[56,8,256]{2,1,0:T(8,128)S(1)}, u32[]{:S(2)}, u32[]{:S(2)}) collective-permute-start(f32[56,8,256]{2,1,0:T(8,128)S(1)} %get-tuple-element.25.refs_1_), channel_id=1, source_target_pairs={{8,0},{9,1},{10,2},{11,3},{12,4},{13,5},{14,6},{15,7},{16,8},{17,9... | collective-permute-start | bytes 1376264 | tf_op jit(solution)/shard_map/ppermute | solution.py:566
  32.6 3.1 %collective-permute-start = (f32[56,8,256]{2,1,0:T(8,128)S(1)}, f32[56,8,256]{2,1,0:T(8,128)S(1)}, u32[]{:S(2)}, u32[]{:S(2)}) collective-permute-start(f32[56,8,256]{2,1,0:T(8,128)S(1)} %get-tuple-element.25.refs_1_), channel_id=1, source_target_pairs={{0,8},{1,9},{2,10},{3,11},{4,12},{5,13},{6,14},{7,15},{8,16},{9,17... | collective-permute-start | bytes 1376264 | tf_op jit(solution)/shard_map/ppermute | solution.py:566
  35.7 2.9 %collective-permute-start.6 = (f32[8,512]{1,0:T(8,128)S(1)}, f32[8,512]{1,0:T(8,128)S(1)}, u32[]{:S(2)}, u32[]{:S(2)}) collective-permute-start(f32[8,512]{1,0:T(8,128)S(1)} %get-tuple-element.26), channel_id=1, source_target_pairs={{8,7},{9,0},{10,1},{11,2},{12,3},{13,4},{14,5},{15,6},{16,15},{17,... | collective-permute-start | bytes 49160 | tf_op jit(solution)/shard_map/ppermute | solution.py:566
  39.1 5.2 %collective-permute-start.2 = (f32[8,512]{1,0:T(8,128)S(1)}, f32[8,512]{1,0:T(8,128)S(1)}, u32[]{:S(2)}, u32[]{:S(2)}) collective-permute-start(f32[8,512]{1,0:T(8,128)S(1)} %get-tuple-element.26), channel_id=1, source_target_pairs={{0,15},{1,8},{2,9},{3,10},{4,11},{5,12},{6,13},{7,14},{8,23},{9,16... | collective-permute-start | bytes 49160 | tf_op jit(solution)/shard_map/ppermute | solution.py:566
  45.0 1.9 collective-permute-start.7
  47.4 5.0 %collective-permute-start.3 = (f32[8,512]{1,0:T(8,128)S(1)}, f32[8,512]{1,0:T(8,128)S(1)}, u32[]{:S(2)}, u32[]{:S(2)}) collective-permute-start(f32[8,512]{1,0:T(8,128)S(1)} %get-tuple-element.27), channel_id=1, source_target_pairs={{0,9},{1,10},{2,11},{3,12},{4,13},{5,14},{6,15},{7,8},{8,17},{9,18... | collective-permute-start | bytes 49160 | tf_op jit(solution)/shard_map/ppermute | solution.py:566
  53.6 1.5 collective-permute-done.3.refs_4_
  55.1 24.4 %shard_map.124 = (f32[512,128]{1,0:T(8,128)S(1)}, f32[16,64,384]{2,1,0:T(8,128)S(1)}, f32[2,24,16,384]{3,2,1,0:T(8,128)S(1)}) custom-call(s32[2]{0:T(128)S(1)} %add_convert_fusion.edge_ref, f32[56,8,256]{2,1,0:T(8,128)S(1)} %collective-permute-done.refs_0_, f32[56,8,256]{2,1,0:T(8,128)S(1)} %get-tuple-element.25.refs_1_, ...), custom_call_target="tpu_custom_call" | custom-call | tf_op jit(solution)/shard_map/pallas_call | solution.py:511
  79.5 15.0 %all_to_all.26 = f32[32,16,128]{2,1,0:T(8,128)S(1)} all-to-all(f32[32,16,128]{2,1,0:T(8,128)S(1)} %bitcast.27), channel_id=1, replica_groups=mesh['lat'=4,'lon'=8] {'lat','lon'}, dimensions={0} | all-to-all | bytes 524288 | tf_op jit(solution)/shard_map/all_to_all | solution.py:556
  94.6 7.9 %shard_map.125 = (f32[512,128]{1,0:T(8,128)S(1)}, f32[32,128]{1,0:T(8,128)S(1)}, f32[8,128]{1,0:T(8,128)S(1)}) custom-call(s32[32]{0:T(128)S(1)} %copy-done.12, s32[32]{0:T(128)S(1)} %copy-done.14, s32[32]{0:T(128)S(1)} %copy-done.16, f32[512,128]{1,0:T(8,128)S(1)} %bitcast.21, s32[4,4096]{1,0:T(4,128)S(1)} %copy-done.1, f32[4,4096]{1,0:T(4,128)S(1)} %copy-done.3, ...), custom_call_target="tpu_custom_call" | custom-call | tf_op jit(solution)/shard_map/pallas_call | solution.py:511
  102.5 12.8 %all_to_all.27 = f32[32,16,128]{2,1,0:T(8,128)S(1)} all-to-all(f32[32,16,128]{2,1,0:T(8,128)S(1)} %bitcast.30), channel_id=1, replica_groups=mesh['lat'=4,'lon'=8] {'lat','lon'}, dimensions={0} | all-to-all | bytes 524288 | tf_op jit(solution)/shard_map/all_to_all | solution.py:556
  116.4 2.5 %collective-permute-start.9 = (f32[24,8,256]{2,1,0:T(8,128)S(1)}, f32[24,8,256]{2,1,0:T(8,128)S(1)}, u32[]{:S(2)}, u32[]{:S(2)}) collective-permute-start(f32[24,8,256]{2,1,0:T(8,128)S(1)} %get-tuple-element.30.refs_1_), channel_id=1, source_target_pairs={{8,0},{9,1},{10,2},{11,3},{12,4},{13,5},{14,6},{15,7},{16,8},{17,9... | collective-permute-start | bytes 589832 | tf_op jit(solution)/shard_map/ppermute | solution.py:566
  118.9 3.1 %collective-permute-start.8 = (f32[24,8,256]{2,1,0:T(8,128)S(1)}, f32[24,8,256]{2,1,0:T(8,128)S(1)}, u32[]{:S(2)}, u32[]{:S(2)}) collective-permute-start(f32[24,8,256]{2,1,0:T(8,128)S(1)} %get-tuple-element.30.refs_1_), channel_id=1, source_target_pairs={{0,8},{1,9},{2,10},{3,11},{4,12},{5,13},{6,14},{7,15},{8,16},{9,17... | collective-permute-start | bytes 589832 | tf_op jit(solution)/shard_map/ppermute | solution.py:566
  122.0 2.9 %collective-permute-start.14 = (f32[8,256]{1,0:T(8,128)S(1)}, f32[8,256]{1,0:T(8,128)S(1)}, u32[]{:S(2)}, u32[]{:S(2)}) collective-permute-start(f32[8,256]{1,0:T(8,128)S(1)} %get-tuple-element.31), channel_id=1, source_target_pairs={{8,7},{9,0},{10,1},{11,2},{12,3},{13,4},{14,5},{15,6},{16,15},{17,... | collective-permute-start | bytes 24584 | tf_op jit(solution)/shard_map/ppermute | solution.py:566
  125.4 5.2 %collective-permute-start.10 = (f32[8,256]{1,0:T(8,128)S(1)}, f32[8,256]{1,0:T(8,128)S(1)}, u32[]{:S(2)}, u32[]{:S(2)}) collective-permute-start(f32[8,256]{1,0:T(8,128)S(1)} %get-tuple-element.31), channel_id=1, source_target_pairs={{0,15},{1,8},{2,9},{3,10},{4,11},{5,12},{6,13},{7,14},{8,23},{9,16... | collective-permute-start | bytes 24584 | tf_op jit(solution)/shard_map/ppermute | solution.py:566
  130.6 1.9 collective-permute-start.15
  133.0 5.0 %collective-permute-start.11 = (f32[8,256]{1,0:T(8,128)S(1)}, f32[8,256]{1,0:T(8,128)S(1)}, u32[]{:S(2)}, u32[]{:S(2)}) collective-permute-start(f32[8,256]{1,0:T(8,128)S(1)} %get-tuple-element.32), channel_id=1, source_target_pairs={{0,9},{1,10},{2,11},{3,12},{4,13},{5,14},{6,15},{7,8},{8,17},{9,18... | collective-permute-start | bytes 24584 | tf_op jit(solution)/shard_map/ppermute | solution.py:566
  140.7 24.4 %shard_map.127 = (f32[512,128]{1,0:T(8,128)S(1)}, f32[16,64,384]{2,1,0:T(8,128)S(1)}) custom-call(s32[2]{0:T(128)S(1)} %add_convert_fusion.edge_ref, f32[24,8,256]{2,1,0:T(8,128)S(1)} %collective-permute-done.8.refs_0_, f32[24,8,256]{2,1,0:T(8,128)S(1)} %get-tuple-element.30.refs_1_, f32[24,8,256]{2,1,0:T(8,128)S(1)} %collective-permute-done.9.refs_2_, ...), custom_call_target="tpu_custom_call" | custom-call | tf_op jit(solution)/shard_map/pallas_call | solution.py:511
  165.1 15.1 %all_to_all.28 = f32[32,16,128]{2,1,0:T(8,128)S(1)} all-to-all(f32[32,16,128]{2,1,0:T(8,128)S(1)} %bitcast.28), channel_id=1, replica_groups=mesh['lat'=4,'lon'=8] {'lat','lon'}, dimensions={0} | all-to-all | bytes 524288 | tf_op jit(solution)/shard_map/all_to_all | solution.py:556
  180.1 8.3 %shard_map.128 = (f32[512,128]{1,0:T(8,128)S(1)}, f32[32,128]{1,0:T(8,128)}, f32[8,128]{1,0:T(8,128)S(1)}) custom-call(s32[32]{0:T(128)S(1)} %copy-done.12, s32[32]{0:T(128)S(1)} %copy-done.14, s32[32]{0:T(128)S(1)} %copy-done.16, f32[512,128]{1,0:T(8,128)S(1)} %bitcast.22, s32[4,4096]{1,0:T(4,128)S(1)} %copy-done.1, f32[4,4096]{1,0:T(4,128)S(1)} %copy-done.3, ...), custom_call_target="tpu_custom_call" | custom-call | tf_op jit(solution)/shard_map/pallas_call | solution.py:511
  188.4 12.8 %all_to_all.29 = f32[32,16,128]{2,1,0:T(8,128)S(1)} all-to-all(f32[32,16,128]{2,1,0:T(8,128)S(1)} %bitcast.29), channel_id=1, replica_groups=mesh['lat'=4,'lon'=8] {'lat','lon'}, dimensions={0} | all-to-all | bytes 524288 | tf_op jit(solution)/shard_map/all_to_all | solution.py:556
  202.3 2.5 %collective-permute-start.17 = (f32[24,8,256]{2,1,0:T(8,128)S(1)}, f32[24,8,256]{2,1,0:T(8,128)S(1)}, u32[]{:S(2)}, u32[]{:S(2)}) collective-permute-start(f32[24,8,256]{2,1,0:T(8,128)S(1)} %get-tuple-element.40.refs_1_), channel_id=1, source_target_pairs={{8,0},{9,1},{10,2},{11,3},{12,4},{13,5},{14,6},{15,7},{16,8},{17,9... | collective-permute-start | bytes 589832 | tf_op jit(solution)/shard_map/ppermute | solution.py:566
  204.8 3.1 %collective-permute-start.16 = (f32[24,8,256]{2,1,0:T(8,128)S(1)}, f32[24,8,256]{2,1,0:T(8,128)S(1)}, u32[]{:S(2)}, u32[]{:S(2)}) collective-permute-start(f32[24,8,256]{2,1,0:T(8,128)S(1)} %get-tuple-element.40.refs_1_), channel_id=1, source_target_pairs={{0,8},{1,9},{2,10},{3,11},{4,12},{5,13},{6,14},{7,15},{8,16},{9,17... | collective-permute-start | bytes 589832 | tf_op jit(solution)/shard_map/ppermute | solution.py:566
  207.9 2.9 %collective-permute-start.22 = (f32[8,256]{1,0:T(8,128)S(1)}, f32[8,256]{1,0:T(8,128)S(1)}, u32[]{:S(2)}, u32[]{:S(2)}) collective-permute-start(f32[8,256]{1,0:T(8,128)S(1)} %get-tuple-element.41), channel_id=1, source_target_pairs={{8,7},{9,0},{10,1},{11,2},{12,3},{13,4},{14,5},{15,6},{16,15},{17,... | collective-permute-start | bytes 24584 | tf_op jit(solution)/shard_map/ppermute | solution.py:566
  211.3 5.2 %collective-permute-start.18 = (f32[8,256]{1,0:T(8,128)S(1)}, f32[8,256]{1,0:T(8,128)S(1)}, u32[]{:S(2)}, u32[]{:S(2)}) collective-permute-start(f32[8,256]{1,0:T(8,128)S(1)} %get-tuple-element.41), channel_id=1, source_target_pairs={{0,15},{1,8},{2,9},{3,10},{4,11},{5,12},{6,13},{7,14},{8,23},{9,16... | collective-permute-start | bytes 24584 | tf_op jit(solution)/shard_map/ppermute | solution.py:566
  216.5 1.9 collective-permute-start.23
  218.9 5.0 %collective-permute-start.19 = (f32[8,256]{1,0:T(8,128)S(1)}, f32[8,256]{1,0:T(8,128)S(1)}, u32[]{:S(2)}, u32[]{:S(2)}) collective-permute-start(f32[8,256]{1,0:T(8,128)S(1)} %get-tuple-element.42), channel_id=1, source_target_pairs={{0,9},{1,10},{2,11},{3,12},{4,13},{5,14},{6,15},{7,8},{8,17},{9,18... | collective-permute-start | bytes 24584 | tf_op jit(solution)/shard_map/ppermute | solution.py:566
  225.1 1.5 collective-permute-done.19.refs_4_
  226.6 14.5 %shard_map.130 = (f32[512,256]{1,0:T(8,128)}, f32[512,256]{1,0:T(8,128)}) custom-call(s32[2]{0:T(128)S(1)} %add_convert_fusion.edge_ref, f32[24,8,256]{2,1,0:T(8,128)S(1)} %collective-permute-done.16.refs_0_, f32[24,8,256]{2,1,0:T(8,128)S(1)} %get-tuple-element.40.refs_1_, f32[24,8,256]{2,1,0:T(8,128)S(1)} %collective-permute-done.17.refs_2_, ...), custom_call_target="tpu_custom_call" | custom-call | tf_op jit(solution)/shard_map/pallas_call | solution.py:511
  (71 shorter events, 18.3 us)
Async XLA Ops:
  5.7 46.8 %copy-start.17 = (f32[8,64]{1,0:T(8,128)S(1)}, f32[8,64]{1,0:T(8,128)}, u32[]{:S(2)}) copy-start(f32[8,64]{1,0:T(8,128)} %param.13) | copy-start | bytes 6148
  5.7 49.4 %copy-start.5 = (s32[1,2048]{1,0:T(1,128)S(1)}, s32[1,2048]{1,0:T(1,128)}, u32[]{:S(2)}) copy-start(s32[1,2048]{1,0:T(1,128)} %refs_1_.11) | copy-start | bytes 24580
  8.9 85.7 %copy-start.1 = (s32[4,4096]{1,0:T(4,128)S(1)}, s32[4,4096]{1,0:T(4,128)}, u32[]{:S(2)}) copy-start(s32[4,4096]{1,0:T(4,128)} %refs_1_.10) | copy-start | bytes 196612
  8.9 85.7 %copy-start.3 = (f32[4,4096]{1,0:T(4,128)S(1)}, f32[4,4096]{1,0:T(4,128)}, u32[]{:S(2)}) copy-start(f32[4,4096]{1,0:T(4,128)} %refs_2_.3) | copy-start | bytes 196612
  8.9 85.6 %copy-start.7 = (f32[4096]{0:T(1024)S(1)}, f32[4096]{0:T(1024)}, u32[]{:S(2)}) copy-start(f32[4096]{0:T(1024)} %param.15) | copy-start | bytes 49156
  8.9 85.6 %copy-start.12 = (s32[32]{0:T(128)S(1)}, s32[32]{0:T(128)}, u32[]{:S(2)}) copy-start(s32[32]{0:T(128)} %count_ref.5) | copy-start | bytes 388
  8.9 85.6 %copy-start.14 = (s32[32]{0:T(128)S(1)}, s32[32]{0:T(128)}, u32[]{:S(2)}) copy-start(s32[32]{0:T(128)} %type_ref.5) | copy-start | bytes 388
  8.9 85.6 %copy-start.16 = (s32[32]{0:T(128)S(1)}, s32[32]{0:T(128)}, u32[]{:S(2)}) copy-start(s32[32]{0:T(128)} %window_ref.5) | copy-start | bytes 388
  30.1 25.0 %collective-permute-start.1 = (f32[56,8,256]{2,1,0:T(8,128)S(1)}, f32[56,8,256]{2,1,0:T(8,128)S(1)}, u32[]{:S(2)}, u32[]{:S(2)}) collective-permute-start(f32[56,8,256]{2,1,0:T(8,128)S(1)} %get-tuple-element.25.refs_1_), channel_id=1, source_target_pairs={{8,0},{9,1},{10,2},{11,3},{12,4},{13,5},{14,6},{15,7},{16,8},{17,9... | collective-permute-start | bytes 1376264 | tf_op jit(solution)/shard_map/ppermute | solution.py:566
  32.6 22.5 %collective-permute-start = (f32[56,8,256]{2,1,0:T(8,128)S(1)}, f32[56,8,256]{2,1,0:T(8,128)S(1)}, u32[]{:S(2)}, u32[]{:S(2)}) collective-permute-start(f32[56,8,256]{2,1,0:T(8,128)S(1)} %get-tuple-element.25.refs_1_), channel_id=1, source_target_pairs={{0,8},{1,9},{2,10},{3,11},{4,12},{5,13},{6,14},{7,15},{8,16},{9,17... | collective-permute-start | bytes 1376264 | tf_op jit(solution)/shard_map/ppermute | solution.py:566
  35.7 9.3 %collective-permute-start.6 = (f32[8,512]{1,0:T(8,128)S(1)}, f32[8,512]{1,0:T(8,128)S(1)}, u32[]{:S(2)}, u32[]{:S(2)}) collective-permute-start(f32[8,512]{1,0:T(8,128)S(1)} %get-tuple-element.26), channel_id=1, source_target_pairs={{8,7},{9,0},{10,1},{11,2},{12,3},{13,4},{14,5},{15,6},{16,15},{17,... | collective-permute-start | bytes 49160 | tf_op jit(solution)/shard_map/ppermute | solution.py:566
  38.6 8.3 %collective-permute-start.4 = (f32[8,512]{1,0:T(8,128)S(1)}, f32[8,512]{1,0:T(8,128)S(1)}, u32[]{:S(2)}, u32[]{:S(2)}) collective-permute-start(f32[8,512]{1,0:T(8,128)S(1)} %get-tuple-element.26), channel_id=1, source_target_pairs={{0,7},{1,0},{2,1},{3,2},{4,3},{5,4},{6,5},{7,6},{8,15},{9,8},{10,9... | collective-permute-start | bytes 49160 | tf_op jit(solution)/shard_map/ppermute | solution.py:566
  39.1 8.3 %collective-permute-start.2 = (f32[8,512]{1,0:T(8,128)S(1)}, f32[8,512]{1,0:T(8,128)S(1)}, u32[]{:S(2)}, u32[]{:S(2)}) collective-permute-start(f32[8,512]{1,0:T(8,128)S(1)} %get-tuple-element.26), channel_id=1, source_target_pairs={{0,15},{1,8},{2,9},{3,10},{4,11},{5,12},{6,13},{7,14},{8,23},{9,16... | collective-permute-start | bytes 49160 | tf_op jit(solution)/shard_map/ppermute | solution.py:566
  45.0 8.6 %collective-permute-start.7 = (f32[8,512]{1,0:T(8,128)S(1)}, f32[8,512]{1,0:T(8,128)S(1)}, u32[]{:S(2)}, u32[]{:S(2)}) collective-permute-start(f32[8,512]{1,0:T(8,128)S(1)} %get-tuple-element.27), channel_id=1, source_target_pairs={{8,1},{9,2},{10,3},{11,4},{12,5},{13,6},{14,7},{15,0},{16,9},{17,1... | collective-permute-start | bytes 49160 | tf_op jit(solution)/shard_map/ppermute | solution.py:566
  46.9 6.7 %collective-permute-start.5 = (f32[8,512]{1,0:T(8,128)S(1)}, f32[8,512]{1,0:T(8,128)S(1)}, u32[]{:S(2)}, u32[]{:S(2)}) collective-permute-start(f32[8,512]{1,0:T(8,128)S(1)} %get-tuple-element.27), channel_id=1, source_target_pairs={{0,1},{1,2},{2,3},{3,4},{4,5},{5,6},{6,7},{7,0},{8,9},{9,10},{10,1... | collective-permute-start | bytes 49160 | tf_op jit(solution)/shard_map/ppermute | solution.py:566
  47.4 7.7 %collective-permute-start.3 = (f32[8,512]{1,0:T(8,128)S(1)}, f32[8,512]{1,0:T(8,128)S(1)}, u32[]{:S(2)}, u32[]{:S(2)}) collective-permute-start(f32[8,512]{1,0:T(8,128)S(1)} %get-tuple-element.27), channel_id=1, source_target_pairs={{0,9},{1,10},{2,11},{3,12},{4,13},{5,14},{6,15},{7,8},{8,17},{9,18... | collective-permute-start | bytes 49160 | tf_op jit(solution)/shard_map/ppermute | solution.py:566
  116.4 24.2 %collective-permute-start.9 = (f32[24,8,256]{2,1,0:T(8,128)S(1)}, f32[24,8,256]{2,1,0:T(8,128)S(1)}, u32[]{:S(2)}, u32[]{:S(2)}) collective-permute-start(f32[24,8,256]{2,1,0:T(8,128)S(1)} %get-tuple-element.30.refs_1_), channel_id=1, source_target_pairs={{8,0},{9,1},{10,2},{11,3},{12,4},{13,5},{14,6},{15,7},{16,8},{17,9... | collective-permute-start | bytes 589832 | tf_op jit(solution)/shard_map/ppermute | solution.py:566
  118.9 21.7 %collective-permute-start.8 = (f32[24,8,256]{2,1,0:T(8,128)S(1)}, f32[24,8,256]{2,1,0:T(8,128)S(1)}, u32[]{:S(2)}, u32[]{:S(2)}) collective-permute-start(f32[24,8,256]{2,1,0:T(8,128)S(1)} %get-tuple-element.30.refs_1_), channel_id=1, source_target_pairs={{0,8},{1,9},{2,10},{3,11},{4,12},{5,13},{6,14},{7,15},{8,16},{9,17... | collective-permute-start | bytes 589832 | tf_op jit(solution)/shard_map/ppermute | solution.py:566
  122.0 8.6 %collective-permute-start.14 = (f32[8,256]{1,0:T(8,128)S(1)}, f32[8,256]{1,0:T(8,128)S(1)}, u32[]{:S(2)}, u32[]{:S(2)}) collective-permute-start(f32[8,256]{1,0:T(8,128)S(1)} %get-tuple-element.31), channel_id=1, source_target_pairs={{8,7},{9,0},{10,1},{11,2},{12,3},{13,4},{14,5},{15,6},{16,15},{17,... | collective-permute-start | bytes 24584 | tf_op jit(solution)/shard_map/ppermute | solution.py:566
  124.9 7.6 %collective-permute-start.12 = (f32[8,256]{1,0:T(8,128)S(1)}, f32[8,256]{1,0:T(8,128)S(1)}, u32[]{:S(2)}, u32[]{:S(2)}) collective-permute-start(f32[8,256]{1,0:T(8,128)S(1)} %get-tuple-element.31), channel_id=1, source_target_pairs={{0,7},{1,0},{2,1},{3,2},{4,3},{5,4},{6,5},{7,6},{8,15},{9,8},{10,9... | collective-permute-start | bytes 24584 | tf_op jit(solution)/shard_map/ppermute | solution.py:566
  125.4 7.6 %collective-permute-start.10 = (f32[8,256]{1,0:T(8,128)S(1)}, f32[8,256]{1,0:T(8,128)S(1)}, u32[]{:S(2)}, u32[]{:S(2)}) collective-permute-start(f32[8,256]{1,0:T(8,128)S(1)} %get-tuple-element.31), channel_id=1, source_target_pairs={{0,15},{1,8},{2,9},{3,10},{4,11},{5,12},{6,13},{7,14},{8,23},{9,16... | collective-permute-start | bytes 24584 | tf_op jit(solution)/shard_map/ppermute | solution.py:566
  130.6 8.6 %collective-permute-start.15 = (f32[8,256]{1,0:T(8,128)S(1)}, f32[8,256]{1,0:T(8,128)S(1)}, u32[]{:S(2)}, u32[]{:S(2)}) collective-permute-start(f32[8,256]{1,0:T(8,128)S(1)} %get-tuple-element.32), channel_id=1, source_target_pairs={{8,1},{9,2},{10,3},{11,4},{12,5},{13,6},{14,7},{15,0},{16,9},{17,1... | collective-permute-start | bytes 24584 | tf_op jit(solution)/shard_map/ppermute | solution.py:566
  132.6 6.6 %collective-permute-start.13 = (f32[8,256]{1,0:T(8,128)S(1)}, f32[8,256]{1,0:T(8,128)S(1)}, u32[]{:S(2)}, u32[]{:S(2)}) collective-permute-start(f32[8,256]{1,0:T(8,128)S(1)} %get-tuple-element.32), channel_id=1, source_target_pairs={{0,1},{1,2},{2,3},{3,4},{4,5},{5,6},{6,7},{7,0},{8,9},{9,10},{10,1... | collective-permute-start | bytes 24584 | tf_op jit(solution)/shard_map/ppermute | solution.py:566
  133.0 7.7 %collective-permute-start.11 = (f32[8,256]{1,0:T(8,128)S(1)}, f32[8,256]{1,0:T(8,128)S(1)}, u32[]{:S(2)}, u32[]{:S(2)}) collective-permute-start(f32[8,256]{1,0:T(8,128)S(1)} %get-tuple-element.32), channel_id=1, source_target_pairs={{0,9},{1,10},{2,11},{3,12},{4,13},{5,14},{6,15},{7,8},{8,17},{9,18... | collective-permute-start | bytes 24584 | tf_op jit(solution)/shard_map/ppermute | solution.py:566
  202.3 24.2 %collective-permute-start.17 = (f32[24,8,256]{2,1,0:T(8,128)S(1)}, f32[24,8,256]{2,1,0:T(8,128)S(1)}, u32[]{:S(2)}, u32[]{:S(2)}) collective-permute-start(f32[24,8,256]{2,1,0:T(8,128)S(1)} %get-tuple-element.40.refs_1_), channel_id=1, source_target_pairs={{8,0},{9,1},{10,2},{11,3},{12,4},{13,5},{14,6},{15,7},{16,8},{17,9... | collective-permute-start | bytes 589832 | tf_op jit(solution)/shard_map/ppermute | solution.py:566
  204.8 21.7 %collective-permute-start.16 = (f32[24,8,256]{2,1,0:T(8,128)S(1)}, f32[24,8,256]{2,1,0:T(8,128)S(1)}, u32[]{:S(2)}, u32[]{:S(2)}) collective-permute-start(f32[24,8,256]{2,1,0:T(8,128)S(1)} %get-tuple-element.40.refs_1_), channel_id=1, source_target_pairs={{0,8},{1,9},{2,10},{3,11},{4,12},{5,13},{6,14},{7,15},{8,16},{9,17... | collective-permute-start | bytes 589832 | tf_op jit(solution)/shard_map/ppermute | solution.py:566
  207.9 8.6 %collective-permute-start.22 = (f32[8,256]{1,0:T(8,128)S(1)}, f32[8,256]{1,0:T(8,128)S(1)}, u32[]{:S(2)}, u32[]{:S(2)}) collective-permute-start(f32[8,256]{1,0:T(8,128)S(1)} %get-tuple-element.41), channel_id=1, source_target_pairs={{8,7},{9,0},{10,1},{11,2},{12,3},{13,4},{14,5},{15,6},{16,15},{17,... | collective-permute-start | bytes 24584 | tf_op jit(solution)/shard_map/ppermute | solution.py:566
  210.8 7.6 %collective-permute-start.20 = (f32[8,256]{1,0:T(8,128)S(1)}, f32[8,256]{1,0:T(8,128)S(1)}, u32[]{:S(2)}, u32[]{:S(2)}) collective-permute-start(f32[8,256]{1,0:T(8,128)S(1)} %get-tuple-element.41), channel_id=1, source_target_pairs={{0,7},{1,0},{2,1},{3,2},{4,3},{5,4},{6,5},{7,6},{8,15},{9,8},{10,9... | collective-permute-start | bytes 24584 | tf_op jit(solution)/shard_map/ppermute | solution.py:566
  211.3 7.6 %collective-permute-start.18 = (f32[8,256]{1,0:T(8,128)S(1)}, f32[8,256]{1,0:T(8,128)S(1)}, u32[]{:S(2)}, u32[]{:S(2)}) collective-permute-start(f32[8,256]{1,0:T(8,128)S(1)} %get-tuple-element.41), channel_id=1, source_target_pairs={{0,15},{1,8},{2,9},{3,10},{4,11},{5,12},{6,13},{7,14},{8,23},{9,16... | collective-permute-start | bytes 24584 | tf_op jit(solution)/shard_map/ppermute | solution.py:566
  216.5 8.6 %collective-permute-start.23 = (f32[8,256]{1,0:T(8,128)S(1)}, f32[8,256]{1,0:T(8,128)S(1)}, u32[]{:S(2)}, u32[]{:S(2)}) collective-permute-start(f32[8,256]{1,0:T(8,128)S(1)} %get-tuple-element.42), channel_id=1, source_target_pairs={{8,1},{9,2},{10,3},{11,4},{12,5},{13,6},{14,7},{15,0},{16,9},{17,1... | collective-permute-start | bytes 24584 | tf_op jit(solution)/shard_map/ppermute | solution.py:566
  218.5 6.6 %collective-permute-start.21 = (f32[8,256]{1,0:T(8,128)S(1)}, f32[8,256]{1,0:T(8,128)S(1)}, u32[]{:S(2)}, u32[]{:S(2)}) collective-permute-start(f32[8,256]{1,0:T(8,128)S(1)} %get-tuple-element.42), channel_id=1, source_target_pairs={{0,1},{1,2},{2,3},{3,4},{4,5},{5,6},{6,7},{7,0},{8,9},{9,10},{10,1... | collective-permute-start | bytes 24584 | tf_op jit(solution)/shard_map/ppermute | solution.py:566
  218.9 7.7 %collective-permute-start.19 = (f32[8,256]{1,0:T(8,128)S(1)}, f32[8,256]{1,0:T(8,128)S(1)}, u32[]{:S(2)}, u32[]{:S(2)}) collective-permute-start(f32[8,256]{1,0:T(8,128)S(1)} %get-tuple-element.42), channel_id=1, source_target_pairs={{0,9},{1,10},{2,11},{3,12},{4,13},{5,14},{6,15},{7,8},{8,17},{9,18... | collective-permute-start | bytes 24584 | tf_op jit(solution)/shard_map/ppermute | solution.py:566
  (10 other events, 7.6 us)

commit v2 on v1

--- a/solution.py
+++ b/solution.py
@@ -37,6 +37,23 @@
 
 def dot(a, b):
     return jnp.dot(a, b, preferred_element_type=F32)
+
+
+def loop(low, high, step, body, carry=0):
+    count = high - low
+    while count % step:
+        step -= 1
+
+    def some(i, carry):
+        for k in range(step):
+            carry = body(low + i * step + k, carry)
+        return carry
+
+    return lax.fori_loop(0, count // step, some, carry)
+
+
+def trims(halo):
+    return [max(halo - STEP_WIN * (WIN - 1 - w), 0) for w in range(WIN)]
 
 
 class Packing:
@@ -95,7 +112,19 @@
 
 def observe_kernel(pack, mode, count_ref, type_ref, window_ref, *refs):
     if mode == "right":
-        slot_ref, weight_ref, error_ref, value_ref, out_ref, total = refs
+        far = (count_ref, type_ref, window_ref) + refs[:4]
+        out_ref, total = refs[4:6]
+        near, done = refs[6:-1], refs[-1]
+        copies = [
+            pltpu.make_async_copy(src, dst, done.at[i])
+            for i, (src, dst) in enumerate(zip(far, near))
+        ]
+        for copy in copies:
+            copy.start()
+        total[...] = jnp.zeros_like(total)
+        for copy in copies:
+            copy.wait()
+        count_ref, type_ref, window_ref, slot_ref, weight_ref, error_ref, value_ref = near
     else:
         if mode == "start":
             recv_ref, slot_ref, weight_ref, error_ref = refs[:4]
@@ -109,8 +138,8 @@
     devices = pack.devices
     wide = points * BLOCK_ROWS
     spare = pack.spare_tile * SUB
-    total[...] = jnp.zeros_like(total)
     if mode != "right":
+        total[...] = jnp.zeros_like(total)
         for j in range(pack.rows):
             table[j] = recv_ref[pl.ds(j, devices, stride=pack.rows), :]
         norm = pack.spare(jnp.sum(table[spare], axis=0, keepdims=True))
@@ -123,49 +152,71 @@
         row = iota((SUB, LANES), 0)
         scalar_ref[...] = jnp.where(row == 0, norm, jnp.where(row == 1, ratio, square))
 
-    def one(b, energy):
-        window = window_ref[b]
-        j = (window >> log2(pack.per)) * SUB + type_ref[b]
-        shift = (window & (pack.per - 1)) * pack.slots
-        lanes = pl.ds(pl.multiple_of(b * BLOCK_ROWS, BLOCK_ROWS), BLOCK_ROWS)
-        slot = slot_ref[:, lanes]
-        weight = weight_ref[:, lanes]
-        device = slot >> pack.group_bits
-        lane = (slot & (pack.slots - 1)) + shift
-        ids = iota((LANES, BLOCK_ROWS), 0)
-        pick = jnp.concatenate(
-            [jnp.where(ids == lane[k : k + 1, :], 1.0, 0.0) for k in range(points)], axis=1
-        ).astype(BF16)
-        device = jnp.concatenate([device[k : k + 1, :] for k in range(points)], axis=1)
-        weight = jnp.concatenate([weight[k : k + 1, :] for k in range(points)], axis=1)
-        owner = iota((devices, wide), 0) == device
+    ids = iota((LANES, BLOCK_ROWS), 0)
+
+    def row(x):
+        return jnp.concatenate([x[k : k + 1, :] for k in range(points)], axis=1)
+
+    def some(first, energy):
+        group = [first * together + i for i in range(together)]
+        places, picks, owners, weights, values = [], [], [], [], []
+        for b in group:
+            window = window_ref[b]
+            places.append((window >> log2(pack.per)) * SUB + type_ref[b])
+            shift = (window & (pack.per - 1)) * pack.slots
+            lanes = pl.ds(pl.multiple_of(b * BLOCK_ROWS, BLOCK_ROWS), BLOCK_ROWS)
+            slot = slot_ref[:, lanes]
+            lane = (slot & (pack.slots - 1)) + shift
+            picks.append(
+                jnp.concatenate(
+                    [jnp.where(ids == lane[k : k + 1, :], 1.0, 0.0) for k in range(points)],
+                    axis=1,
+                ).astype(BF16)
+            )
+            owners.append(iota((devices, wide), 0) == row(slot >> pack.group_bits))
+            weights.append(row(weight_ref[:, lanes]))
         if mode == "right":
-            value = value_ref[pl.ds(b, 1), :]
+            values = [value_ref[pl.ds(b, 1), :] for b in group]
         else:
-            top, rest = halves(table[j])
-            both = dot(jnp.concatenate([top, rest], axis=0).astype(BF16), pick)
-            both = both[:devices] + both[devices:]
-            found = jnp.sum(jnp.where(owner, both, 0.0), axis=0, keepdims=True) * weight
-            value = found[:, :BLOCK_ROWS]
-            for k in range(1, points):
-                value = value + found[:, k * BLOCK_ROWS : (k + 1) * BLOCK_ROWS]
-            if mode == "next":
-                value = value + ratio * value_ref[pl.ds(b, 1), :]
-            observed_ref[pl.ds(b, 1), :] = value
-        live = iota((1, BLOCK_ROWS), 1) < count_ref[b]
-        weighted = jnp.where(live, error_ref[pl.ds(b, 1), :], 0.0) * value
-        spread = jnp.concatenate([weighted] * points, axis=1) * weight
-        top, rest = halves(jnp.where(owner, spread, 0.0))
-        both = lax.dot_general(
-            jnp.concatenate([top, rest], axis=0).astype(BF16),
-            pick,
-            NT,
-            preferred_element_type=F32,
-        )
-        total[j] += both[:devices] + both[devices:]
-        return energy + weighted * value
-
-    energy = lax.fori_loop(0, blocks, one, jnp.zeros((1, BLOCK_ROWS), F32), unroll=4)
+            found = []
+            for j, pick in zip(places, picks):
+                top, rest = halves(table[j])
+                found.append(dot(jnp.concatenate([top, rest], axis=0).astype(BF16), pick))
+            for b, both, owner, weight in zip(group, found, owners, weights):
+                both = both[:devices] + both[devices:]
+                both = jnp.sum(jnp.where(owner, both, 0.0), axis=0, keepdims=True) * weight
+                value = both[:, :BLOCK_ROWS]
+                for k in range(1, points):
+                    value = value + both[:, k * BLOCK_ROWS : (k + 1) * BLOCK_ROWS]
+                if mode == "next":
+                    value = value + ratio * value_ref[pl.ds(b, 1), :]
+                values.append(value)
+            for b, value in zip(group, values):
+                observed_ref[pl.ds(b, 1), :] = value
+        sums = []
+        for b, pick, owner, weight, value in zip(group, picks, owners, weights, values):
+            live = iota((1, BLOCK_ROWS), 1) < count_ref[b]
+            weighted = jnp.where(live, error_ref[pl.ds(b, 1), :], 0.0) * value
+            energy = energy + weighted * value
+            spread = jnp.concatenate([weighted] * points, axis=1) * weight
+            top, rest = halves(jnp.where(owner, spread, 0.0))
+            sums.append(
+                lax.dot_general(
+                    jnp.concatenate([top, rest], axis=0).astype(BF16),
+                    pick,
+                    NT,
+                    preferred_element_type=F32,
+                )
+            )
+        for j, both in zip(places, sums):
+            total[j] += both[:devices] + both[devices:]
+        return energy
+
+    together = 8
+    while blocks % together:
+        together -= 1
+    energy = jnp.zeros((1, BLOCK_ROWS), F32)
+    energy = lax.fori_loop(0, blocks // together, some, energy)
     energy = jnp.sum(energy, axis=1, keepdims=True)
     for j in range(pack.rows):
         chunk = total[j]
@@ -182,6 +233,14 @@
         recv_ref, send_ref = refs[:2]
         refs = refs[2:]
     main_ref, west_ref, east_ref, scalar_ref = refs[:4]
+    if with_winds:
+        held, near, done = refs[4:-3], refs[-3:-1], refs[-1]
+        copies = [
+            pltpu.make_async_copy(src, dst, done.at[i])
+            for i, (src, dst) in enumerate(zip((zonal_ref, merid_ref), near))
+        ]
+        for copy in copies:
+            copy.start()
     lon_cells = main_ref.shape[2]
     cols = lon_cells // LANES
     tiles = pack.recv // LANES
@@ -223,10 +282,10 @@
     if with_winds:
         slab = WIN * lat_cells
         levels = zonal_ref.shape[0] // lat_cells
-        held = refs[4:]
-        for ref in (zonal_ref, merid_ref):
+        for which in range(2):
+            copies[which].wait()
             for c in range(cols):
-                held[c][...] = ref[:, c * LANES : (c + 1) * LANES]
+                held[c][...] = near[which][:, c * LANES : (c + 1) * LANES]
             for row in range(lat_cells):
                 for part in range(levels // SUB):
                     at = pl.ds(part * SUB * lat_cells + row, SUB, stride=lat_cells)
@@ -244,12 +303,34 @@
     scalar_ref[...] = jnp.broadcast_to(energy, scalar_ref.shape)
 
 
+def merge_kernel(halo, lat_cells, main_ref, east_ref, west_ref, up_ref, down_ref):
+    slab = 0
+    for w, count in enumerate(trims(halo)):
+        for row in range(count):
+            up_ref[slab] = main_ref[w * lat_cells + lat_cells - count + row]
+            down_ref[slab] = main_ref[w * lat_cells + row]
+            slab += 1
+    for at in range(WIN * lat_cells, main_ref.shape[0]):
+        up_ref[slab] = main_ref[at]
+        down_ref[slab] = main_ref[at]
+        slab += 1
+    wide = main_ref.shape[2]
+    for ref in (east_ref, west_ref):
+        for part in range(ref.shape[1] // wide):
+            piece = ref[:, part * wide : (part + 1) * wide]
+            up_ref[slab] = piece
+            down_ref[slab] = piece
+            slab += 1
+
+
 def model_kernel(pack, mode, dims, edge_ref, *refs):
     layers, levels, lat_cells, lon_cells = dims
     channels = layers * levels
-    rows = lat_cells + 2 * HALO
+    halo = REACH if mode == "last" else HALO
+    rows = lat_cells + 2 * halo
     cols = lon_cells // LANES
     width = lon_cells + LANES
+    kept = trims(halo)
     refs = list(refs)
 
     def take(count):
@@ -257,8 +338,7 @@
         del refs[:count]
         return got
 
-    mains = take(3)
-    strips = [take(2), take(2), take(2)]
+    south_ref, main_ref, north_ref, east_ref, west_ref = take(5)
     into_ref, back_ref = take(2)
     if mode != "right":
         (winds,) = take(1)
@@ -278,17 +358,27 @@
 
     lane = iota((SUB, LANES), 1)
 
-    def assemble(slab, block):
-        main = mains[block]
-        east, west = strips[block]
+    slabs = main_ref.shape[0]
+    parts = east_ref.shape[1] // LANES
+    beyond = [sum(kept) + slabs - WIN * lat_cells + i * (parts // cols) for i in range(2)]
+
+    def assemble(slab, block, at):
         q, s = slab * HALO // LANES, slab * HALO % LANES
-        right = turn(east[:, q * LANES : (q + 1) * LANES], -s)
-        left = turn(west[:, q * LANES : (q + 1) * LANES], LANES - HALO - s)
+        if block == 1:
+            main = main_ref[slab]
+            east, west = (ref[:, q * LANES : (q + 1) * LANES] for ref in (east_ref, west_ref))
+        else:
+            ref = south_ref if block == 0 else north_ref
+            main = ref[at]
+            lanes = slice(q % cols * LANES, (q % cols + 1) * LANES)
+            east, west = (ref[b + q // cols, :, lanes] for b in beyond)
+        right = turn(east, -s)
+        left = turn(west, LANES - HALO - s)
         edge = jnp.where(lane < HALO, right, jnp.where(lane >= LANES - HALO, left, 0.0))
-        return jnp.concatenate([main[slab], edge], axis=1)
+        return jnp.concatenate([main, edge], axis=1)
 
     def source(e):
-        at = e - HALO
+        at = e - halo
         if at < 0:
             return 0, lat_cells + at
         if at < lat_cells:
@@ -296,20 +386,23 @@
         return 2, at - lat_cells
 
     for w in range(WIN):
-        trim = STEP_WIN * (WIN - 1 - w)
+        trim = halo - kept[w] if kept[w] else halo
         for e in range(trim, rows - trim):
             block, row = source(e)
-            forced[w, e] = assemble(w * lat_cells + row, block)
+            at = sum(kept[:w]) + (row - (lat_cells - kept[w]) if block == 0 else row)
+            forced[w, e] = assemble(w * lat_cells + row, block, at)
     if mode == "right":
         for which in range(2):
             for e in range(rows):
                 block, row = source(e)
                 for part in range(levels // SUB):
-                    slab = WIN * lat_cells + (which * lat_cells + row) * (levels // SUB) + part
-                    winds[which, e, part * SUB : (part + 1) * SUB, :] = assemble(slab, block)
+                    at = (which * lat_cells + row) * (levels // SUB) + part
+                    winds[which, e, part * SUB : (part + 1) * SUB, :] = assemble(
+                        WIN * lat_cells + at, block, sum(kept) + at
+                    )
 
     def prepare(e, carry):
-        u, v = winds[0, e], winds[1, e]
+        u, v = winds[0, e + HALO - halo], winds[1, e + HALO - halo]
         coef[0, e] = 1.0 - jnp.abs(u) - jnp.abs(v)
         coef[1, e] = jnp.maximum(u, 0.0)
         coef[2, e] = jnp.maximum(-u, 0.0)
@@ -317,7 +410,7 @@
         coef[4, e] = jnp.maximum(-v, 0.0)
         return carry
 
-    lax.fori_loop(0, rows, prepare, 0)
+    loop(0, rows, 4, prepare)
 
     into = into_ref[...]
     top, rest = halves(into)
@@ -377,7 +470,7 @@
         fields[0][e] = force(WIN - 1, e)
         return carry
 
-    lax.fori_loop(0, rows, begin, 0)
+    loop(0, rows, 8, begin)
     now = 0
     for step in range(1, REACH):
         old, new = fields[now], fields[1 - now]
@@ -388,7 +481,7 @@
             adjoint(old, e, put_in(new, e), extra)
             return carry
 
-        lax.fori_loop(step, rows - step, body, 0)
+        loop(step, rows - step, 4 if w is not None else 2, body)
         now = 1 - now
     old, new = fields[now], fields[1 - now]
 
@@ -399,7 +492,7 @@
         alpha0 = scalar0_ref[0:1, 0:1] / (scalar0_ref[2:3, 0:1] + energy0_ref[0:1, 0:1])
 
         def finish(row, carry):
-            e = row + HALO
+            e = row + halo
 
             def put(chan, value):
                 at = pl.ds(chan.start * lat_cells + row, SUB, stride=lat_cells)
@@ -415,7 +508,7 @@
             adjoint(old, e, put, force(0, e))
             return carry
 
-        lax.fori_loop(0, lat_cells, finish, 0)
+        loop(0, lat_cells, 4, finish)
         for c in range(cols):
             part = slice(c * LANES, (c + 1) * LANES)
             increment_out[:, part] = ends[c][...]
@@ -446,7 +539,7 @@
 
     zero = jnp.zeros((SUB, lon_cells), F32)
     sums = (zero,) if mode == "right" else (zero, zero)
-    sums = lax.fori_loop(REACH, rows - REACH, update, sums)
+    sums = loop(REACH, rows - REACH, 4, update, sums)
     sums = [jnp.sum(jnp.sum(s, axis=1, keepdims=True), axis=0, keepdims=True) for s in sums]
     now = 1 - now
 
@@ -464,7 +557,7 @@
                 picked[pl.ds(at, SUB), :] = typed[:, c * LANES : (c + 1) * LANES]
             return carry
 
-        lax.fori_loop(0, lat_cells, body, 0)
+        loop(0, lat_cells, 8, body)
 
     look(fields[now], 0)
     for step in range(1, REACH + 1):
@@ -474,7 +567,7 @@
             tangent(old, e, put_in(new, e))
             return carry
 
-        lax.fori_loop(REACH + step, rows - REACH - step, body, 0)
+        loop(REACH + step, rows - REACH - step, 2, body)
         now = 1 - now
         if step % STEP_WIN == 0:
             look(fields[now], step // STEP_WIN)
@@ -505,15 +598,15 @@
             pack.write(out_ref, [x[:, lanes] for x in typed], spare, c * (chunk // LANES) + t)
 
 
-def call(kernel, out_shapes, args, scalars, scratch, limit=40):
-    specs = [pl.BlockSpec(memory_space=pltpu.SMEM)] * scalars
-    specs += [pl.BlockSpec(memory_space=pltpu.VMEM)] * (len(args) - scalars)
+def call(kernel, out_shapes, args, places, scratch, limit=40):
+    specs = [pl.BlockSpec(memory_space=place) for place in places]
+    specs += [pl.BlockSpec(memory_space=pltpu.VMEM)] * (len(args) - len(places))
     return pl.pallas_call(
         kernel,
         out_shape=[jax.ShapeDtypeStruct(s, F32) for s in out_shapes],
         in_specs=specs,
         out_specs=[pl.BlockSpec(memory_space=pltpu.VMEM)] * len(out_shapes),
-        scratch_shapes=[pltpu.VMEM(s, F32) for s in scratch],
+        scratch_shapes=[pltpu.VMEM(s, F32) if isinstance(s, tuple) else s for s in scratch],
         compiler_params=pltpu.CompilerParams(vmem_limit_bytes=limit << 20),
     )(*args)
 
@@ -540,7 +633,7 @@
     pack = Packing(n_lat * n_lon, recv)
     assert types == SUB and lat_cells >= HALO and lon_cells % LANES == 0
     dims = (layers, levels, lat_cells, lon_cells)
-    rows, width = lat_cells + 2 * HALO, lon_cells + LANES
+    width = lon_cells + LANES
     chunks = (pack.devices * pack.rows, LANES)
     block_args = [block_count, block_type, block_window]
     rows_of = lambda x: x.reshape(blocks, BLOCK_ROWS)
@@ -565,29 +658,40 @@
         ]
         return lax.ppermute(x, AXES, pairs)
 
-    def collect(received, with_winds):
+    def collect(received, with_winds, halo):
         slabs = WIN * lat_cells
-        args = [received, send_cols]
+        args, places, scratch = [received, send_cols], [], []
         if with_winds:
             slabs += 2 * lat_cells * (levels // SUB)
-            args += [x.reshape(levels * lat_cells, lon_cells) for x in (zonal_wind, merid_wind)]
-        strip = (SUB, -(-slabs * HALO // LANES) * LANES)
+            winds2d = (levels * lat_cells, lon_cells)
+            args += [x.reshape(winds2d) for x in (zonal_wind, merid_wind)]
+            places = [pltpu.VMEM, pltpu.VMEM, pl.ANY, pl.ANY]
+            scratch = [(winds2d[0], LANES)] * (lon_cells // LANES)
+            scratch += [winds2d, winds2d, pltpu.SemaphoreType.DMA((2,))]
+        strip = (SUB, -(-slabs * HALO // lon_cells) * lon_cells)
         main, west, east, energy = call(
             functools.partial(collect_kernel, pack, lat_cells, with_winds),
             [(slabs, SUB, lon_cells), strip, strip, (SUB, LANES)],
             args,
-            0,
-            [(levels * lat_cells, LANES)] * (lon_cells // LANES) if with_winds else [],
+            places,
+            scratch,
+            48 if with_winds else 40,
         )
-        mains = [send(main, 1, 0), main, send(main, -1, 0)]
-        strips = []
-        for up in (1, 0, -1):
-            strips += [send(west, up, -1), send(east, up, 1)]
-        return mains + strips, energy
+        east, west = send(west, 0, -1), send(east, 0, 1)
+        count = sum(trims(halo)) + slabs - WIN * lat_cells + 2 * strip[1] // lon_cells
+        up, down = call(
+            functools.partial(merge_kernel, halo, lat_cells),
+            [(count, SUB, lon_cells)] * 2,
+            [main, east, west],
+            [],
+            [],
+        )
+        return [send(up, 1, 0), main, send(down, -1, 0), east, west], energy
 
     def model(mode, halos, extra):
         ends = (channels * lat_cells, lon_cells)
         state = (lat_cells + 2 * REACH, channels, width)
+        rows = lat_cells + 2 * (REACH if mode == "last" else HALO)
         outs = [ends, ends] if mode == "last" else [chunks, state]
         scratch = [(rows, channels, width)] * 2
         scratch += [(WIN, rows, SUB, width), (5, rows, levels, width)]
@@ -601,32 +705,34 @@
             functools.partial(model_kernel, pack, mode, dims),
             outs,
             [edges, *halos, into, back, *extra],
-            1,
+            [pltpu.SMEM],
             scratch,
         )
 
     def observe(mode, received, extra):
         outs, scratch = [chunks], [total]
-        if mode != "right":
+        args = block_args + received + [obs_slot, interp_weight, error] + extra
+        if mode == "right":
+            places, limit = [pl.ANY] * len(args), 56
+            scratch += [pltpu.SMEM(x.shape, x.dtype) for x in args[:3]]
+            scratch += [pltpu.VMEM(x.shape, x.dtype) for x in args[3:]]
+            scratch += [pltpu.SemaphoreType.DMA((len(args),))]
+        else:
+            places, limit = [pltpu.SMEM] * 3, 40
             outs += [(blocks, BLOCK_ROWS), (SUB, LANES)]
             scratch += [total]
-        return call(
-            functools.partial(observe_kernel, pack, mode),
-            outs,
-            block_args + received + [obs_slot, interp_weight, error] + extra,
-            3,
-            scratch,
-        )
+        kernel = functools.partial(observe_kernel, pack, mode)
+        return call(kernel, outs, args, places, scratch, limit)
 
     assert ITERS == 2
     (chunk,) = observe("right", [], [rows_of(innovation)])
-    halos, _ = collect(exchange(chunk), True)
+    halos, _ = collect(exchange(chunk), True, HALO)
     chunk, right, winds = model("right", halos, [send_cols])
     chunk, seen, scalar0 = observe("start", [exchange(chunk)], [])
-    halos, energy0 = collect(exchange(chunk), False)
+    halos, energy0 = collect(exchange(chunk), False, HALO)
     chunk, residual = model("next", halos, [winds, energy0, scalar0, right, send_cols])
     chunk, seen, scalar1 = observe("next", [exchange(chunk)], [seen, scalar0])
-    halos, energy1 = collect(exchange(chunk), False)
+    halos, energy1 = collect(exchange(chunk), False, REACH)
     ends = model(
         "last", halos, [winds, energy1, scalar1, residual, energy0, scalar0, right]
     )

time: 244 us -> 173 us (0.71)
  starting transfers between devices: 64.5 us -> 23.7 us
  Pallas kernels: 86.5 us -> 49.7 us
  waiting for transfers between devices: 7.86 us -> 31 us
  blocking collectives: 72.7 us -> 63.9 us
  local copies, waits for them, and re-layouts: 8.48 us -> 2.75 us
    ppermute x24 -> x12, starting transfers between devices: 64.5 us -> 23.7 us  [send(): return lax.ppermute(x, AXES, pairs)]
    pallas_call x9 -> x12, Pallas kernels: 86.5 us -> 49.7 us  [call(): pl.pallas_call(kernel, out_shape=[jax.ShapeDtypeStruct(s, F32) for s in o...]
    ppermute x24 -> x12, waiting for transfers between devices: 7.86 us -> 31 us  [send(): return lax.ppermute(x, AXES, pairs)]
    all_to_all x5, blocking collectives: 72.7 us -> 63.9 us  [exchange(): x = lax.all_to_all(x, AXES, split_axis=0, concat_axis=0, tiled=True)]
    unnamed x36 -> x22, local copies, waits for them, and re-layouts: 7.62 us -> 2.58 us
  transfers between devices with their start and end apart: 24 -> 12, of which waited for: 6 -> 11; matrix products, arithmetic and copies ran while one was open for 0% -> 0% of each run, Pallas kernels for 0% -> 0%
where the time goes in v2:
time: 173 us; the launch traced here: 172 us
  blocking collectives  63.9 us (37%)
  Pallas kernels  49.7 us (29%)
  waiting for transfers between devices  31 us (18%)
  starting transfers between devices  23.7 us (14%)
  local copies, waits for them, and re-layouts  2.75 us (2%)
    all_to_all x5, blocking collectives, exchange(): x = lax.all_to_all(x, AXES, split_axis=0, concat_axis=0, tiled=True)  63.9 us
    pallas_call x12, Pallas kernels, call(): pl.pallas_call(kernel, out_shape=[jax.ShapeDtypeStruct(s, F32) for s in o...  49.7 us
    ppermute x12, waiting for transfers between devices, send(): return lax.ppermute(x, AXES, pairs)  31 us
    ppermute x12, starting transfers between devices, send(): return lax.ppermute(x, AXES, pairs)  23.7 us
  transfers between devices with their start and end apart: 12, of which 11 were waited for; matrix products, arithmetic and copies ran while one was open for 0% of the time, Pallas kernels for 0%

profile of v2, /device:TPU:1, one launch (start us, length us, event | category | flops | bytes accessed | tf_op | source)
XLA Modules:
  0.0 172.0 jit_solution(952569812624460942)
XLA Ops:
  0.7 3.7 %shard_map.122 = f32[512,128]{1,0:T(8,128)} custom-call(s32[32]{0:T(128)} %count_ref.5, s32[32]{0:T(128)} %type_ref.5, s32[32]{0:T(128)} %window_ref.5, s32[4,4096]{1,0:T(4,128)} %refs_1_.10, f32[4,4096]{1,0:T(4,128)} %refs_2_.3, f32[32,128]{1,0:T(8,128)} %bitcast.30, f32[32,128]{1,0:T(8,128)} %bitcast.37), custom_call_target="tpu_custom_call" | custom-call | tf_op jit(solution)/shard_map/pallas_call | solution.py:604
  4.4 17.2 %all_to_all.25 = f32[32,16,128]{2,1,0:T(8,128)S(1)} all-to-all(f32[32,16,128]{2,1,0:T(8,128)} %bitcast.35), channel_id=1, replica_groups=mesh['lat'=4,'lon'=8] {'lat','lon'}, dimensions={0} | all-to-all | bytes 524288 | tf_op jit(solution)/shard_map/all_to_all | solution.py:649
  24.2 2.3 %shard_map.123 = (f32[56,8,256]{2,1,0:T(8,128)S(1)}, f32[8,512]{1,0:T(8,128)S(1)}, f32[8,512]{1,0:T(8,128)S(1)}, f32[8,128]{1,0:T(8,128)}) custom-call(f32[512,128]{1,0:T(8,128)S(1)} %bitcast.23, s32[1,2048]{1,0:T(1,128)S(1)} %copy-done.2, f32[128,256]{1,0:T(8,128)S(1)} %bitcast.33, f32[128,256]{1,0:T(8,128)S(1)} %bitcast.34), custom_call_target="tpu_custom_call" | custom-call | tf_op jit(solution)/shard_map/pallas_call | solution.py:604
  26.5 1.4 collective-permute-start
  28.0 1.1 collective-permute-done.east_ref.refs_3_
  29.1 4.0 %collective-permute-done.1.west_ref.refs_4_ = f32[8,512]{1,0:T(8,128)S(1)} collective-permute-done((f32[8,512]{1,0:T(8,128)S(1)}, f32[8,512]{1,0:T(8,128)S(1)}, u32[]{:S(2)}, u32[]{:S(2)}) %collective-permute-start.1) | collective-permute-done | bytes 16416 | tf_op jit(solution)/shard_map/ppermute | solution.py:659
  33.2 4.5 %collective-permute-start.2 = (f32[54,8,256]{2,1,0:T(8,128)S(1)}, f32[54,8,256]{2,1,0:T(8,128)S(1)}, u32[]{:S(2)}, u32[]{:S(2)}) collective-permute-start(f32[54,8,256]{2,1,0:T(8,128)S(1)} %get-tuple-element.34), channel_id=1, source_target_pairs={{0,8},{1,9},{2,10},{3,11},{4,12},{5,13},{6,14},{7,15},{8,16},{9,17... | collective-permute-start | bytes 1327112 | tf_op jit(solution)/shard_map/ppermute | solution.py:659
  37.7 1.9 %collective-permute-start.3 = (f32[54,8,256]{2,1,0:T(8,128)S(1)}, f32[54,8,256]{2,1,0:T(8,128)S(1)}, u32[]{:S(2)}, u32[]{:S(2)}) collective-permute-start(f32[54,8,256]{2,1,0:T(8,128)S(1)} %get-tuple-element.35), channel_id=1, source_target_pairs={{8,0},{9,1},{10,2},{11,3},{12,4},{13,5},{14,6},{15,7},{16,8},{17,9... | collective-permute-start | bytes 1327112 | tf_op jit(solution)/shard_map/ppermute | solution.py:659
  39.9 3.0 %collective-permute-done.2.refs_0_ = f32[54,8,256]{2,1,0:T(8,128)S(1)} collective-permute-done((f32[54,8,256]{2,1,0:T(8,128)S(1)}, f32[54,8,256]{2,1,0:T(8,128)S(1)}, u32[]{:S(2)}, u32[]{:S(2)}) %collective-permute-start.2) | collective-permute-done | bytes 442400 | tf_op jit(solution)/shard_map/ppermute | solution.py:659
  42.9 4.4 %collective-permute-done.3.refs_2_ = f32[54,8,256]{2,1,0:T(8,128)S(1)} collective-permute-done((f32[54,8,256]{2,1,0:T(8,128)S(1)}, f32[54,8,256]{2,1,0:T(8,128)S(1)}, u32[]{:S(2)}, u32[]{:S(2)}) %collective-permute-start.3) | collective-permute-done | bytes 442400 | tf_op jit(solution)/shard_map/ppermute | solution.py:659
  47.3 13.3 %shard_map.125 = (f32[512,128]{1,0:T(8,128)S(1)}, f32[16,64,384]{2,1,0:T(8,128)S(1)}, f32[2,24,16,384]{3,2,1,0:T(8,128)S(1)}) custom-call(s32[2]{0:T(128)S(1)} %add_convert_fusion.edge_ref, f32[54,8,256]{2,1,0:T(8,128)S(1)} %collective-permute-done.2.refs_0_, f32[56,8,256]{2,1,0:T(8,128)S(1)} %get-tuple-element.31.main_ref.refs_1_, ...), custom_call_target="tpu_custom_call" | custom-call | tf_op jit(solution)/shard_map/pallas_call | solution.py:604
  60.6 10.6 %all_to_all.26 = f32[32,16,128]{2,1,0:T(8,128)S(1)} all-to-all(f32[32,16,128]{2,1,0:T(8,128)S(1)} %bitcast.26), channel_id=1, replica_groups=mesh['lat'=4,'lon'=8] {'lat','lon'}, dimensions={0} | all-to-all | bytes 524288 | tf_op jit(solution)/shard_map/all_to_all | solution.py:649
  71.2 4.2 %shard_map.126 = (f32[512,128]{1,0:T(8,128)S(1)}, f32[32,128]{1,0:T(8,128)S(1)}, f32[8,128]{1,0:T(8,128)S(1)}) custom-call(s32[32]{0:T(128)S(1)} %copy-done.7, s32[32]{0:T(128)S(1)} %copy-done.8, s32[32]{0:T(128)S(1)} %copy-done.9, f32[512,128]{1,0:T(8,128)S(1)} %bitcast.21, s32[4,4096]{1,0:T(4,128)S(1)} %copy-done, f32[4,4096]{1,0:T(4,128)S(1)} %copy-done.1, ...), custom_call_target="tpu_custom_call" | custom-call | tf_op jit(solution)/shard_map/pallas_call | solution.py:604
  75.4 12.8 %all_to_all.27 = f32[32,16,128]{2,1,0:T(8,128)S(1)} all-to-all(f32[32,16,128]{2,1,0:T(8,128)S(1)} %bitcast.29), channel_id=1, replica_groups=mesh['lat'=4,'lon'=8] {'lat','lon'}, dimensions={0} | all-to-all | bytes 524288 | tf_op jit(solution)/shard_map/all_to_all | solution.py:649
  88.2 1.1 shard_map.127
  89.3 1.4 collective-permute-start.4
  90.8 1.0 collective-permute-done.4.east_ref.refs_3_
  91.9 4.0 %collective-permute-done.5.west_ref.refs_4_ = f32[8,256]{1,0:T(8,128)S(1)} collective-permute-done((f32[8,256]{1,0:T(8,128)S(1)}, f32[8,256]{1,0:T(8,128)S(1)}, u32[]{:S(2)}, u32[]{:S(2)}) %collective-permute-start.5) | collective-permute-done | bytes 8224 | tf_op jit(solution)/shard_map/ppermute | solution.py:659
  95.9 4.5 %collective-permute-start.6 = (f32[20,8,256]{2,1,0:T(8,128)S(1)}, f32[20,8,256]{2,1,0:T(8,128)S(1)}, u32[]{:S(2)}, u32[]{:S(2)}) collective-permute-start(f32[20,8,256]{2,1,0:T(8,128)S(1)} %get-tuple-element.41), channel_id=1, source_target_pairs={{0,8},{1,9},{2,10},{3,11},{4,12},{5,13},{6,14},{7,15},{8,16},{9,17... | collective-permute-start | bytes 491528 | tf_op jit(solution)/shard_map/ppermute | solution.py:659
  100.4 1.9 %collective-permute-start.7 = (f32[20,8,256]{2,1,0:T(8,128)S(1)}, f32[20,8,256]{2,1,0:T(8,128)S(1)}, u32[]{:S(2)}, u32[]{:S(2)}) collective-permute-start(f32[20,8,256]{2,1,0:T(8,128)S(1)} %get-tuple-element.42), channel_id=1, source_target_pairs={{8,0},{9,1},{10,2},{11,3},{12,4},{13,5},{14,6},{15,7},{16,8},{17,9... | collective-permute-start | bytes 491528 | tf_op jit(solution)/shard_map/ppermute | solution.py:659
  102.6 4.4 %collective-permute-done.7.refs_2_ = f32[20,8,256]{2,1,0:T(8,128)S(1)} collective-permute-done((f32[20,8,256]{2,1,0:T(8,128)S(1)}, f32[20,8,256]{2,1,0:T(8,128)S(1)}, u32[]{:S(2)}, u32[]{:S(2)}) %collective-permute-start.7) | collective-permute-done | bytes 163872 | tf_op jit(solution)/shard_map/ppermute | solution.py:659
  107.0 13.3 %shard_map.129 = (f32[512,128]{1,0:T(8,128)S(1)}, f32[16,64,384]{2,1,0:T(8,128)S(1)}) custom-call(s32[2]{0:T(128)S(1)} %add_convert_fusion.edge_ref, f32[20,8,256]{2,1,0:T(8,128)S(1)} %collective-permute-done.6.refs_0_, f32[24,8,256]{2,1,0:T(8,128)S(1)} %get-tuple-element.38.main_ref.refs_1_, f32[20,8,256]{2,1,0:T(8,128)S(1)} %collective-permute-done.7.refs_2_, ...), custom_call_target="tpu_custom_call" | custom-call | tf_op jit(solution)/shard_map/pallas_call | solution.py:604
  120.4 10.6 %all_to_all.28 = f32[32,16,128]{2,1,0:T(8,128)S(1)} all-to-all(f32[32,16,128]{2,1,0:T(8,128)S(1)} %bitcast.27), channel_id=1, replica_groups=mesh['lat'=4,'lon'=8] {'lat','lon'}, dimensions={0} | all-to-all | bytes 524288 | tf_op jit(solution)/shard_map/all_to_all | solution.py:649
  130.9 4.4 %shard_map.130 = (f32[512,128]{1,0:T(8,128)S(1)}, f32[32,128]{1,0:T(8,128)}, f32[8,128]{1,0:T(8,128)S(1)}) custom-call(s32[32]{0:T(128)S(1)} %copy-done.7, s32[32]{0:T(128)S(1)} %copy-done.8, s32[32]{0:T(128)S(1)} %copy-done.9, f32[512,128]{1,0:T(8,128)S(1)} %bitcast.22, s32[4,4096]{1,0:T(4,128)S(1)} %copy-done, f32[4,4096]{1,0:T(4,128)S(1)} %copy-done.1, ...), custom_call_target="tpu_custom_call" | custom-call | tf_op jit(solution)/shard_map/pallas_call | solution.py:604
  135.4 12.8 %all_to_all.29 = f32[32,16,128]{2,1,0:T(8,128)S(1)} all-to-all(f32[32,16,128]{2,1,0:T(8,128)S(1)} %bitcast.28), channel_id=1, replica_groups=mesh['lat'=4,'lon'=8] {'lat','lon'}, dimensions={0} | all-to-all | bytes 524288 | tf_op jit(solution)/shard_map/all_to_all | solution.py:649
  148.1 1.1 shard_map.131
  149.3 1.4 collective-permute-start.8
  151.8 4.0 %collective-permute-done.9.west_ref.refs_4_ = f32[8,256]{1,0:T(8,128)S(1)} collective-permute-done((f32[8,256]{1,0:T(8,128)S(1)}, f32[8,256]{1,0:T(8,128)S(1)}, u32[]{:S(2)}, u32[]{:S(2)}) %collective-permute-start.9) | collective-permute-done | bytes 8224 | tf_op jit(solution)/shard_map/ppermute | solution.py:659
  155.8 4.5 %collective-permute-start.10 = (f32[8,8,256]{2,1,0:T(8,128)S(1)}, f32[8,8,256]{2,1,0:T(8,128)S(1)}, u32[]{:S(2)}, u32[]{:S(2)}) collective-permute-start(f32[8,8,256]{2,1,0:T(8,128)S(1)} %get-tuple-element.53), channel_id=1, source_target_pairs={{0,8},{1,9},{2,10},{3,11},{4,12},{5,13},{6,14},{7,15},{8,16},{9,17... | collective-permute-start | bytes 196616 | tf_op jit(solution)/shard_map/ppermute | solution.py:659
  160.3 1.9 %collective-permute-start.11 = (f32[8,8,256]{2,1,0:T(8,128)S(1)}, f32[8,8,256]{2,1,0:T(8,128)S(1)}, u32[]{:S(2)}, u32[]{:S(2)}) collective-permute-start(f32[8,8,256]{2,1,0:T(8,128)S(1)} %get-tuple-element.54), channel_id=1, source_target_pairs={{8,0},{9,1},{10,2},{11,3},{12,4},{13,5},{14,6},{15,7},{16,8},{17,9... | collective-permute-start | bytes 196616 | tf_op jit(solution)/shard_map/ppermute | solution.py:659
  162.3 3.6 %collective-permute-done.11.refs_2_ = f32[8,8,256]{2,1,0:T(8,128)S(1)} collective-permute-done((f32[8,8,256]{2,1,0:T(8,128)S(1)}, f32[8,8,256]{2,1,0:T(8,128)S(1)}, u32[]{:S(2)}, u32[]{:S(2)}) %collective-permute-start.11) | collective-permute-done | bytes 65568 | tf_op jit(solution)/shard_map/ppermute | solution.py:659
  165.9 6.1 %shard_map.133 = (f32[512,256]{1,0:T(8,128)}, f32[512,256]{1,0:T(8,128)}) custom-call(s32[2]{0:T(128)S(1)} %add_convert_fusion.edge_ref, f32[8,8,256]{2,1,0:T(8,128)S(1)} %collective-permute-done.10.refs_0_, f32[24,8,256]{2,1,0:T(8,128)S(1)} %get-tuple-element.50.main_ref.refs_1_, f32[8,8,256]{2,1,0:T(8,128)S(1)} %collective-permute-done.11.refs_2_, ...), custom_call_target="tpu_custom_call" | custom-call | tf_op jit(solution)/shard_map/pallas_call | solution.py:604
  (36 shorter events, 4.7 us)
Async XLA Ops:
  0.6 46.7 %copy-start.3 = (s32[1,2048]{1,0:T(1,128)S(1)}, s32[1,2048]{1,0:T(1,128)}, u32[]{:S(2)}) copy-start(s32[1,2048]{1,0:T(1,128)} %refs_1_.11) | copy-start | bytes 24580
  0.6 39.0 %copy-start.10 = (f32[8,64]{1,0:T(8,128)S(1)}, f32[8,64]{1,0:T(8,128)}, u32[]{:S(2)}) copy-start(f32[8,64]{1,0:T(8,128)} %param.13) | copy-start | bytes 6148
  4.4 66.8 %copy-start.4 = (f32[4096]{0:T(1024)S(1)}, f32[4096]{0:T(1024)}, u32[]{:S(2)}) copy-start(f32[4096]{0:T(1024)} %param.15) | copy-start | bytes 49156
  4.4 66.8 %copy-start.7 = (s32[32]{0:T(128)S(1)}, s32[32]{0:T(128)}, u32[]{:S(2)}) copy-start(s32[32]{0:T(128)} %count_ref.5) | copy-start | bytes 388
  4.4 66.7 %copy-start.8 = (s32[32]{0:T(128)S(1)}, s32[32]{0:T(128)}, u32[]{:S(2)}) copy-start(s32[32]{0:T(128)} %type_ref.5) | copy-start | bytes 388
  4.4 66.7 %copy-start.9 = (s32[32]{0:T(128)S(1)}, s32[32]{0:T(128)}, u32[]{:S(2)}) copy-start(s32[32]{0:T(128)} %window_ref.5) | copy-start | bytes 388
  21.7 49.5 %copy-start = (s32[4,4096]{1,0:T(4,128)S(1)}, s32[4,4096]{1,0:T(4,128)}, u32[]{:S(2)}) copy-start(s32[4,4096]{1,0:T(4,128)} %refs_1_.10) | copy-start | bytes 196612
  21.7 49.5 %copy-start.1 = (f32[4,4096]{1,0:T(4,128)S(1)}, f32[4,4096]{1,0:T(4,128)}, u32[]{:S(2)}) copy-start(f32[4,4096]{1,0:T(4,128)} %refs_2_.3) | copy-start | bytes 196612
  21.7 0.7 copy-start.2
  22.4 0.9 copy-start.5
  23.3 0.9 copy-start.6
  26.5 2.6 %collective-permute-start = (f32[8,512]{1,0:T(8,128)S(1)}, f32[8,512]{1,0:T(8,128)S(1)}, u32[]{:S(2)}, u32[]{:S(2)}) collective-permute-start(f32[8,512]{1,0:T(8,128)S(1)} %get-tuple-element.32), channel_id=1, source_target_pairs={{0,7},{1,0},{2,1},{3,2},{4,3},{5,4},{6,5},{7,6},{8,15},{9,8},{10,9... | collective-permute-start | bytes 49160 | tf_op jit(solution)/shard_map/ppermute | solution.py:659
  27.9 5.3 %collective-permute-start.1 = (f32[8,512]{1,0:T(8,128)S(1)}, f32[8,512]{1,0:T(8,128)S(1)}, u32[]{:S(2)}, u32[]{:S(2)}) collective-permute-start(f32[8,512]{1,0:T(8,128)S(1)} %get-tuple-element.33), channel_id=1, source_target_pairs={{0,1},{1,2},{2,3},{3,4},{4,5},{5,6},{6,7},{7,0},{8,9},{9,10},{10,1... | collective-permute-start | bytes 49160 | tf_op jit(solution)/shard_map/ppermute | solution.py:659
  33.2 9.7 %collective-permute-start.2 = (f32[54,8,256]{2,1,0:T(8,128)S(1)}, f32[54,8,256]{2,1,0:T(8,128)S(1)}, u32[]{:S(2)}, u32[]{:S(2)}) collective-permute-start(f32[54,8,256]{2,1,0:T(8,128)S(1)} %get-tuple-element.34), channel_id=1, source_target_pairs={{0,8},{1,9},{2,10},{3,11},{4,12},{5,13},{6,14},{7,15},{8,16},{9,17... | collective-permute-start | bytes 1327112 | tf_op jit(solution)/shard_map/ppermute | solution.py:659
  37.7 9.6 %collective-permute-start.3 = (f32[54,8,256]{2,1,0:T(8,128)S(1)}, f32[54,8,256]{2,1,0:T(8,128)S(1)}, u32[]{:S(2)}, u32[]{:S(2)}) collective-permute-start(f32[54,8,256]{2,1,0:T(8,128)S(1)} %get-tuple-element.35), channel_id=1, source_target_pairs={{8,0},{9,1},{10,2},{11,3},{12,4},{13,5},{14,6},{15,7},{16,8},{17,9... | collective-permute-start | bytes 1327112 | tf_op jit(solution)/shard_map/ppermute | solution.py:659
  89.3 2.6 %collective-permute-start.4 = (f32[8,256]{1,0:T(8,128)S(1)}, f32[8,256]{1,0:T(8,128)S(1)}, u32[]{:S(2)}, u32[]{:S(2)}) collective-permute-start(f32[8,256]{1,0:T(8,128)S(1)} %get-tuple-element.39), channel_id=1, source_target_pairs={{0,7},{1,0},{2,1},{3,2},{4,3},{5,4},{6,5},{7,6},{8,15},{9,8},{10,9... | collective-permute-start | bytes 24584 | tf_op jit(solution)/shard_map/ppermute | solution.py:659
  90.7 5.2 %collective-permute-start.5 = (f32[8,256]{1,0:T(8,128)S(1)}, f32[8,256]{1,0:T(8,128)S(1)}, u32[]{:S(2)}, u32[]{:S(2)}) collective-permute-start(f32[8,256]{1,0:T(8,128)S(1)} %get-tuple-element.40), channel_id=1, source_target_pairs={{0,1},{1,2},{2,3},{3,4},{4,5},{5,6},{6,7},{7,0},{8,9},{9,10},{10,1... | collective-permute-start | bytes 24584 | tf_op jit(solution)/shard_map/ppermute | solution.py:659
  95.9 6.7 %collective-permute-start.6 = (f32[20,8,256]{2,1,0:T(8,128)S(1)}, f32[20,8,256]{2,1,0:T(8,128)S(1)}, u32[]{:S(2)}, u32[]{:S(2)}) collective-permute-start(f32[20,8,256]{2,1,0:T(8,128)S(1)} %get-tuple-element.41), channel_id=1, source_target_pairs={{0,8},{1,9},{2,10},{3,11},{4,12},{5,13},{6,14},{7,15},{8,16},{9,17... | collective-permute-start | bytes 491528 | tf_op jit(solution)/shard_map/ppermute | solution.py:659
  100.4 6.6 %collective-permute-start.7 = (f32[20,8,256]{2,1,0:T(8,128)S(1)}, f32[20,8,256]{2,1,0:T(8,128)S(1)}, u32[]{:S(2)}, u32[]{:S(2)}) collective-permute-start(f32[20,8,256]{2,1,0:T(8,128)S(1)} %get-tuple-element.42), channel_id=1, source_target_pairs={{8,0},{9,1},{10,2},{11,3},{12,4},{13,5},{14,6},{15,7},{16,8},{17,9... | collective-permute-start | bytes 491528 | tf_op jit(solution)/shard_map/ppermute | solution.py:659
  149.3 2.6 %collective-permute-start.8 = (f32[8,256]{1,0:T(8,128)S(1)}, f32[8,256]{1,0:T(8,128)S(1)}, u32[]{:S(2)}, u32[]{:S(2)}) collective-permute-start(f32[8,256]{1,0:T(8,128)S(1)} %get-tuple-element.51), channel_id=1, source_target_pairs={{0,7},{1,0},{2,1},{3,2},{4,3},{5,4},{6,5},{7,6},{8,15},{9,8},{10,9... | collective-permute-start | bytes 24584 | tf_op jit(solution)/shard_map/ppermute | solution.py:659
  150.6 5.2 %collective-permute-start.9 = (f32[8,256]{1,0:T(8,128)S(1)}, f32[8,256]{1,0:T(8,128)S(1)}, u32[]{:S(2)}, u32[]{:S(2)}) collective-permute-start(f32[8,256]{1,0:T(8,128)S(1)} %get-tuple-element.52), channel_id=1, source_target_pairs={{0,1},{1,2},{2,3},{3,4},{4,5},{5,6},{6,7},{7,0},{8,9},{9,10},{10,1... | collective-permute-start | bytes 24584 | tf_op jit(solution)/shard_map/ppermute | solution.py:659
  155.8 6.4 %collective-permute-start.10 = (f32[8,8,256]{2,1,0:T(8,128)S(1)}, f32[8,8,256]{2,1,0:T(8,128)S(1)}, u32[]{:S(2)}, u32[]{:S(2)}) collective-permute-start(f32[8,8,256]{2,1,0:T(8,128)S(1)} %get-tuple-element.53), channel_id=1, source_target_pairs={{0,8},{1,9},{2,10},{3,11},{4,12},{5,13},{6,14},{7,15},{8,16},{9,17... | collective-permute-start | bytes 196616 | tf_op jit(solution)/shard_map/ppermute | solution.py:659
  160.3 5.6 %collective-permute-start.11 = (f32[8,8,256]{2,1,0:T(8,128)S(1)}, f32[8,8,256]{2,1,0:T(8,128)S(1)}, u32[]{:S(2)}, u32[]{:S(2)}) collective-permute-start(f32[8,8,256]{2,1,0:T(8,128)S(1)} %get-tuple-element.54), channel_id=1, source_target_pairs={{8,0},{9,1},{10,2},{11,3},{12,4},{13,5},{14,6},{15,7},{16,8},{17,9... | collective-permute-start | bytes 196616 | tf_op jit(solution)/shard_map/ppermute | solution.py:659

commit v3 on v2

--- a/solution.py
+++ b/solution.py
@@ -63,46 +63,76 @@
         self.slots = recv // devices
         assert self.slots <= LANES and recv % LANES == 0
         self.per = LANES // self.slots
-        self.tiles = WIN // self.per + 1
-        self.rows = self.tiles * SUB
-        self.spare_tile, self.spare_group = WIN // self.per, WIN % self.per
+        self.full = WIN // self.per
+        self.left = WIN - self.full * self.per
+        self.short = -(-self.left * SUB // self.per)
+        self.spare = self.full * SUB + self.short
+        self.rows = self.spare + 1
         self.group_bits = log2(self.slots)
 
     def group(self, shape):
         return iota(shape, len(shape) - 1) >> self.group_bits
 
-    def spare(self, row):
-        lane = iota(row.shape, 1)
-        first = lane == self.spare_group * self.slots
-        return jnp.sum(jnp.where(first, row, 0.0), axis=1, keepdims=True)
+    def place(self, window, kind):
+        row = (window >> log2(self.per)) * SUB + kind
+        group = window & (self.per - 1)
+        if self.left:
+            at = (window - self.full * self.per) * SUB + kind
+            late = window >= self.full * self.per
+            row = jnp.where(late, self.full * SUB + lax.rem(at, self.short), row)
+            group = jnp.where(late, lax.div(at, self.short), group)
+        return row, group * self.slots
+
+    def sums(self, row):
+        total = jnp.sum(row, axis=0, keepdims=True)
+        lane = iota(total.shape, 1)
+        return [
+            jnp.sum(jnp.where(lane == at, total, 0.0), axis=1, keepdims=True)
+            for at in (0, LANES // 2)
+        ]
 
     def write(self, out_ref, typed, spare, tile):
-        group = self.group((SUB, LANES))
+        late = typed[self.full * self.per :]
+        late = late[0] if len(late) == 1 else jnp.concatenate(late, axis=0)
         for d in range(self.per):
-            device = tile * self.per + d
-            for part in range(self.tiles):
-                chunk = jnp.zeros((SUB, LANES), F32)
+            base = (tile * self.per + d) * self.rows
+            for part in range(self.full):
+                chunk = None
+                for g in range(self.per):
+                    piece = turn(typed[part * self.per + g], (g - d) * self.slots)
+                    chunk = piece if g == 0 else self.select(g, piece, chunk)
+                out_ref[base + part * SUB : base + (part + 1) * SUB, :] = chunk
+            chunk = jnp.zeros((self.short, LANES), F32)
+            for g in range(self.per):
+                piece = turn(late, (g - d) * self.slots)
+                piece = piece[g * self.short : (g + 1) * self.short]
+                chunk = piece if g == 0 else self.select(g, piece, chunk)
+            base += self.full * SUB
+            out_ref[base : base + self.short, :] = chunk
+            out_ref[base + self.short : base + self.short + 1, :] = spare
+
+    def select(self, group, yes, no):
+        return jnp.where(self.group(yes.shape) == group, yes, no)
+
+    def read(self, ref, tile):
+        typed = [None] * WIN
+        for d in range(self.per):
+            base = (tile * self.per + d) * self.rows
+            for part in range(self.full):
+                piece = ref[base + part * SUB : base + (part + 1) * SUB, :]
                 for g in range(self.per):
                     w = part * self.per + g
-                    if w < WIN:
-                        piece = turn(typed[w], (g - d) * self.slots)
-                    elif w == WIN:
-                        piece = spare
-                    else:
-                        continue
-                    chunk = jnp.where(group == g, piece, chunk)
-                at = (device * self.tiles + part) * SUB
-                out_ref[at : at + SUB, :] = chunk
-
-    def read(self, ref, w, tile):
-        group = self.group((SUB, LANES))
-        part, g = w // self.per, w % self.per
-        found = jnp.zeros((SUB, LANES), F32)
-        for d in range(self.per):
-            at = ((tile * self.per + d) * self.tiles + part) * SUB
-            piece = turn(ref[at : at + SUB, :], (d - g) * self.slots)
-            found = jnp.where(group == d, piece, found)
-        return found
+                    found = turn(piece, (d - g) * self.slots)
+                    typed[w] = found if d == 0 else self.select(d, found, typed[w])
+            base += self.full * SUB
+            piece = ref[base : base + self.short, :]
+            late = [turn(piece, (d - g) * self.slots) for g in range(self.per)]
+            late = jnp.concatenate(late, axis=0)
+            for i in range(self.left):
+                w = self.full * self.per + i
+                found = late[i * SUB : (i + 1) * SUB]
+                typed[w] = found if d == 0 else self.select(d, found, typed[w])
+        return typed
 
 
 def turn(x, shift):
@@ -110,11 +140,43 @@
     return pltpu.roll(x, shift, len(x.shape) - 1) if shift else x
 
 
-def observe_kernel(pack, mode, count_ref, type_ref, window_ref, *refs):
+def note(strips, slab, left, right):
+    q, s = slab * HALO // LANES, slab * HALO % LANES
+    lane = iota((SUB, LANES), 1)
+    inside = (lane >= s) & (lane < s + HALO)
+    west, east = strips.get(q, (jnp.zeros((SUB, LANES), F32),) * 2)
+    west = jnp.where(inside, turn(left, s), west)
+    east = jnp.where(inside, turn(right, s - (LANES - HALO)), east)
+    strips[q] = (west, east)
+
+
+def lay_winds(first, refs, held, out_ref):
+    cols, lat_cells = len(held), first // WIN
+    slab, strips = 0, {}
+    for ref in refs:
+        for c in range(cols):
+            held[c][...] = ref[:, c * LANES : (c + 1) * LANES]
+        for row in range(lat_cells):
+            for part in range(ref.shape[0] // lat_cells // SUB):
+                at = pl.ds(part * SUB * lat_cells + row, SUB, stride=lat_cells)
+                pieces = [held[c][at, :] for c in range(cols)]
+                for c in range(cols):
+                    out_ref[slab, :, c * LANES : (c + 1) * LANES] = pieces[c]
+                note(strips, first + slab, pieces[0], pieces[-1])
+                slab += 1
+    count = (out_ref.shape[0] - 1 - slab) // 2
+    for q in range(count * cols):
+        for side in range(2):
+            piece = strips[q][side] if q in strips else jnp.zeros((SUB, LANES), F32)
+            lanes = slice(q % cols * LANES, (q % cols + 1) * LANES)
+            out_ref[slab + side * count + q // cols, :, lanes] = piece
+
+
+def observe_kernel(pack, mode, lat_cells, count_ref, type_ref, window_ref, *refs):
     if mode == "right":
-        far = (count_ref, type_ref, window_ref) + refs[:4]
-        out_ref, total = refs[4:6]
-        near, done = refs[6:-1], refs[-1]
+        far = (count_ref, type_ref, window_ref) + refs[:7]
+        out_ref, winds_ref, total = refs[7:10]
+        near, held, done = refs[10:20], refs[20:-1], refs[-1]
         copies = [
             pltpu.make_async_copy(src, dst, done.at[i])
             for i, (src, dst) in enumerate(zip(far, near))
@@ -122,9 +184,9 @@
         for copy in copies:
             copy.start()
         total[...] = jnp.zeros_like(total)
-        for copy in copies:
+        for copy in copies[:7]:
             copy.wait()
-        count_ref, type_ref, window_ref, slot_ref, weight_ref, error_ref, value_ref = near
+        count_ref, type_ref, window_ref, slot_ref, weight_ref, error_ref, value_ref = near[:7]
     else:
         if mode == "start":
             recv_ref, slot_ref, weight_ref, error_ref = refs[:4]
@@ -137,16 +199,14 @@
     blocks = error_ref.shape[0]
     devices = pack.devices
     wide = points * BLOCK_ROWS
-    spare = pack.spare_tile * SUB
     if mode != "right":
         total[...] = jnp.zeros_like(total)
         for j in range(pack.rows):
             table[j] = recv_ref[pl.ds(j, devices, stride=pack.rows), :]
-        norm = pack.spare(jnp.sum(table[spare], axis=0, keepdims=True))
+        norm, cross = pack.sums(table[pack.spare])
         if mode == "start":
             ratio, square = jnp.zeros_like(norm), norm
         else:
-            cross = pack.spare(jnp.sum(table[spare + 1], axis=0, keepdims=True))
             ratio = norm / before_ref[0:1, 0:1]
             square = norm + 2.0 * ratio * cross + ratio * ratio * before_ref[2:3, 0:1]
         row = iota((SUB, LANES), 0)
@@ -161,9 +221,8 @@
         group = [first * together + i for i in range(together)]
         places, picks, owners, weights, values = [], [], [], [], []
         for b in group:
-            window = window_ref[b]
-            places.append((window >> log2(pack.per)) * SUB + type_ref[b])
-            shift = (window & (pack.per - 1)) * pack.slots
+            place, shift = pack.place(window_ref[b], type_ref[b])
+            places.append(place)
             lanes = pl.ds(pl.multiple_of(b * BLOCK_ROWS, BLOCK_ROWS), BLOCK_ROWS)
             slot = slot_ref[:, lanes]
             lane = (slot & (pack.slots - 1)) + shift
@@ -220,47 +279,45 @@
     energy = jnp.sum(energy, axis=1, keepdims=True)
     for j in range(pack.rows):
         chunk = total[j]
-        if j == spare:
-            chunk = jnp.where(pack.group((devices, LANES)) == pack.spare_group, energy, chunk)
+        if j == pack.spare:
+            chunk = jnp.broadcast_to(energy, (devices, LANES))
         out_ref[pl.ds(j, devices, stride=pack.rows), :] = chunk
-
-
-def collect_kernel(pack, lat_cells, with_winds, *refs):
-    if with_winds:
-        recv_ref, send_ref, zonal_ref, merid_ref = refs[:4]
-        refs = refs[4:]
-    else:
-        recv_ref, send_ref = refs[:2]
-        refs = refs[2:]
-    main_ref, west_ref, east_ref, scalar_ref = refs[:4]
-    if with_winds:
-        held, near, done = refs[4:-3], refs[-3:-1], refs[-1]
-        copies = [
-            pltpu.make_async_copy(src, dst, done.at[i])
-            for i, (src, dst) in enumerate(zip((zonal_ref, merid_ref), near))
-        ]
-        for copy in copies:
-            copy.start()
+    if mode == "right":
+        for copy in copies[7:]:
+            copy.wait()
+        lay_winds(WIN * lat_cells, near[7:9], held, winds_ref)
+        wide = winds_ref.shape[2]
+        send = near[9][...].astype(F32)
+        rows = [send[:, i * wide : (i + 1) * wide] for i in range(pack.recv // wide)]
+        rows += [jnp.zeros((1, wide), F32)] * (SUB - len(rows))
+        winds_ref[winds_ref.shape[0] - 1] = jnp.concatenate(rows, axis=0)
+
+
+def collect_kernel(pack, lat_cells, with_winds, recv_ref, send_ref, *refs):
+    main_ref, west_ref, east_ref, scalar_ref = refs
     lon_cells = main_ref.shape[2]
     cols = lon_cells // LANES
     tiles = pack.recv // LANES
-    send = send_ref[...]
+    strips = {}
+    if with_winds:
+        send = send_ref[send_ref.shape[0] - 1]
+        send = [send[i : i + 1] for i in range(pack.recv // lon_cells)]
+        send = jnp.concatenate(send, axis=1).astype(jnp.int32)
+        count = main_ref.shape[0] - WIN * lat_cells
+        main_ref[WIN * lat_cells :] = send_ref[:count]
+        half = west_ref.shape[1] // lon_cells
+        for q in range(half * cols):
+            lanes = slice(q % cols * LANES, (q % cols + 1) * LANES)
+            at = count + q // cols
+            strips[q] = (send_ref[at, :, lanes], send_ref[at + half, :, lanes])
+    else:
+        send = send_ref[...]
     pick = jnp.where(iota((LANES, pack.recv), 0) == (send & (LANES - 1)), 1.0, 0.0).astype(BF16)
     high = send >> log2(LANES)
-    strips = {}
-
-    def note(slab, left, right):
-        at = slab * HALO
-        q, s = at // LANES, at % LANES
-        lane = iota((SUB, LANES), 1)
-        inside = (lane >= s) & (lane < s + HALO)
-        west, east = strips.get(q, (jnp.zeros((SUB, LANES), F32),) * 2)
-        west = jnp.where(inside, turn(left, s), west)
-        east = jnp.where(inside, turn(right, s - (LANES - HALO)), east)
-        strips[q] = (west, east)
-
+
+    every = [pack.read(recv_ref, t) for t in range(tiles)]
     for w in range(WIN):
-        typed = jnp.concatenate([pack.read(recv_ref, w, t) for t in range(tiles)], axis=1)
+        typed = jnp.concatenate([x[w] for x in every], axis=1)
         masked = []
         for part in halves(typed):
             masked += [
@@ -278,28 +335,12 @@
             ]
             for c in range(cols):
                 main_ref[slab, :, c * LANES : (c + 1) * LANES] = pieces[c]
-            note(slab, pieces[0], pieces[-1])
-    if with_winds:
-        slab = WIN * lat_cells
-        levels = zonal_ref.shape[0] // lat_cells
-        for which in range(2):
-            copies[which].wait()
-            for c in range(cols):
-                held[c][...] = near[which][:, c * LANES : (c + 1) * LANES]
-            for row in range(lat_cells):
-                for part in range(levels // SUB):
-                    at = pl.ds(part * SUB * lat_cells + row, SUB, stride=lat_cells)
-                    pieces = [held[c][at, :] for c in range(cols)]
-                    for c in range(cols):
-                        main_ref[slab, :, c * LANES : (c + 1) * LANES] = pieces[c]
-                    note(slab, pieces[0], pieces[-1])
-                    slab += 1
+            note(strips, slab, pieces[0], pieces[-1])
     for q in range(west_ref.shape[1] // LANES):
         west, east = strips[q]
         west_ref[:, q * LANES : (q + 1) * LANES] = west
         east_ref[:, q * LANES : (q + 1) * LANES] = east
-    row = recv_ref[pl.ds(pack.spare_tile * SUB, pack.devices, stride=pack.rows), :]
-    energy = pack.spare(jnp.sum(row, axis=0, keepdims=True))
+    energy, _ = pack.sums(recv_ref[pl.ds(pack.spare, pack.devices, stride=pack.rows), :])
     scalar_ref[...] = jnp.broadcast_to(energy, scalar_ref.shape)
 
 
@@ -397,9 +438,10 @@
                 block, row = source(e)
                 for part in range(levels // SUB):
                     at = (which * lat_cells + row) * (levels // SUB) + part
-                    winds[which, e, part * SUB : (part + 1) * SUB, :] = assemble(
-                        WIN * lat_cells + at, block, sum(kept) + at
-                    )
+                    wind = assemble(WIN * lat_cells + at, block, sum(kept) + at)
+                    if block != 1:
+                        wind = jnp.where(edge_ref[block // 2] > 0, wind, 0.0)
+                    winds[which, e, part * SUB : (part + 1) * SUB, :] = wind
 
     def prepare(e, carry):
         u, v = winds[0, e + HALO - halo], winds[1, e + HALO - halo]
@@ -491,8 +533,8 @@
     if mode == "last":
         alpha0 = scalar0_ref[0:1, 0:1] / (scalar0_ref[2:3, 0:1] + energy0_ref[0:1, 0:1])
 
-        def finish(row, carry):
-            e = row + halo
+        def finish(e, carry):
+            row = e - halo
 
             def put(chan, value):
                 at = pl.ds(chan.start * lat_cells + row, SUB, stride=lat_cells)
@@ -508,7 +550,7 @@
             adjoint(old, e, put, force(0, e))
             return carry
 
-        loop(0, lat_cells, 4, finish)
+        loop(halo, halo + lat_cells, 4, finish)
         for c in range(cols):
             part = slice(c * LANES, (c + 1) * LANES)
             increment_out[:, part] = ends[c][...]
@@ -572,10 +614,7 @@
         if step % STEP_WIN == 0:
             look(fields[now], step // STEP_WIN)
 
-    row = iota((SUB, LANES), 0)
-    spare = jnp.where(row == 0, sums[0], 0.0)
-    if mode != "right":
-        spare = jnp.where(row == 1, sums[1], spare)
+    spare = jnp.where(iota((1, LANES), 1) < LANES // 2, sums[0], sums[-1])
     top, rest = halves(picked[...])
     values = jnp.concatenate([top, rest], axis=1).astype(BF16)
     chunk = 2 * LANES
@@ -598,12 +637,14 @@
             pack.write(out_ref, [x[:, lanes] for x in typed], spare, c * (chunk // LANES) + t)
 
 
-def call(kernel, out_shapes, args, places, scratch, limit=40):
+def call(kernel, out_shapes, args, places, scratch, limit=24):
     specs = [pl.BlockSpec(memory_space=place) for place in places]
     specs += [pl.BlockSpec(memory_space=pltpu.VMEM)] * (len(args) - len(places))
     return pl.pallas_call(
         kernel,
-        out_shape=[jax.ShapeDtypeStruct(s, F32) for s in out_shapes],
+        out_shape=[
+            jax.ShapeDtypeStruct(s, F32) if isinstance(s, tuple) else s for s in out_shapes
+        ],
         in_specs=specs,
         out_specs=[pl.BlockSpec(memory_space=pltpu.VMEM)] * len(out_shapes),
         scratch_shapes=[pltpu.VMEM(s, F32) if isinstance(s, tuple) else s for s in scratch],
@@ -632,6 +673,7 @@
     blocks = block_count.shape[0]
     pack = Packing(n_lat * n_lon, recv)
     assert types == SUB and lat_cells >= HALO and lon_cells % LANES == 0
+    assert recv % lon_cells == 0 and recv // lon_cells <= SUB
     dims = (layers, levels, lat_cells, lon_cells)
     width = lon_cells + LANES
     chunks = (pack.devices * pack.rows, LANES)
@@ -645,37 +687,30 @@
     back = jnp.tile(operator_rows, (2, 2))
 
     def exchange(x):
-        x = x.reshape(pack.devices, pack.rows, LANES)
+        x = x.reshape(pack.devices * pack.rows, 1, LANES)
         x = lax.all_to_all(x, AXES, split_axis=0, concat_axis=0, tiled=True)
         return x.reshape(chunks)
 
     def send(x, up, right):
         pairs = [
-            (i * n_lon + j, (i + up) * n_lon + (j + right) % n_lon)
+            (i * n_lon + j, (i + up) % n_lat * n_lon + (j + right) % n_lon)
             for i in range(n_lat)
             for j in range(n_lon)
-            if 0 <= i + up < n_lat
         ]
         return lax.ppermute(x, AXES, pairs)
 
-    def collect(received, with_winds, halo):
-        slabs = WIN * lat_cells
-        args, places, scratch = [received, send_cols], [], []
-        if with_winds:
-            slabs += 2 * lat_cells * (levels // SUB)
-            winds2d = (levels * lat_cells, lon_cells)
-            args += [x.reshape(winds2d) for x in (zonal_wind, merid_wind)]
-            places = [pltpu.VMEM, pltpu.VMEM, pl.ANY, pl.ANY]
-            scratch = [(winds2d[0], LANES)] * (lon_cells // LANES)
-            scratch += [winds2d, winds2d, pltpu.SemaphoreType.DMA((2,))]
+    wind_slabs = 2 * lat_cells * (levels // SUB)
+
+    def collect(received, halo, cells, with_winds=False):
+        slabs = WIN * lat_cells + with_winds * wind_slabs
         strip = (SUB, -(-slabs * HALO // lon_cells) * lon_cells)
         main, west, east, energy = call(
             functools.partial(collect_kernel, pack, lat_cells, with_winds),
             [(slabs, SUB, lon_cells), strip, strip, (SUB, LANES)],
-            args,
-            places,
-            scratch,
-            48 if with_winds else 40,
+            [received, cells],
+            [],
+            [],
+            16,
         )
         east, west = send(west, 0, -1), send(east, 0, 1)
         count = sum(trims(halo)) + slabs - WIN * lat_cells + 2 * strip[1] // lon_cells
@@ -714,25 +749,29 @@
         args = block_args + received + [obs_slot, interp_weight, error] + extra
         if mode == "right":
             places, limit = [pl.ANY] * len(args), 56
+            strip = -(-(WIN * lat_cells + wind_slabs) * HALO // lon_cells)
+            outs += [(wind_slabs + 2 * strip + 1, SUB, lon_cells)]
             scratch += [pltpu.SMEM(x.shape, x.dtype) for x in args[:3]]
             scratch += [pltpu.VMEM(x.shape, x.dtype) for x in args[3:]]
+            scratch += [(levels * lat_cells, LANES)] * (lon_cells // LANES)
             scratch += [pltpu.SemaphoreType.DMA((len(args),))]
         else:
-            places, limit = [pltpu.SMEM] * 3, 40
+            places, limit = [pltpu.SMEM] * 3, 12
             outs += [(blocks, BLOCK_ROWS), (SUB, LANES)]
             scratch += [total]
-        kernel = functools.partial(observe_kernel, pack, mode)
+        kernel = functools.partial(observe_kernel, pack, mode, lat_cells)
         return call(kernel, outs, args, places, scratch, limit)
 
     assert ITERS == 2
-    (chunk,) = observe("right", [], [rows_of(innovation)])
-    halos, _ = collect(exchange(chunk), True, HALO)
+    winds = [x.reshape(levels * lat_cells, lon_cells) for x in (zonal_wind, merid_wind)]
+    chunk, winds = observe("right", [], [rows_of(innovation), *winds, send_cols])
+    halos, _ = collect(exchange(chunk), HALO, winds, True)
     chunk, right, winds = model("right", halos, [send_cols])
     chunk, seen, scalar0 = observe("start", [exchange(chunk)], [])
-    halos, energy0 = collect(exchange(chunk), False, HALO)
+    halos, energy0 = collect(exchange(chunk), HALO, send_cols)
     chunk, residual = model("next", halos, [winds, energy0, scalar0, right, send_cols])
     chunk, seen, scalar1 = observe("next", [exchange(chunk)], [seen, scalar0])
-    halos, energy1 = collect(exchange(chunk), False, REACH)
+    halos, energy1 = collect(exchange(chunk), REACH, send_cols)
     ends = model(
         "last", halos, [winds, energy1, scalar1, residual, energy0, scalar0, right]
     )

time: 173 us -> 160 us (0.925)
  starting transfers between devices: 23.7 us -> 12.8 us
  waiting for transfers between devices: 31 us -> 36.5 us
  blocking collectives: 63.9 us -> 59.4 us
    ppermute x12, starting transfers between devices: 23.7 us -> 12.8 us  [send(): return lax.ppermute(x, AXES, pairs)]
    ppermute x12, waiting for transfers between devices: 31 us -> 36.5 us  [send(): return lax.ppermute(x, AXES, pairs)]
    all_to_all x5, blocking collectives: 63.9 us -> 59.4 us  [exchange(): x = lax.all_to_all(x, AXES, split_axis=0, concat_axis=0, tiled=True)]
  transfers between devices with their start and end apart: 12 -> 12, of which waited for: 11 -> 12; matrix products, arithmetic and copies ran while one was open for 0% -> 0% of each run, Pallas kernels for 0% -> 0%
where the time goes in v3:
time: 160 us
  blocking collectives  59.4 us (37%)
  Pallas kernels  49.2 us (31%)
  waiting for transfers between devices  36.5 us (23%)
  starting transfers between devices  12.8 us (8%)
    all_to_all x5, blocking collectives, exchange(): x = lax.all_to_all(x, AXES, split_axis=0, concat_axis=0, tiled=True)  59.4 us
    pallas_call x12, Pallas kernels, call(): pl.pallas_call(kernel, out_shape=[jax.ShapeDtypeStruct(s, F32) if isinsta...  49.2 us
    ppermute x12, waiting for transfers between devices, send(): return lax.ppermute(x, AXES, pairs)  36.5 us
    ppermute x12, starting transfers between devices, send(): return lax.ppermute(x, AXES, pairs)  12.8 us
  transfers between devices with their start and end apart: 12, of which 12 were waited for; matrix products, arithmetic and copies ran while one was open for 0% of the time, Pallas kernels for 0%

profile of v3, /device:TPU:1, one launch (start us, length us, event | category | flops | bytes accessed | tf_op | source)
XLA Modules:
  0.0 160.0 jit_solution(16203483471358552667)
XLA Ops:
  0.7 3.9 %shard_map.122 = (f32[416,128]{1,0:T(8,128)}, f32[37,8,256]{2,1,0:T(8,128)}) custom-call(s32[32]{0:T(128)} %count_ref.5, s32[32]{0:T(128)} %type_ref.5, s32[32]{0:T(128)} %window_ref.5, s32[4,4096]{1,0:T(4,128)} %refs_1_.5, f32[4,4096]{1,0:T(4,128)} %refs_2_.3, f32[32,128]{1,0:T(8,128)} %bitcast.40, f32[32,128]{1,0:T(8,128)} %bitcast.47, ...), custom_call_target="tpu_custom_call" | custom-call | tf_op jit(solution)/shard_map/pallas_call | solution.py:643
  4.6 15.9 %all_to_all.25 = f32[416,1,128]{2,1,0:T(1,128)S(1)} all-to-all(f32[416,1,128]{2,1,0:T(1,128)} %bitcast.43), channel_id=1, replica_groups=mesh['lat'=4,'lon'=8] {'lat','lon'}, dimensions={0} | all-to-all | bytes 425984 | tf_op jit(solution)/shard_map/all_to_all | solution.py:691
  20.5 1.0 copy-done.2
  21.5 1.7 %shard_map.123 = (f32[56,8,256]{2,1,0:T(8,128)S(1)}, f32[8,512]{1,0:T(8,128)S(1)}, f32[8,512]{1,0:T(8,128)S(1)}, f32[8,128]{1,0:T(8,128)}) custom-call(f32[416,128]{1,0:T(8,128)S(1)} %bitcast.34, f32[37,8,256]{2,1,0:T(8,128)S(1)} %copy-done.2), custom_call_target="tpu_custom_call" | custom-call | tf_op jit(solution)/shard_map/pallas_call | solution.py:643
  23.2 1.9 %collective-permute-start = (f32[8,512]{1,0:T(8,128)S(1)}, f32[8,512]{1,0:T(8,128)S(1)}, u32[]{:S(2)}, u32[]{:S(2)}) collective-permute-start(f32[8,512]{1,0:T(8,128)S(1)} %get-tuple-element.36), channel_id=1, source_target_pairs={{0,7},{1,0},{2,1},{3,2},{4,3},{5,4},{6,5},{7,6},{8,15},{9,8},{10,9... | collective-permute-start | bytes 49160 | tf_op jit(solution)/shard_map/ppermute | solution.py:700
  25.1 0.9 collective-permute-done.east_ref.refs_3_
  26.0 4.4 %collective-permute-done.1.west_ref.refs_4_ = f32[8,512]{1,0:T(8,128)S(1)} collective-permute-done((f32[8,512]{1,0:T(8,128)S(1)}, f32[8,512]{1,0:T(8,128)S(1)}, u32[]{:S(2)}, u32[]{:S(2)}) %collective-permute-start.1) | collective-permute-done | bytes 16416 | tf_op jit(solution)/shard_map/ppermute | solution.py:700
  30.5 2.3 %collective-permute-start.2 = (f32[54,8,256]{2,1,0:T(8,128)S(1)}, f32[54,8,256]{2,1,0:T(8,128)S(1)}, u32[]{:S(2)}, u32[]{:S(2)}) collective-permute-start(f32[54,8,256]{2,1,0:T(8,128)S(1)} %get-tuple-element.38), channel_id=1, source_target_pairs={{0,8},{1,9},{2,10},{3,11},{4,12},{5,13},{6,14},{7,15},{8,16},{9,17... | collective-permute-start | bytes 1327112 | tf_op jit(solution)/shard_map/ppermute | solution.py:700
  33.0 7.9 %collective-permute-done.2.refs_0_ = f32[54,8,256]{2,1,0:T(8,128)S(1)} collective-permute-done((f32[54,8,256]{2,1,0:T(8,128)S(1)}, f32[54,8,256]{2,1,0:T(8,128)S(1)}, u32[]{:S(2)}, u32[]{:S(2)}) %collective-permute-start.2) | collective-permute-done | bytes 442400 | tf_op jit(solution)/shard_map/ppermute | solution.py:700
  40.9 3.6 %collective-permute-done.3.refs_2_ = f32[54,8,256]{2,1,0:T(8,128)S(1)} collective-permute-done((f32[54,8,256]{2,1,0:T(8,128)S(1)}, f32[54,8,256]{2,1,0:T(8,128)S(1)}, u32[]{:S(2)}, u32[]{:S(2)}) %collective-permute-start.3) | collective-permute-done | bytes 442400 | tf_op jit(solution)/shard_map/ppermute | solution.py:700
  44.5 13.2 %shard_map.125 = (f32[416,128]{1,0:T(8,128)S(1)}, f32[16,64,384]{2,1,0:T(8,128)S(1)}, f32[2,24,16,384]{3,2,1,0:T(8,128)S(1)}) custom-call(s32[2]{0:T(128)S(1)} %add_convert_fusion.edge_ref, f32[54,8,256]{2,1,0:T(8,128)S(1)} %collective-permute-done.2.refs_0_, f32[56,8,256]{2,1,0:T(8,128)S(1)} %get-tuple-element.35.main_ref.refs_1_, ...), custom_call_target="tpu_custom_call" | custom-call | tf_op jit(solution)/shard_map/pallas_call | solution.py:643
  57.7 10.1 %all_to_all.26 = f32[416,1,128]{2,1,0:T(1,128)S(1)} all-to-all(f32[416,1,128]{2,1,0:T(1,128)S(1)} %bitcast.36), channel_id=1, replica_groups=mesh['lat'=4,'lon'=8] {'lat','lon'}, dimensions={0} | all-to-all | bytes 425984 | tf_op jit(solution)/shard_map/all_to_all | solution.py:691
  67.9 4.0 %shard_map.126 = (f32[416,128]{1,0:T(8,128)S(1)}, f32[32,128]{1,0:T(8,128)S(1)}, f32[8,128]{1,0:T(8,128)S(1)}) custom-call(s32[32]{0:T(128)S(1)} %copy-done.5, s32[32]{0:T(128)S(1)} %copy-done.6, s32[32]{0:T(128)S(1)} %copy-done.7, f32[416,128]{1,0:T(8,128)S(1)} %bitcast.35, s32[4,4096]{1,0:T(4,128)S(1)} %copy-done, f32[4,4096]{1,0:T(4,128)S(1)} %copy-done.1, ...), custom_call_target="tpu_custom_call" | custom-call | tf_op jit(solution)/shard_map/pallas_call | solution.py:643
  72.0 11.6 %all_to_all.27 = f32[416,1,128]{2,1,0:T(1,128)S(1)} all-to-all(f32[416,1,128]{2,1,0:T(1,128)S(1)} %bitcast.39), channel_id=1, replica_groups=mesh['lat'=4,'lon'=8] {'lat','lon'}, dimensions={0} | all-to-all | bytes 425984 | tf_op jit(solution)/shard_map/all_to_all | solution.py:691
  83.6 1.1 shard_map.127
  84.7 2.0 %collective-permute-start.4 = (f32[8,256]{1,0:T(8,128)S(1)}, f32[8,256]{1,0:T(8,128)S(1)}, u32[]{:S(2)}, u32[]{:S(2)}) collective-permute-start(f32[8,256]{1,0:T(8,128)S(1)} %get-tuple-element.43), channel_id=1, source_target_pairs={{0,7},{1,0},{2,1},{3,2},{4,3},{5,4},{6,5},{7,6},{8,15},{9,8},{10,9... | collective-permute-start | bytes 24584 | tf_op jit(solution)/shard_map/ppermute | solution.py:700
  86.7 0.8 collective-permute-done.4.east_ref.refs_3_
  87.5 4.4 %collective-permute-done.5.west_ref.refs_4_ = f32[8,256]{1,0:T(8,128)S(1)} collective-permute-done((f32[8,256]{1,0:T(8,128)S(1)}, f32[8,256]{1,0:T(8,128)S(1)}, u32[]{:S(2)}, u32[]{:S(2)}) %collective-permute-start.5) | collective-permute-done | bytes 8224 | tf_op jit(solution)/shard_map/ppermute | solution.py:700
  91.9 2.3 %collective-permute-start.6 = (f32[20,8,256]{2,1,0:T(8,128)S(1)}, f32[20,8,256]{2,1,0:T(8,128)S(1)}, u32[]{:S(2)}, u32[]{:S(2)}) collective-permute-start(f32[20,8,256]{2,1,0:T(8,128)S(1)} %get-tuple-element.45), channel_id=1, source_target_pairs={{0,8},{1,9},{2,10},{3,11},{4,12},{5,13},{6,14},{7,15},{8,16},{9,17... | collective-permute-start | bytes 491528 | tf_op jit(solution)/shard_map/ppermute | solution.py:700
  94.2 2.3 %collective-permute-done.6.refs_0_ = f32[20,8,256]{2,1,0:T(8,128)S(1)} collective-permute-done((f32[20,8,256]{2,1,0:T(8,128)S(1)}, f32[20,8,256]{2,1,0:T(8,128)S(1)}, u32[]{:S(2)}, u32[]{:S(2)}) %collective-permute-start.6) | collective-permute-done | bytes 163872 | tf_op jit(solution)/shard_map/ppermute | solution.py:700
  96.5 3.5 %collective-permute-done.7.refs_2_ = f32[20,8,256]{2,1,0:T(8,128)S(1)} collective-permute-done((f32[20,8,256]{2,1,0:T(8,128)S(1)}, f32[20,8,256]{2,1,0:T(8,128)S(1)}, u32[]{:S(2)}, u32[]{:S(2)}) %collective-permute-start.7) | collective-permute-done | bytes 163872 | tf_op jit(solution)/shard_map/ppermute | solution.py:700
  100.0 13.3 %shard_map.129 = (f32[416,128]{1,0:T(8,128)S(1)}, f32[16,64,384]{2,1,0:T(8,128)S(1)}) custom-call(s32[2]{0:T(128)S(1)} %add_convert_fusion.edge_ref, f32[20,8,256]{2,1,0:T(8,128)S(1)} %collective-permute-done.6.refs_0_, f32[24,8,256]{2,1,0:T(8,128)S(1)} %get-tuple-element.42.main_ref.refs_1_, f32[20,8,256]{2,1,0:T(8,128)S(1)} %collective-permute-done.7.refs_2_, ...), custom_call_target="tpu_custom_call" | custom-call | tf_op jit(solution)/shard_map/pallas_call | solution.py:643
  113.3 10.2 %all_to_all.28 = f32[416,1,128]{2,1,0:T(1,128)S(1)} all-to-all(f32[416,1,128]{2,1,0:T(1,128)S(1)} %bitcast.37), channel_id=1, replica_groups=mesh['lat'=4,'lon'=8] {'lat','lon'}, dimensions={0} | all-to-all | bytes 425984 | tf_op jit(solution)/shard_map/all_to_all | solution.py:691
  123.4 4.5 %shard_map.130 = (f32[416,128]{1,0:T(8,128)S(1)}, f32[32,128]{1,0:T(8,128)}, f32[8,128]{1,0:T(8,128)S(1)}) custom-call(s32[32]{0:T(128)S(1)} %copy-done.5, s32[32]{0:T(128)S(1)} %copy-done.6, s32[32]{0:T(128)S(1)} %copy-done.7, f32[416,128]{1,0:T(8,128)S(1)} %bitcast.31, s32[4,4096]{1,0:T(4,128)S(1)} %copy-done, f32[4,4096]{1,0:T(4,128)S(1)} %copy-done.1, ...), custom_call_target="tpu_custom_call" | custom-call | tf_op jit(solution)/shard_map/pallas_call | solution.py:643
  128.0 11.6 %all_to_all.29 = f32[416,1,128]{2,1,0:T(1,128)S(1)} all-to-all(f32[416,1,128]{2,1,0:T(1,128)S(1)} %bitcast.38), channel_id=1, replica_groups=mesh['lat'=4,'lon'=8] {'lat','lon'}, dimensions={0} | all-to-all | bytes 425984 | tf_op jit(solution)/shard_map/all_to_all | solution.py:691
  139.6 1.1 shard_map.131
  140.7 2.0 %collective-permute-start.8 = (f32[8,256]{1,0:T(8,128)S(1)}, f32[8,256]{1,0:T(8,128)S(1)}, u32[]{:S(2)}, u32[]{:S(2)}) collective-permute-start(f32[8,256]{1,0:T(8,128)S(1)} %get-tuple-element.55), channel_id=1, source_target_pairs={{0,7},{1,0},{2,1},{3,2},{4,3},{5,4},{6,5},{7,6},{8,15},{9,8},{10,9... | collective-permute-start | bytes 24584 | tf_op jit(solution)/shard_map/ppermute | solution.py:700
  143.5 4.4 %collective-permute-done.9.west_ref.refs_4_ = f32[8,256]{1,0:T(8,128)S(1)} collective-permute-done((f32[8,256]{1,0:T(8,128)S(1)}, f32[8,256]{1,0:T(8,128)S(1)}, u32[]{:S(2)}, u32[]{:S(2)}) %collective-permute-start.9) | collective-permute-done | bytes 8224 | tf_op jit(solution)/shard_map/ppermute | solution.py:700
  147.9 2.3 %collective-permute-start.10 = (f32[8,8,256]{2,1,0:T(8,128)S(1)}, f32[8,8,256]{2,1,0:T(8,128)S(1)}, u32[]{:S(2)}, u32[]{:S(2)}) collective-permute-start(f32[8,8,256]{2,1,0:T(8,128)S(1)} %get-tuple-element.57), channel_id=1, source_target_pairs={{0,8},{1,9},{2,10},{3,11},{4,12},{5,13},{6,14},{7,15},{8,16},{9,17... | collective-permute-start | bytes 196616 | tf_op jit(solution)/shard_map/ppermute | solution.py:700
  150.2 1.3 collective-permute-done.10.refs_0_
  151.6 2.4 %collective-permute-done.11.refs_2_ = f32[8,8,256]{2,1,0:T(8,128)S(1)} collective-permute-done((f32[8,8,256]{2,1,0:T(8,128)S(1)}, f32[8,8,256]{2,1,0:T(8,128)S(1)}, u32[]{:S(2)}, u32[]{:S(2)}) %collective-permute-start.11) | collective-permute-done | bytes 65568 | tf_op jit(solution)/shard_map/ppermute | solution.py:700
  153.9 6.1 %shard_map.133 = (f32[512,256]{1,0:T(8,128)}, f32[512,256]{1,0:T(8,128)}) custom-call(s32[2]{0:T(128)S(1)} %add_convert_fusion.edge_ref, f32[8,8,256]{2,1,0:T(8,128)S(1)} %collective-permute-done.10.refs_0_, f32[24,8,256]{2,1,0:T(8,128)S(1)} %get-tuple-element.54.main_ref.refs_1_, f32[8,8,256]{2,1,0:T(8,128)S(1)} %collective-permute-done.11.refs_2_, ...), custom_call_target="tpu_custom_call" | custom-call | tf_op jit(solution)/shard_map/pallas_call | solution.py:643
  (32 shorter events, 1.2 us)
Async XLA Ops:
  0.6 43.8 %copy-start.3 = (s32[1,2048]{1,0:T(1,128)S(1)}, s32[1,2048]{1,0:T(1,128)}, u32[]{:S(2)}) copy-start(s32[1,2048]{1,0:T(1,128)} %send_ref.3) | copy-start | bytes 24580
  0.6 32.1 %copy-start.8 = (f32[8,64]{1,0:T(8,128)S(1)}, f32[8,64]{1,0:T(8,128)}, u32[]{:S(2)}) copy-start(f32[8,64]{1,0:T(8,128)} %param.13) | copy-start | bytes 6148
  4.5 63.3 %copy-start.4 = (f32[4096]{0:T(1024)S(1)}, f32[4096]{0:T(1024)}, u32[]{:S(2)}) copy-start(f32[4096]{0:T(1024)} %param.15) | copy-start | bytes 49156
  4.5 63.3 %copy-start.5 = (s32[32]{0:T(128)S(1)}, s32[32]{0:T(128)}, u32[]{:S(2)}) copy-start(s32[32]{0:T(128)} %count_ref.5) | copy-start | bytes 388
  4.6 63.3 %copy-start.6 = (s32[32]{0:T(128)S(1)}, s32[32]{0:T(128)}, u32[]{:S(2)}) copy-start(s32[32]{0:T(128)} %type_ref.5) | copy-start | bytes 388
  4.6 63.3 %copy-start.7 = (s32[32]{0:T(128)S(1)}, s32[32]{0:T(128)}, u32[]{:S(2)}) copy-start(s32[32]{0:T(128)} %window_ref.5) | copy-start | bytes 388
  20.5 47.4 %copy-start = (s32[4,4096]{1,0:T(4,128)S(1)}, s32[4,4096]{1,0:T(4,128)}, u32[]{:S(2)}) copy-start(s32[4,4096]{1,0:T(4,128)} %refs_1_.5) | copy-start | bytes 196612
  20.5 47.4 %copy-start.1 = (f32[4,4096]{1,0:T(4,128)S(1)}, f32[4,4096]{1,0:T(4,128)}, u32[]{:S(2)}) copy-start(f32[4,4096]{1,0:T(4,128)} %refs_2_.3) | copy-start | bytes 196612
  20.5 1.0 copy-start.2
  23.2 2.8 %collective-permute-start = (f32[8,512]{1,0:T(8,128)S(1)}, f32[8,512]{1,0:T(8,128)S(1)}, u32[]{:S(2)}, u32[]{:S(2)}) collective-permute-start(f32[8,512]{1,0:T(8,128)S(1)} %get-tuple-element.36), channel_id=1, source_target_pairs={{0,7},{1,0},{2,1},{3,2},{4,3},{5,4},{6,5},{7,6},{8,15},{9,8},{10,9... | collective-permute-start | bytes 49160 | tf_op jit(solution)/shard_map/ppermute | solution.py:700
  25.1 5.3 %collective-permute-start.1 = (f32[8,512]{1,0:T(8,128)S(1)}, f32[8,512]{1,0:T(8,128)S(1)}, u32[]{:S(2)}, u32[]{:S(2)}) collective-permute-start(f32[8,512]{1,0:T(8,128)S(1)} %get-tuple-element.37), channel_id=1, source_target_pairs={{0,1},{1,2},{2,3},{3,4},{4,5},{5,6},{6,7},{7,0},{8,9},{9,10},{10,1... | collective-permute-start | bytes 49160 | tf_op jit(solution)/shard_map/ppermute | solution.py:700
  30.5 10.5 %collective-permute-start.2 = (f32[54,8,256]{2,1,0:T(8,128)S(1)}, f32[54,8,256]{2,1,0:T(8,128)S(1)}, u32[]{:S(2)}, u32[]{:S(2)}) collective-permute-start(f32[54,8,256]{2,1,0:T(8,128)S(1)} %get-tuple-element.38), channel_id=1, source_target_pairs={{0,8},{1,9},{2,10},{3,11},{4,12},{5,13},{6,14},{7,15},{8,16},{9,17... | collective-permute-start | bytes 1327112 | tf_op jit(solution)/shard_map/ppermute | solution.py:700
  32.8 11.7 %collective-permute-start.3 = (f32[54,8,256]{2,1,0:T(8,128)S(1)}, f32[54,8,256]{2,1,0:T(8,128)S(1)}, u32[]{:S(2)}, u32[]{:S(2)}) collective-permute-start(f32[54,8,256]{2,1,0:T(8,128)S(1)} %get-tuple-element.39), channel_id=1, source_target_pairs={{0,24},{1,25},{2,26},{3,27},{4,28},{5,29},{6,30},{7,31},{8,0},{9,1... | collective-permute-start | bytes 1327112 | tf_op jit(solution)/shard_map/ppermute | solution.py:700
  84.7 2.8 %collective-permute-start.4 = (f32[8,256]{1,0:T(8,128)S(1)}, f32[8,256]{1,0:T(8,128)S(1)}, u32[]{:S(2)}, u32[]{:S(2)}) collective-permute-start(f32[8,256]{1,0:T(8,128)S(1)} %get-tuple-element.43), channel_id=1, source_target_pairs={{0,7},{1,0},{2,1},{3,2},{4,3},{5,4},{6,5},{7,6},{8,15},{9,8},{10,9... | collective-permute-start | bytes 24584 | tf_op jit(solution)/shard_map/ppermute | solution.py:700
  86.7 5.2 %collective-permute-start.5 = (f32[8,256]{1,0:T(8,128)S(1)}, f32[8,256]{1,0:T(8,128)S(1)}, u32[]{:S(2)}, u32[]{:S(2)}) collective-permute-start(f32[8,256]{1,0:T(8,128)S(1)} %get-tuple-element.44), channel_id=1, source_target_pairs={{0,1},{1,2},{2,3},{3,4},{4,5},{5,6},{6,7},{7,0},{8,9},{9,10},{10,1... | collective-permute-start | bytes 24584 | tf_op jit(solution)/shard_map/ppermute | solution.py:700
  91.9 4.6 %collective-permute-start.6 = (f32[20,8,256]{2,1,0:T(8,128)S(1)}, f32[20,8,256]{2,1,0:T(8,128)S(1)}, u32[]{:S(2)}, u32[]{:S(2)}) collective-permute-start(f32[20,8,256]{2,1,0:T(8,128)S(1)} %get-tuple-element.45), channel_id=1, source_target_pairs={{0,8},{1,9},{2,10},{3,11},{4,12},{5,13},{6,14},{7,15},{8,16},{9,17... | collective-permute-start | bytes 491528 | tf_op jit(solution)/shard_map/ppermute | solution.py:700
  94.2 5.7 %collective-permute-start.7 = (f32[20,8,256]{2,1,0:T(8,128)S(1)}, f32[20,8,256]{2,1,0:T(8,128)S(1)}, u32[]{:S(2)}, u32[]{:S(2)}) collective-permute-start(f32[20,8,256]{2,1,0:T(8,128)S(1)} %get-tuple-element.46), channel_id=1, source_target_pairs={{0,24},{1,25},{2,26},{3,27},{4,28},{5,29},{6,30},{7,31},{8,0},{9,1... | collective-permute-start | bytes 491528 | tf_op jit(solution)/shard_map/ppermute | solution.py:700
  140.7 2.8 %collective-permute-start.8 = (f32[8,256]{1,0:T(8,128)S(1)}, f32[8,256]{1,0:T(8,128)S(1)}, u32[]{:S(2)}, u32[]{:S(2)}) collective-permute-start(f32[8,256]{1,0:T(8,128)S(1)} %get-tuple-element.55), channel_id=1, source_target_pairs={{0,7},{1,0},{2,1},{3,2},{4,3},{5,4},{6,5},{7,6},{8,15},{9,8},{10,9... | collective-permute-start | bytes 24584 | tf_op jit(solution)/shard_map/ppermute | solution.py:700
  142.7 5.2 %collective-permute-start.9 = (f32[8,256]{1,0:T(8,128)S(1)}, f32[8,256]{1,0:T(8,128)S(1)}, u32[]{:S(2)}, u32[]{:S(2)}) collective-permute-start(f32[8,256]{1,0:T(8,128)S(1)} %get-tuple-element.56), channel_id=1, source_target_pairs={{0,1},{1,2},{2,3},{3,4},{4,5},{5,6},{6,7},{7,0},{8,9},{9,10},{10,1... | collective-permute-start | bytes 24584 | tf_op jit(solution)/shard_map/ppermute | solution.py:700
  147.9 3.6 %collective-permute-start.10 = (f32[8,8,256]{2,1,0:T(8,128)S(1)}, f32[8,8,256]{2,1,0:T(8,128)S(1)}, u32[]{:S(2)}, u32[]{:S(2)}) collective-permute-start(f32[8,8,256]{2,1,0:T(8,128)S(1)} %get-tuple-element.57), channel_id=1, source_target_pairs={{0,8},{1,9},{2,10},{3,11},{4,12},{5,13},{6,14},{7,15},{8,16},{9,17... | collective-permute-start | bytes 196616 | tf_op jit(solution)/shard_map/ppermute | solution.py:700
  150.2 3.7 %collective-permute-start.11 = (f32[8,8,256]{2,1,0:T(8,128)S(1)}, f32[8,8,256]{2,1,0:T(8,128)S(1)}, u32[]{:S(2)}, u32[]{:S(2)}) collective-permute-start(f32[8,8,256]{2,1,0:T(8,128)S(1)} %get-tuple-element.58), channel_id=1, source_target_pairs={{0,24},{1,25},{2,26},{3,27},{4,28},{5,29},{6,30},{7,31},{8,0},{9,1... | collective-permute-start | bytes 196616 | tf_op jit(solution)/shard_map/ppermute | solution.py:700

commit v4 on v3

--- a/solution.py
+++ b/solution.py
@@ -271,7 +271,7 @@
             total[j] += both[:devices] + both[devices:]
         return energy
 
-    together = 8
+    together = 16 if mode == "right" else 8
     while blocks % together:
         together -= 1
     energy = jnp.zeros((1, BLOCK_ROWS), F32)
@@ -452,7 +452,7 @@
         coef[4, e] = jnp.maximum(-v, 0.0)
         return carry
 
-    loop(0, rows, 4, prepare)
+    loop(0, rows, 8, prepare)
 
     into = into_ref[...]
     top, rest = halves(into)
@@ -512,7 +512,7 @@
         fields[0][e] = force(WIN - 1, e)
         return carry
 
-    loop(0, rows, 8, begin)
+    loop(0, rows, 12, begin)
     now = 0
     for step in range(1, REACH):
         old, new = fields[now], fields[1 - now]
@@ -523,7 +523,7 @@
             adjoint(old, e, put_in(new, e), extra)
             return carry
 
-        loop(step, rows - step, 4 if w is not None else 2, body)
+        loop(step, rows - step, 11 if w is None else 10, body)
         now = 1 - now
     old, new = fields[now], fields[1 - now]
 
@@ -550,7 +550,7 @@
             adjoint(old, e, put, force(0, e))
             return carry
 
-        loop(halo, halo + lat_cells, 4, finish)
+        loop(halo, halo + lat_cells, 8, finish)
         for c in range(cols):
             part = slice(c * LANES, (c + 1) * LANES)
             increment_out[:, part] = ends[c][...]
@@ -581,7 +581,7 @@
 
     zero = jnp.zeros((SUB, lon_cells), F32)
     sums = (zero,) if mode == "right" else (zero, zero)
-    sums = loop(REACH, rows - REACH, 4, update, sums)
+    sums = loop(REACH, rows - REACH, 8, update, sums)
     sums = [jnp.sum(jnp.sum(s, axis=1, keepdims=True), axis=0, keepdims=True) for s in sums]
     now = 1 - now
 
@@ -609,7 +609,7 @@
             tangent(old, e, put_in(new, e))
             return carry
 
-        loop(REACH + step, rows - REACH - step, 2, body)
+        loop(REACH + step, rows - REACH - step, 11, body)
         now = 1 - now
         if step % STEP_WIN == 0:
             look(fields[now], step // STEP_WIN)

time: 160 us -> 153 us (0.956)
  Pallas kernels: 49.2 us -> 41.9 us
    pallas_call x12, Pallas kernels: 49.2 us -> 41.9 us  [call(): pl.pallas_call(kernel, out_shape=[jax.ShapeDtypeStruct(s, F32) if isinsta...]
where the time goes in v4:
time: 153 us
  blocking collectives  59.5 us (39%)
  Pallas kernels  41.9 us (27%)
  waiting for transfers between devices  36.4 us (24%)
  starting transfers between devices  13 us (8%)
    all_to_all x5, blocking collectives, exchange(): x = lax.all_to_all(x, AXES, split_axis=0, concat_axis=0, tiled=True)  59.5 us
    pallas_call x12, Pallas kernels, call(): pl.pallas_call(kernel, out_shape=[jax.ShapeDtypeStruct(s, F32) if isinsta...  41.9 us
    ppermute x12, waiting for transfers between devices, send(): return lax.ppermute(x, AXES, pairs)  36.4 us
    ppermute x12, starting transfers between devices, send(): return lax.ppermute(x, AXES, pairs)  13 us
  transfers between devices with their start and end apart: 12, of which 12 were waited for; matrix products, arithmetic and copies ran while one was open for 0% of the time, Pallas kernels for 0%

profile of v4, /device:TPU:1, one launch (start us, length us, event | category | flops | bytes accessed | tf_op | source)
XLA Modules:
  0.0 152.8 jit_solution(16732471446119418123)
XLA Ops:
  0.7 3.6 %shard_map.122 = (f32[416,128]{1,0:T(8,128)}, f32[37,8,256]{2,1,0:T(8,128)}) custom-call(s32[32]{0:T(128)} %count_ref.5, s32[32]{0:T(128)} %type_ref.5, s32[32]{0:T(128)} %window_ref.5, s32[4,4096]{1,0:T(4,128)} %refs_1_.5, f32[4,4096]{1,0:T(4,128)} %refs_2_.3, f32[32,128]{1,0:T(8,128)} %bitcast.40, f32[32,128]{1,0:T(8,128)} %bitcast.47, ...), custom_call_target="tpu_custom_call" | custom-call | tf_op jit(solution)/shard_map/pallas_call | solution.py:643
  4.3 15.9 %all_to_all.25 = f32[416,1,128]{2,1,0:T(1,128)S(1)} all-to-all(f32[416,1,128]{2,1,0:T(1,128)} %bitcast.43), channel_id=1, replica_groups=mesh['lat'=4,'lon'=8] {'lat','lon'}, dimensions={0} | all-to-all | bytes 425984 | tf_op jit(solution)/shard_map/all_to_all | solution.py:691
  20.2 1.0 copy-done.2
  21.2 1.7 %shard_map.123 = (f32[56,8,256]{2,1,0:T(8,128)S(1)}, f32[8,512]{1,0:T(8,128)S(1)}, f32[8,512]{1,0:T(8,128)S(1)}, f32[8,128]{1,0:T(8,128)}) custom-call(f32[416,128]{1,0:T(8,128)S(1)} %bitcast.34, f32[37,8,256]{2,1,0:T(8,128)S(1)} %copy-done.2), custom_call_target="tpu_custom_call" | custom-call | tf_op jit(solution)/shard_map/pallas_call | solution.py:643
  22.9 1.9 %collective-permute-start = (f32[8,512]{1,0:T(8,128)S(1)}, f32[8,512]{1,0:T(8,128)S(1)}, u32[]{:S(2)}, u32[]{:S(2)}) collective-permute-start(f32[8,512]{1,0:T(8,128)S(1)} %get-tuple-element.36), channel_id=1, source_target_pairs={{0,7},{1,0},{2,1},{3,2},{4,3},{5,4},{6,5},{7,6},{8,15},{9,8},{10,9... | collective-permute-start | bytes 49160 | tf_op jit(solution)/shard_map/ppermute | solution.py:700
  24.8 0.9 collective-permute-done.east_ref.refs_3_
  25.7 4.4 %collective-permute-done.1.west_ref.refs_4_ = f32[8,512]{1,0:T(8,128)S(1)} collective-permute-done((f32[8,512]{1,0:T(8,128)S(1)}, f32[8,512]{1,0:T(8,128)S(1)}, u32[]{:S(2)}, u32[]{:S(2)}) %collective-permute-start.1) | collective-permute-done | bytes 16416 | tf_op jit(solution)/shard_map/ppermute | solution.py:700
  30.2 2.3 %collective-permute-start.2 = (f32[54,8,256]{2,1,0:T(8,128)S(1)}, f32[54,8,256]{2,1,0:T(8,128)S(1)}, u32[]{:S(2)}, u32[]{:S(2)}) collective-permute-start(f32[54,8,256]{2,1,0:T(8,128)S(1)} %get-tuple-element.38), channel_id=1, source_target_pairs={{0,8},{1,9},{2,10},{3,11},{4,12},{5,13},{6,14},{7,15},{8,16},{9,17... | collective-permute-start | bytes 1327112 | tf_op jit(solution)/shard_map/ppermute | solution.py:700
  32.8 7.9 %collective-permute-done.2.refs_0_ = f32[54,8,256]{2,1,0:T(8,128)S(1)} collective-permute-done((f32[54,8,256]{2,1,0:T(8,128)S(1)}, f32[54,8,256]{2,1,0:T(8,128)S(1)}, u32[]{:S(2)}, u32[]{:S(2)}) %collective-permute-start.2) | collective-permute-done | bytes 442400 | tf_op jit(solution)/shard_map/ppermute | solution.py:700
  40.7 3.6 %collective-permute-done.3.refs_2_ = f32[54,8,256]{2,1,0:T(8,128)S(1)} collective-permute-done((f32[54,8,256]{2,1,0:T(8,128)S(1)}, f32[54,8,256]{2,1,0:T(8,128)S(1)}, u32[]{:S(2)}, u32[]{:S(2)}) %collective-permute-start.3) | collective-permute-done | bytes 442400 | tf_op jit(solution)/shard_map/ppermute | solution.py:700
  44.2 10.2 %shard_map.125 = (f32[416,128]{1,0:T(8,128)S(1)}, f32[16,64,384]{2,1,0:T(8,128)S(1)}, f32[2,24,16,384]{3,2,1,0:T(8,128)S(1)}) custom-call(s32[2]{0:T(128)S(1)} %add_convert_fusion.edge_ref, f32[54,8,256]{2,1,0:T(8,128)S(1)} %collective-permute-done.2.refs_0_, f32[56,8,256]{2,1,0:T(8,128)S(1)} %get-tuple-element.35.main_ref.refs_1_, ...), custom_call_target="tpu_custom_call" | custom-call | tf_op jit(solution)/shard_map/pallas_call | solution.py:643
  54.5 10.2 %all_to_all.26 = f32[416,1,128]{2,1,0:T(1,128)S(1)} all-to-all(f32[416,1,128]{2,1,0:T(1,128)S(1)} %bitcast.36), channel_id=1, replica_groups=mesh['lat'=4,'lon'=8] {'lat','lon'}, dimensions={0} | all-to-all | bytes 425984 | tf_op jit(solution)/shard_map/all_to_all | solution.py:691
  64.7 4.0 %shard_map.126 = (f32[416,128]{1,0:T(8,128)S(1)}, f32[32,128]{1,0:T(8,128)S(1)}, f32[8,128]{1,0:T(8,128)S(1)}) custom-call(s32[32]{0:T(128)S(1)} %copy-done.5, s32[32]{0:T(128)S(1)} %copy-done.6, s32[32]{0:T(128)S(1)} %copy-done.7, f32[416,128]{1,0:T(8,128)S(1)} %bitcast.35, s32[4,4096]{1,0:T(4,128)S(1)} %copy-done, f32[4,4096]{1,0:T(4,128)S(1)} %copy-done.1, ...), custom_call_target="tpu_custom_call" | custom-call | tf_op jit(solution)/shard_map/pallas_call | solution.py:643
  68.7 11.6 %all_to_all.27 = f32[416,1,128]{2,1,0:T(1,128)S(1)} all-to-all(f32[416,1,128]{2,1,0:T(1,128)S(1)} %bitcast.39), channel_id=1, replica_groups=mesh['lat'=4,'lon'=8] {'lat','lon'}, dimensions={0} | all-to-all | bytes 425984 | tf_op jit(solution)/shard_map/all_to_all | solution.py:691
  80.3 1.1 shard_map.127
  81.5 2.0 %collective-permute-start.4 = (f32[8,256]{1,0:T(8,128)S(1)}, f32[8,256]{1,0:T(8,128)S(1)}, u32[]{:S(2)}, u32[]{:S(2)}) collective-permute-start(f32[8,256]{1,0:T(8,128)S(1)} %get-tuple-element.43), channel_id=1, source_target_pairs={{0,7},{1,0},{2,1},{3,2},{4,3},{5,4},{6,5},{7,6},{8,15},{9,8},{10,9... | collective-permute-start | bytes 24584 | tf_op jit(solution)/shard_map/ppermute | solution.py:700
  83.4 0.8 collective-permute-done.4.east_ref.refs_3_
  84.2 4.4 %collective-permute-done.5.west_ref.refs_4_ = f32[8,256]{1,0:T(8,128)S(1)} collective-permute-done((f32[8,256]{1,0:T(8,128)S(1)}, f32[8,256]{1,0:T(8,128)S(1)}, u32[]{:S(2)}, u32[]{:S(2)}) %collective-permute-start.5) | collective-permute-done | bytes 8224 | tf_op jit(solution)/shard_map/ppermute | solution.py:700
  88.7 2.3 %collective-permute-start.6 = (f32[20,8,256]{2,1,0:T(8,128)S(1)}, f32[20,8,256]{2,1,0:T(8,128)S(1)}, u32[]{:S(2)}, u32[]{:S(2)}) collective-permute-start(f32[20,8,256]{2,1,0:T(8,128)S(1)} %get-tuple-element.45), channel_id=1, source_target_pairs={{0,8},{1,9},{2,10},{3,11},{4,12},{5,13},{6,14},{7,15},{8,16},{9,17... | collective-permute-start | bytes 491528 | tf_op jit(solution)/shard_map/ppermute | solution.py:700
  91.2 2.1 %collective-permute-done.6.refs_0_ = f32[20,8,256]{2,1,0:T(8,128)S(1)} collective-permute-done((f32[20,8,256]{2,1,0:T(8,128)S(1)}, f32[20,8,256]{2,1,0:T(8,128)S(1)}, u32[]{:S(2)}, u32[]{:S(2)}) %collective-permute-start.6) | collective-permute-done | bytes 163872 | tf_op jit(solution)/shard_map/ppermute | solution.py:700
  93.3 3.5 %collective-permute-done.7.refs_2_ = f32[20,8,256]{2,1,0:T(8,128)S(1)} collective-permute-done((f32[20,8,256]{2,1,0:T(8,128)S(1)}, f32[20,8,256]{2,1,0:T(8,128)S(1)}, u32[]{:S(2)}, u32[]{:S(2)}) %collective-permute-start.7) | collective-permute-done | bytes 163872 | tf_op jit(solution)/shard_map/ppermute | solution.py:700
  96.7 10.3 %shard_map.129 = (f32[416,128]{1,0:T(8,128)S(1)}, f32[16,64,384]{2,1,0:T(8,128)S(1)}) custom-call(s32[2]{0:T(128)S(1)} %add_convert_fusion.edge_ref, f32[20,8,256]{2,1,0:T(8,128)S(1)} %collective-permute-done.6.refs_0_, f32[24,8,256]{2,1,0:T(8,128)S(1)} %get-tuple-element.42.main_ref.refs_1_, f32[20,8,256]{2,1,0:T(8,128)S(1)} %collective-permute-done.7.refs_2_, ...), custom_call_target="tpu_custom_call" | custom-call | tf_op jit(solution)/shard_map/pallas_call | solution.py:643
  107.1 10.2 %all_to_all.28 = f32[416,1,128]{2,1,0:T(1,128)S(1)} all-to-all(f32[416,1,128]{2,1,0:T(1,128)S(1)} %bitcast.37), channel_id=1, replica_groups=mesh['lat'=4,'lon'=8] {'lat','lon'}, dimensions={0} | all-to-all | bytes 425984 | tf_op jit(solution)/shard_map/all_to_all | solution.py:691
  117.2 4.5 %shard_map.130 = (f32[416,128]{1,0:T(8,128)S(1)}, f32[32,128]{1,0:T(8,128)}, f32[8,128]{1,0:T(8,128)S(1)}) custom-call(s32[32]{0:T(128)S(1)} %copy-done.5, s32[32]{0:T(128)S(1)} %copy-done.6, s32[32]{0:T(128)S(1)} %copy-done.7, f32[416,128]{1,0:T(8,128)S(1)} %bitcast.31, s32[4,4096]{1,0:T(4,128)S(1)} %copy-done, f32[4,4096]{1,0:T(4,128)S(1)} %copy-done.1, ...), custom_call_target="tpu_custom_call" | custom-call | tf_op jit(solution)/shard_map/pallas_call | solution.py:643
  121.7 11.6 %all_to_all.29 = f32[416,1,128]{2,1,0:T(1,128)S(1)} all-to-all(f32[416,1,128]{2,1,0:T(1,128)S(1)} %bitcast.38), channel_id=1, replica_groups=mesh['lat'=4,'lon'=8] {'lat','lon'}, dimensions={0} | all-to-all | bytes 425984 | tf_op jit(solution)/shard_map/all_to_all | solution.py:691
  133.4 1.1 shard_map.131
  134.5 2.0 %collective-permute-start.8 = (f32[8,256]{1,0:T(8,128)S(1)}, f32[8,256]{1,0:T(8,128)S(1)}, u32[]{:S(2)}, u32[]{:S(2)}) collective-permute-start(f32[8,256]{1,0:T(8,128)S(1)} %get-tuple-element.55), channel_id=1, source_target_pairs={{0,7},{1,0},{2,1},{3,2},{4,3},{5,4},{6,5},{7,6},{8,15},{9,8},{10,9... | collective-permute-start | bytes 24584 | tf_op jit(solution)/shard_map/ppermute | solution.py:700
  137.3 4.4 %collective-permute-done.9.west_ref.refs_4_ = f32[8,256]{1,0:T(8,128)S(1)} collective-permute-done((f32[8,256]{1,0:T(8,128)S(1)}, f32[8,256]{1,0:T(8,128)S(1)}, u32[]{:S(2)}, u32[]{:S(2)}) %collective-permute-start.9) | collective-permute-done | bytes 8224 | tf_op jit(solution)/shard_map/ppermute | solution.py:700
  141.7 2.3 %collective-permute-start.10 = (f32[8,8,256]{2,1,0:T(8,128)S(1)}, f32[8,8,256]{2,1,0:T(8,128)S(1)}, u32[]{:S(2)}, u32[]{:S(2)}) collective-permute-start(f32[8,8,256]{2,1,0:T(8,128)S(1)} %get-tuple-element.57), channel_id=1, source_target_pairs={{0,8},{1,9},{2,10},{3,11},{4,12},{5,13},{6,14},{7,15},{8,16},{9,17... | collective-permute-start | bytes 196616 | tf_op jit(solution)/shard_map/ppermute | solution.py:700
  144.0 1.3 collective-permute-done.10.refs_0_
  145.3 2.4 %collective-permute-done.11.refs_2_ = f32[8,8,256]{2,1,0:T(8,128)S(1)} collective-permute-done((f32[8,8,256]{2,1,0:T(8,128)S(1)}, f32[8,8,256]{2,1,0:T(8,128)S(1)}, u32[]{:S(2)}, u32[]{:S(2)}) %collective-permute-start.11) | collective-permute-done | bytes 65568 | tf_op jit(solution)/shard_map/ppermute | solution.py:700
  147.7 5.1 %shard_map.133 = (f32[512,256]{1,0:T(8,128)}, f32[512,256]{1,0:T(8,128)}) custom-call(s32[2]{0:T(128)S(1)} %add_convert_fusion.edge_ref, f32[8,8,256]{2,1,0:T(8,128)S(1)} %collective-permute-done.10.refs_0_, f32[24,8,256]{2,1,0:T(8,128)S(1)} %get-tuple-element.54.main_ref.refs_1_, f32[8,8,256]{2,1,0:T(8,128)S(1)} %collective-permute-done.11.refs_2_, ...), custom_call_target="tpu_custom_call" | custom-call | tf_op jit(solution)/shard_map/pallas_call | solution.py:643
  (32 shorter events, 1.3 us)
Async XLA Ops:
  0.6 43.6 %copy-start.3 = (s32[1,2048]{1,0:T(1,128)S(1)}, s32[1,2048]{1,0:T(1,128)}, u32[]{:S(2)}) copy-start(s32[1,2048]{1,0:T(1,128)} %send_ref.3) | copy-start | bytes 24580
  0.6 31.9 %copy-start.8 = (f32[8,64]{1,0:T(8,128)S(1)}, f32[8,64]{1,0:T(8,128)}, u32[]{:S(2)}) copy-start(f32[8,64]{1,0:T(8,128)} %param.13) | copy-start | bytes 6148
  4.3 60.4 %copy-start.4 = (f32[4096]{0:T(1024)S(1)}, f32[4096]{0:T(1024)}, u32[]{:S(2)}) copy-start(f32[4096]{0:T(1024)} %param.15) | copy-start | bytes 49156
  4.3 60.3 %copy-start.5 = (s32[32]{0:T(128)S(1)}, s32[32]{0:T(128)}, u32[]{:S(2)}) copy-start(s32[32]{0:T(128)} %count_ref.5) | copy-start | bytes 388
  4.3 60.3 %copy-start.6 = (s32[32]{0:T(128)S(1)}, s32[32]{0:T(128)}, u32[]{:S(2)}) copy-start(s32[32]{0:T(128)} %type_ref.5) | copy-start | bytes 388
  4.3 60.3 %copy-start.7 = (s32[32]{0:T(128)S(1)}, s32[32]{0:T(128)}, u32[]{:S(2)}) copy-start(s32[32]{0:T(128)} %window_ref.5) | copy-start | bytes 388
  20.2 44.4 %copy-start = (s32[4,4096]{1,0:T(4,128)S(1)}, s32[4,4096]{1,0:T(4,128)}, u32[]{:S(2)}) copy-start(s32[4,4096]{1,0:T(4,128)} %refs_1_.5) | copy-start | bytes 196612
  20.2 44.4 %copy-start.1 = (f32[4,4096]{1,0:T(4,128)S(1)}, f32[4,4096]{1,0:T(4,128)}, u32[]{:S(2)}) copy-start(f32[4,4096]{1,0:T(4,128)} %refs_2_.3) | copy-start | bytes 196612
  20.2 1.0 copy-start.2
  22.9 2.8 %collective-permute-start = (f32[8,512]{1,0:T(8,128)S(1)}, f32[8,512]{1,0:T(8,128)S(1)}, u32[]{:S(2)}, u32[]{:S(2)}) collective-permute-start(f32[8,512]{1,0:T(8,128)S(1)} %get-tuple-element.36), channel_id=1, source_target_pairs={{0,7},{1,0},{2,1},{3,2},{4,3},{5,4},{6,5},{7,6},{8,15},{9,8},{10,9... | collective-permute-start | bytes 49160 | tf_op jit(solution)/shard_map/ppermute | solution.py:700
  24.8 5.3 %collective-permute-start.1 = (f32[8,512]{1,0:T(8,128)S(1)}, f32[8,512]{1,0:T(8,128)S(1)}, u32[]{:S(2)}, u32[]{:S(2)}) collective-permute-start(f32[8,512]{1,0:T(8,128)S(1)} %get-tuple-element.37), channel_id=1, source_target_pairs={{0,1},{1,2},{2,3},{3,4},{4,5},{5,6},{6,7},{7,0},{8,9},{9,10},{10,1... | collective-permute-start | bytes 49160 | tf_op jit(solution)/shard_map/ppermute | solution.py:700
  30.2 10.5 %collective-permute-start.2 = (f32[54,8,256]{2,1,0:T(8,128)S(1)}, f32[54,8,256]{2,1,0:T(8,128)S(1)}, u32[]{:S(2)}, u32[]{:S(2)}) collective-permute-start(f32[54,8,256]{2,1,0:T(8,128)S(1)} %get-tuple-element.38), channel_id=1, source_target_pairs={{0,8},{1,9},{2,10},{3,11},{4,12},{5,13},{6,14},{7,15},{8,16},{9,17... | collective-permute-start | bytes 1327112 | tf_op jit(solution)/shard_map/ppermute | solution.py:700
  32.5 11.7 %collective-permute-start.3 = (f32[54,8,256]{2,1,0:T(8,128)S(1)}, f32[54,8,256]{2,1,0:T(8,128)S(1)}, u32[]{:S(2)}, u32[]{:S(2)}) collective-permute-start(f32[54,8,256]{2,1,0:T(8,128)S(1)} %get-tuple-element.39), channel_id=1, source_target_pairs={{0,24},{1,25},{2,26},{3,27},{4,28},{5,29},{6,30},{7,31},{8,0},{9,1... | collective-permute-start | bytes 1327112 | tf_op jit(solution)/shard_map/ppermute | solution.py:700
  81.5 2.8 %collective-permute-start.4 = (f32[8,256]{1,0:T(8,128)S(1)}, f32[8,256]{1,0:T(8,128)S(1)}, u32[]{:S(2)}, u32[]{:S(2)}) collective-permute-start(f32[8,256]{1,0:T(8,128)S(1)} %get-tuple-element.43), channel_id=1, source_target_pairs={{0,7},{1,0},{2,1},{3,2},{4,3},{5,4},{6,5},{7,6},{8,15},{9,8},{10,9... | collective-permute-start | bytes 24584 | tf_op jit(solution)/shard_map/ppermute | solution.py:700
  83.4 5.2 %collective-permute-start.5 = (f32[8,256]{1,0:T(8,128)S(1)}, f32[8,256]{1,0:T(8,128)S(1)}, u32[]{:S(2)}, u32[]{:S(2)}) collective-permute-start(f32[8,256]{1,0:T(8,128)S(1)} %get-tuple-element.44), channel_id=1, source_target_pairs={{0,1},{1,2},{2,3},{3,4},{4,5},{5,6},{6,7},{7,0},{8,9},{9,10},{10,1... | collective-permute-start | bytes 24584 | tf_op jit(solution)/shard_map/ppermute | solution.py:700
  88.7 4.6 %collective-permute-start.6 = (f32[20,8,256]{2,1,0:T(8,128)S(1)}, f32[20,8,256]{2,1,0:T(8,128)S(1)}, u32[]{:S(2)}, u32[]{:S(2)}) collective-permute-start(f32[20,8,256]{2,1,0:T(8,128)S(1)} %get-tuple-element.45), channel_id=1, source_target_pairs={{0,8},{1,9},{2,10},{3,11},{4,12},{5,13},{6,14},{7,15},{8,16},{9,17... | collective-permute-start | bytes 491528 | tf_op jit(solution)/shard_map/ppermute | solution.py:700
  91.0 5.7 %collective-permute-start.7 = (f32[20,8,256]{2,1,0:T(8,128)S(1)}, f32[20,8,256]{2,1,0:T(8,128)S(1)}, u32[]{:S(2)}, u32[]{:S(2)}) collective-permute-start(f32[20,8,256]{2,1,0:T(8,128)S(1)} %get-tuple-element.46), channel_id=1, source_target_pairs={{0,24},{1,25},{2,26},{3,27},{4,28},{5,29},{6,30},{7,31},{8,0},{9,1... | collective-permute-start | bytes 491528 | tf_op jit(solution)/shard_map/ppermute | solution.py:700
  134.5 2.8 %collective-permute-start.8 = (f32[8,256]{1,0:T(8,128)S(1)}, f32[8,256]{1,0:T(8,128)S(1)}, u32[]{:S(2)}, u32[]{:S(2)}) collective-permute-start(f32[8,256]{1,0:T(8,128)S(1)} %get-tuple-element.55), channel_id=1, source_target_pairs={{0,7},{1,0},{2,1},{3,2},{4,3},{5,4},{6,5},{7,6},{8,15},{9,8},{10,9... | collective-permute-start | bytes 24584 | tf_op jit(solution)/shard_map/ppermute | solution.py:700
  136.5 5.2 %collective-permute-start.9 = (f32[8,256]{1,0:T(8,128)S(1)}, f32[8,256]{1,0:T(8,128)S(1)}, u32[]{:S(2)}, u32[]{:S(2)}) collective-permute-start(f32[8,256]{1,0:T(8,128)S(1)} %get-tuple-element.56), channel_id=1, source_target_pairs={{0,1},{1,2},{2,3},{3,4},{4,5},{5,6},{6,7},{7,0},{8,9},{9,10},{10,1... | collective-permute-start | bytes 24584 | tf_op jit(solution)/shard_map/ppermute | solution.py:700
  141.7 3.7 %collective-permute-start.10 = (f32[8,8,256]{2,1,0:T(8,128)S(1)}, f32[8,8,256]{2,1,0:T(8,128)S(1)}, u32[]{:S(2)}, u32[]{:S(2)}) collective-permute-start(f32[8,8,256]{2,1,0:T(8,128)S(1)} %get-tuple-element.57), channel_id=1, source_target_pairs={{0,8},{1,9},{2,10},{3,11},{4,12},{5,13},{6,14},{7,15},{8,16},{9,17... | collective-permute-start | bytes 196616 | tf_op jit(solution)/shard_map/ppermute | solution.py:700
  144.0 3.7 %collective-permute-start.11 = (f32[8,8,256]{2,1,0:T(8,128)S(1)}, f32[8,8,256]{2,1,0:T(8,128)S(1)}, u32[]{:S(2)}, u32[]{:S(2)}) collective-permute-start(f32[8,8,256]{2,1,0:T(8,128)S(1)} %get-tuple-element.58), channel_id=1, source_target_pairs={{0,24},{1,25},{2,26},{3,27},{4,28},{5,29},{6,30},{7,31},{8,0},{9,1... | collective-permute-start | bytes 196616 | tf_op jit(solution)/shard_map/ppermute | solution.py:700

commit v5 on v4

--- a/solution.py
+++ b/solution.py
@@ -133,6 +133,11 @@
                 found = late[i * SUB : (i + 1) * SUB]
                 typed[w] = found if d == 0 else self.select(d, found, typed[w])
         return typed
+
+
+def one_hot(ids):
+    rows = iota((LANES, ids.shape[1]), 0).astype(F32).astype(BF16)
+    return jnp.where(rows == ids.astype(F32).astype(BF16), jnp.ones((), BF16), jnp.zeros((), BF16))
 
 
 def turn(x, shift):
@@ -212,8 +217,6 @@
         row = iota((SUB, LANES), 0)
         scalar_ref[...] = jnp.where(row == 0, norm, jnp.where(row == 1, ratio, square))
 
-    ids = iota((LANES, BLOCK_ROWS), 0)
-
     def row(x):
         return jnp.concatenate([x[k : k + 1, :] for k in range(points)], axis=1)
 
@@ -226,12 +229,7 @@
             lanes = pl.ds(pl.multiple_of(b * BLOCK_ROWS, BLOCK_ROWS), BLOCK_ROWS)
             slot = slot_ref[:, lanes]
             lane = (slot & (pack.slots - 1)) + shift
-            picks.append(
-                jnp.concatenate(
-                    [jnp.where(ids == lane[k : k + 1, :], 1.0, 0.0) for k in range(points)],
-                    axis=1,
-                ).astype(BF16)
-            )
+            picks.append(one_hot(row(lane)))
             owners.append(iota((devices, wide), 0) == row(slot >> pack.group_bits))
             weights.append(row(weight_ref[:, lanes]))
         if mode == "right":
@@ -271,7 +269,7 @@
             total[j] += both[:devices] + both[devices:]
         return energy
 
-    together = 16 if mode == "right" else 8
+    together = 16
     while blocks % together:
         together -= 1
     energy = jnp.zeros((1, BLOCK_ROWS), F32)
@@ -312,7 +310,7 @@
             strips[q] = (send_ref[at, :, lanes], send_ref[at + half, :, lanes])
     else:
         send = send_ref[...]
-    pick = jnp.where(iota((LANES, pack.recv), 0) == (send & (LANES - 1)), 1.0, 0.0).astype(BF16)
+    pick = one_hot(send & (LANES - 1))
     high = send >> log2(LANES)
 
     every = [pack.read(recv_ref, t) for t in range(tiles)]
@@ -617,12 +615,12 @@
     spare = jnp.where(iota((1, LANES), 1) < LANES // 2, sums[0], sums[-1])
     top, rest = halves(picked[...])
     values = jnp.concatenate([top, rest], axis=1).astype(BF16)
-    chunk = 2 * LANES
+    chunk = 4 * LANES
     parts = lat_cells * cols
     for c in range(pack.recv // chunk):
         send = send_ref[:, c * chunk : (c + 1) * chunk]
-        pick = jnp.where(iota((LANES, chunk), 0) == (send & (LANES - 1)), 1.0, 0.0)
-        pick = jnp.concatenate([pick, pick], axis=0).astype(BF16)
+        pick = one_hot(send & (LANES - 1))
+        pick = jnp.concatenate([pick, pick], axis=0)
         high = send >> log2(LANES)
         every = dot(values, pick)
         typed = []

time: 153 us -> 152 us (level)
  Pallas kernels: 41.9 us -> 40.3 us
    pallas_call x12, Pallas kernels: 41.9 us -> 40.3 us  [call(): pl.pallas_call(kernel, out_shape=[jax.ShapeDtypeStruct(s, F32) if isinsta...]
where the time goes in v5:
time: 152 us; the launch traced here: 151 us
  blocking collectives  59.5 us (39%)
  Pallas kernels  40.3 us (27%)
  waiting for transfers between devices  36.4 us (24%)
  starting transfers between devices  13 us (9%)
    all_to_all x5, blocking collectives, exchange(): x = lax.all_to_all(x, AXES, split_axis=0, concat_axis=0, tiled=True)  59.5 us
    pallas_call x12, Pallas kernels, call(): pl.pallas_call(kernel, out_shape=[jax.ShapeDtypeStruct(s, F32) if isinsta...  40.3 us
    ppermute x12, waiting for transfers between devices, send(): return lax.ppermute(x, AXES, pairs)  36.4 us
    ppermute x12, starting transfers between devices, send(): return lax.ppermute(x, AXES, pairs)  13 us
  transfers between devices with their start and end apart: 12, of which 12 were waited for; matrix products, arithmetic and copies ran while one was open for 0% of the time, Pallas kernels for 0%

profile of v5, /device:TPU:1, one launch (start us, length us, event | category | flops | bytes accessed | tf_op | source)
XLA Modules:
  0.0 151.2 jit_solution(3161376427763142524)
XLA Ops:
  0.7 3.6 %shard_map.122 = (f32[416,128]{1,0:T(8,128)}, f32[37,8,256]{2,1,0:T(8,128)}) custom-call(s32[32]{0:T(128)} %count_ref.5, s32[32]{0:T(128)} %type_ref.5, s32[32]{0:T(128)} %window_ref.5, s32[4,4096]{1,0:T(4,128)} %refs_1_.5, f32[4,4096]{1,0:T(4,128)} %refs_2_.3, f32[32,128]{1,0:T(8,128)} %bitcast.40, f32[32,128]{1,0:T(8,128)} %bitcast.47, ...), custom_call_target="tpu_custom_call" | custom-call | tf_op jit(solution)/shard_map/pallas_call | solution.py:641
  4.3 15.9 %all_to_all.25 = f32[416,1,128]{2,1,0:T(1,128)S(1)} all-to-all(f32[416,1,128]{2,1,0:T(1,128)} %bitcast.43), channel_id=1, replica_groups=mesh['lat'=4,'lon'=8] {'lat','lon'}, dimensions={0} | all-to-all | bytes 425984 | tf_op jit(solution)/shard_map/all_to_all | solution.py:689
  20.2 1.0 copy-done.2
  21.2 1.7 %shard_map.123 = (f32[56,8,256]{2,1,0:T(8,128)S(1)}, f32[8,512]{1,0:T(8,128)S(1)}, f32[8,512]{1,0:T(8,128)S(1)}, f32[8,128]{1,0:T(8,128)}) custom-call(f32[416,128]{1,0:T(8,128)S(1)} %bitcast.34, f32[37,8,256]{2,1,0:T(8,128)S(1)} %copy-done.2), custom_call_target="tpu_custom_call" | custom-call | tf_op jit(solution)/shard_map/pallas_call | solution.py:641
  22.9 1.9 %collective-permute-start = (f32[8,512]{1,0:T(8,128)S(1)}, f32[8,512]{1,0:T(8,128)S(1)}, u32[]{:S(2)}, u32[]{:S(2)}) collective-permute-start(f32[8,512]{1,0:T(8,128)S(1)} %get-tuple-element.36), channel_id=1, source_target_pairs={{0,7},{1,0},{2,1},{3,2},{4,3},{5,4},{6,5},{7,6},{8,15},{9,8},{10,9... | collective-permute-start | bytes 49160 | tf_op jit(solution)/shard_map/ppermute | solution.py:698
  24.8 0.9 collective-permute-done.east_ref.refs_3_
  25.7 4.4 %collective-permute-done.1.west_ref.refs_4_ = f32[8,512]{1,0:T(8,128)S(1)} collective-permute-done((f32[8,512]{1,0:T(8,128)S(1)}, f32[8,512]{1,0:T(8,128)S(1)}, u32[]{:S(2)}, u32[]{:S(2)}) %collective-permute-start.1) | collective-permute-done | bytes 16416 | tf_op jit(solution)/shard_map/ppermute | solution.py:698
  30.1 2.3 %collective-permute-start.2 = (f32[54,8,256]{2,1,0:T(8,128)S(1)}, f32[54,8,256]{2,1,0:T(8,128)S(1)}, u32[]{:S(2)}, u32[]{:S(2)}) collective-permute-start(f32[54,8,256]{2,1,0:T(8,128)S(1)} %get-tuple-element.38), channel_id=1, source_target_pairs={{0,8},{1,9},{2,10},{3,11},{4,12},{5,13},{6,14},{7,15},{8,16},{9,17... | collective-permute-start | bytes 1327112 | tf_op jit(solution)/shard_map/ppermute | solution.py:698
  32.7 7.9 %collective-permute-done.2.refs_0_ = f32[54,8,256]{2,1,0:T(8,128)S(1)} collective-permute-done((f32[54,8,256]{2,1,0:T(8,128)S(1)}, f32[54,8,256]{2,1,0:T(8,128)S(1)}, u32[]{:S(2)}, u32[]{:S(2)}) %collective-permute-start.2) | collective-permute-done | bytes 442400 | tf_op jit(solution)/shard_map/ppermute | solution.py:698
  40.6 3.6 %collective-permute-done.3.refs_2_ = f32[54,8,256]{2,1,0:T(8,128)S(1)} collective-permute-done((f32[54,8,256]{2,1,0:T(8,128)S(1)}, f32[54,8,256]{2,1,0:T(8,128)S(1)}, u32[]{:S(2)}, u32[]{:S(2)}) %collective-permute-start.3) | collective-permute-done | bytes 442400 | tf_op jit(solution)/shard_map/ppermute | solution.py:698
  44.2 10.2 %shard_map.125 = (f32[416,128]{1,0:T(8,128)S(1)}, f32[16,64,384]{2,1,0:T(8,128)S(1)}, f32[2,24,16,384]{3,2,1,0:T(8,128)S(1)}) custom-call(s32[2]{0:T(128)S(1)} %add_convert_fusion.edge_ref, f32[54,8,256]{2,1,0:T(8,128)S(1)} %collective-permute-done.2.refs_0_, f32[56,8,256]{2,1,0:T(8,128)S(1)} %get-tuple-element.35.main_ref.refs_1_, ...), custom_call_target="tpu_custom_call" | custom-call | tf_op jit(solution)/shard_map/pallas_call | solution.py:641
  54.3 10.2 %all_to_all.26 = f32[416,1,128]{2,1,0:T(1,128)S(1)} all-to-all(f32[416,1,128]{2,1,0:T(1,128)S(1)} %bitcast.36), channel_id=1, replica_groups=mesh['lat'=4,'lon'=8] {'lat','lon'}, dimensions={0} | all-to-all | bytes 425984 | tf_op jit(solution)/shard_map/all_to_all | solution.py:689
  64.6 3.4 %shard_map.126 = (f32[416,128]{1,0:T(8,128)S(1)}, f32[32,128]{1,0:T(8,128)S(1)}, f32[8,128]{1,0:T(8,128)S(1)}) custom-call(s32[32]{0:T(128)S(1)} %copy-done.5, s32[32]{0:T(128)S(1)} %copy-done.6, s32[32]{0:T(128)S(1)} %copy-done.7, f32[416,128]{1,0:T(8,128)S(1)} %bitcast.35, s32[4,4096]{1,0:T(4,128)S(1)} %copy-done, f32[4,4096]{1,0:T(4,128)S(1)} %copy-done.1, ...), custom_call_target="tpu_custom_call" | custom-call | tf_op jit(solution)/shard_map/pallas_call | solution.py:641
  67.9 11.6 %all_to_all.27 = f32[416,1,128]{2,1,0:T(1,128)S(1)} all-to-all(f32[416,1,128]{2,1,0:T(1,128)S(1)} %bitcast.39), channel_id=1, replica_groups=mesh['lat'=4,'lon'=8] {'lat','lon'}, dimensions={0} | all-to-all | bytes 425984 | tf_op jit(solution)/shard_map/all_to_all | solution.py:689
  79.6 1.1 shard_map.127
  80.7 2.0 %collective-permute-start.4 = (f32[8,256]{1,0:T(8,128)S(1)}, f32[8,256]{1,0:T(8,128)S(1)}, u32[]{:S(2)}, u32[]{:S(2)}) collective-permute-start(f32[8,256]{1,0:T(8,128)S(1)} %get-tuple-element.43), channel_id=1, source_target_pairs={{0,7},{1,0},{2,1},{3,2},{4,3},{5,4},{6,5},{7,6},{8,15},{9,8},{10,9... | collective-permute-start | bytes 24584 | tf_op jit(solution)/shard_map/ppermute | solution.py:698
  82.6 0.8 collective-permute-done.4.east_ref.refs_3_
  83.4 4.4 %collective-permute-done.5.west_ref.refs_4_ = f32[8,256]{1,0:T(8,128)S(1)} collective-permute-done((f32[8,256]{1,0:T(8,128)S(1)}, f32[8,256]{1,0:T(8,128)S(1)}, u32[]{:S(2)}, u32[]{:S(2)}) %collective-permute-start.5) | collective-permute-done | bytes 8224 | tf_op jit(solution)/shard_map/ppermute | solution.py:698
  87.9 2.3 %collective-permute-start.6 = (f32[20,8,256]{2,1,0:T(8,128)S(1)}, f32[20,8,256]{2,1,0:T(8,128)S(1)}, u32[]{:S(2)}, u32[]{:S(2)}) collective-permute-start(f32[20,8,256]{2,1,0:T(8,128)S(1)} %get-tuple-element.45), channel_id=1, source_target_pairs={{0,8},{1,9},{2,10},{3,11},{4,12},{5,13},{6,14},{7,15},{8,16},{9,17... | collective-permute-start | bytes 491528 | tf_op jit(solution)/shard_map/ppermute | solution.py:698
  90.3 2.1 %collective-permute-done.6.refs_0_ = f32[20,8,256]{2,1,0:T(8,128)S(1)} collective-permute-done((f32[20,8,256]{2,1,0:T(8,128)S(1)}, f32[20,8,256]{2,1,0:T(8,128)S(1)}, u32[]{:S(2)}, u32[]{:S(2)}) %collective-permute-start.6) | collective-permute-done | bytes 163872 | tf_op jit(solution)/shard_map/ppermute | solution.py:698
  92.4 3.5 %collective-permute-done.7.refs_2_ = f32[20,8,256]{2,1,0:T(8,128)S(1)} collective-permute-done((f32[20,8,256]{2,1,0:T(8,128)S(1)}, f32[20,8,256]{2,1,0:T(8,128)S(1)}, u32[]{:S(2)}, u32[]{:S(2)}) %collective-permute-start.7) | collective-permute-done | bytes 163872 | tf_op jit(solution)/shard_map/ppermute | solution.py:698
  95.9 10.3 %shard_map.129 = (f32[416,128]{1,0:T(8,128)S(1)}, f32[16,64,384]{2,1,0:T(8,128)S(1)}) custom-call(s32[2]{0:T(128)S(1)} %add_convert_fusion.edge_ref, f32[20,8,256]{2,1,0:T(8,128)S(1)} %collective-permute-done.6.refs_0_, f32[24,8,256]{2,1,0:T(8,128)S(1)} %get-tuple-element.42.main_ref.refs_1_, f32[20,8,256]{2,1,0:T(8,128)S(1)} %collective-permute-done.7.refs_2_, ...), custom_call_target="tpu_custom_call" | custom-call | tf_op jit(solution)/shard_map/pallas_call | solution.py:641
  106.2 10.2 %all_to_all.28 = f32[416,1,128]{2,1,0:T(1,128)S(1)} all-to-all(f32[416,1,128]{2,1,0:T(1,128)S(1)} %bitcast.37), channel_id=1, replica_groups=mesh['lat'=4,'lon'=8] {'lat','lon'}, dimensions={0} | all-to-all | bytes 425984 | tf_op jit(solution)/shard_map/all_to_all | solution.py:689
  116.3 3.8 %shard_map.130 = (f32[416,128]{1,0:T(8,128)S(1)}, f32[32,128]{1,0:T(8,128)}, f32[8,128]{1,0:T(8,128)S(1)}) custom-call(s32[32]{0:T(128)S(1)} %copy-done.5, s32[32]{0:T(128)S(1)} %copy-done.6, s32[32]{0:T(128)S(1)} %copy-done.7, f32[416,128]{1,0:T(8,128)S(1)} %bitcast.31, s32[4,4096]{1,0:T(4,128)S(1)} %copy-done, f32[4,4096]{1,0:T(4,128)S(1)} %copy-done.1, ...), custom_call_target="tpu_custom_call" | custom-call | tf_op jit(solution)/shard_map/pallas_call | solution.py:641
  120.2 11.6 %all_to_all.29 = f32[416,1,128]{2,1,0:T(1,128)S(1)} all-to-all(f32[416,1,128]{2,1,0:T(1,128)S(1)} %bitcast.38), channel_id=1, replica_groups=mesh['lat'=4,'lon'=8] {'lat','lon'}, dimensions={0} | all-to-all | bytes 425984 | tf_op jit(solution)/shard_map/all_to_all | solution.py:689
  131.8 1.1 shard_map.131
  132.9 2.0 %collective-permute-start.8 = (f32[8,256]{1,0:T(8,128)S(1)}, f32[8,256]{1,0:T(8,128)S(1)}, u32[]{:S(2)}, u32[]{:S(2)}) collective-permute-start(f32[8,256]{1,0:T(8,128)S(1)} %get-tuple-element.55), channel_id=1, source_target_pairs={{0,7},{1,0},{2,1},{3,2},{4,3},{5,4},{6,5},{7,6},{8,15},{9,8},{10,9... | collective-permute-start | bytes 24584 | tf_op jit(solution)/shard_map/ppermute | solution.py:698
  135.7 4.4 %collective-permute-done.9.west_ref.refs_4_ = f32[8,256]{1,0:T(8,128)S(1)} collective-permute-done((f32[8,256]{1,0:T(8,128)S(1)}, f32[8,256]{1,0:T(8,128)S(1)}, u32[]{:S(2)}, u32[]{:S(2)}) %collective-permute-start.9) | collective-permute-done | bytes 8224 | tf_op jit(solution)/shard_map/ppermute | solution.py:698
  140.1 2.3 %collective-permute-start.10 = (f32[8,8,256]{2,1,0:T(8,128)S(1)}, f32[8,8,256]{2,1,0:T(8,128)S(1)}, u32[]{:S(2)}, u32[]{:S(2)}) collective-permute-start(f32[8,8,256]{2,1,0:T(8,128)S(1)} %get-tuple-element.57), channel_id=1, source_target_pairs={{0,8},{1,9},{2,10},{3,11},{4,12},{5,13},{6,14},{7,15},{8,16},{9,17... | collective-permute-start | bytes 196616 | tf_op jit(solution)/shard_map/ppermute | solution.py:698
  142.4 1.3 collective-permute-done.10.refs_0_
  143.7 2.4 %collective-permute-done.11.refs_2_ = f32[8,8,256]{2,1,0:T(8,128)S(1)} collective-permute-done((f32[8,8,256]{2,1,0:T(8,128)S(1)}, f32[8,8,256]{2,1,0:T(8,128)S(1)}, u32[]{:S(2)}, u32[]{:S(2)}) %collective-permute-start.11) | collective-permute-done | bytes 65568 | tf_op jit(solution)/shard_map/ppermute | solution.py:698
  146.1 5.1 %shard_map.133 = (f32[512,256]{1,0:T(8,128)}, f32[512,256]{1,0:T(8,128)}) custom-call(s32[2]{0:T(128)S(1)} %add_convert_fusion.edge_ref, f32[8,8,256]{2,1,0:T(8,128)S(1)} %collective-permute-done.10.refs_0_, f32[24,8,256]{2,1,0:T(8,128)S(1)} %get-tuple-element.54.main_ref.refs_1_, f32[8,8,256]{2,1,0:T(8,128)S(1)} %collective-permute-done.11.refs_2_, ...), custom_call_target="tpu_custom_call" | custom-call | tf_op jit(solution)/shard_map/pallas_call | solution.py:641
  (32 shorter events, 1.3 us)
Async XLA Ops:
  0.6 43.5 %copy-start.3 = (s32[1,2048]{1,0:T(1,128)S(1)}, s32[1,2048]{1,0:T(1,128)}, u32[]{:S(2)}) copy-start(s32[1,2048]{1,0:T(1,128)} %send_ref.3) | copy-start | bytes 24580
  0.6 31.8 %copy-start.8 = (f32[8,64]{1,0:T(8,128)S(1)}, f32[8,64]{1,0:T(8,128)}, u32[]{:S(2)}) copy-start(f32[8,64]{1,0:T(8,128)} %param.13) | copy-start | bytes 6148
  4.3 60.2 %copy-start.4 = (f32[4096]{0:T(1024)S(1)}, f32[4096]{0:T(1024)}, u32[]{:S(2)}) copy-start(f32[4096]{0:T(1024)} %param.15) | copy-start | bytes 49156
  4.3 60.2 %copy-start.5 = (s32[32]{0:T(128)S(1)}, s32[32]{0:T(128)}, u32[]{:S(2)}) copy-start(s32[32]{0:T(128)} %count_ref.5) | copy-start | bytes 388
  4.3 60.2 %copy-start.6 = (s32[32]{0:T(128)S(1)}, s32[32]{0:T(128)}, u32[]{:S(2)}) copy-start(s32[32]{0:T(128)} %type_ref.5) | copy-start | bytes 388
  4.3 60.2 %copy-start.7 = (s32[32]{0:T(128)S(1)}, s32[32]{0:T(128)}, u32[]{:S(2)}) copy-start(s32[32]{0:T(128)} %window_ref.5) | copy-start | bytes 388
  20.2 44.3 %copy-start = (s32[4,4096]{1,0:T(4,128)S(1)}, s32[4,4096]{1,0:T(4,128)}, u32[]{:S(2)}) copy-start(s32[4,4096]{1,0:T(4,128)} %refs_1_.5) | copy-start | bytes 196612
  20.2 44.3 %copy-start.1 = (f32[4,4096]{1,0:T(4,128)S(1)}, f32[4,4096]{1,0:T(4,128)}, u32[]{:S(2)}) copy-start(f32[4,4096]{1,0:T(4,128)} %refs_2_.3) | copy-start | bytes 196612
  20.2 1.0 copy-start.2
  22.9 2.8 %collective-permute-start = (f32[8,512]{1,0:T(8,128)S(1)}, f32[8,512]{1,0:T(8,128)S(1)}, u32[]{:S(2)}, u32[]{:S(2)}) collective-permute-start(f32[8,512]{1,0:T(8,128)S(1)} %get-tuple-element.36), channel_id=1, source_target_pairs={{0,7},{1,0},{2,1},{3,2},{4,3},{5,4},{6,5},{7,6},{8,15},{9,8},{10,9... | collective-permute-start | bytes 49160 | tf_op jit(solution)/shard_map/ppermute | solution.py:698
  24.8 5.3 %collective-permute-start.1 = (f32[8,512]{1,0:T(8,128)S(1)}, f32[8,512]{1,0:T(8,128)S(1)}, u32[]{:S(2)}, u32[]{:S(2)}) collective-permute-start(f32[8,512]{1,0:T(8,128)S(1)} %get-tuple-element.37), channel_id=1, source_target_pairs={{0,1},{1,2},{2,3},{3,4},{4,5},{5,6},{6,7},{7,0},{8,9},{9,10},{10,1... | collective-permute-start | bytes 49160 | tf_op jit(solution)/shard_map/ppermute | solution.py:698
  30.1 10.4 %collective-permute-start.2 = (f32[54,8,256]{2,1,0:T(8,128)S(1)}, f32[54,8,256]{2,1,0:T(8,128)S(1)}, u32[]{:S(2)}, u32[]{:S(2)}) collective-permute-start(f32[54,8,256]{2,1,0:T(8,128)S(1)} %get-tuple-element.38), channel_id=1, source_target_pairs={{0,8},{1,9},{2,10},{3,11},{4,12},{5,13},{6,14},{7,15},{8,16},{9,17... | collective-permute-start | bytes 1327112 | tf_op jit(solution)/shard_map/ppermute | solution.py:698
  32.4 11.7 %collective-permute-start.3 = (f32[54,8,256]{2,1,0:T(8,128)S(1)}, f32[54,8,256]{2,1,0:T(8,128)S(1)}, u32[]{:S(2)}, u32[]{:S(2)}) collective-permute-start(f32[54,8,256]{2,1,0:T(8,128)S(1)} %get-tuple-element.39), channel_id=1, source_target_pairs={{0,24},{1,25},{2,26},{3,27},{4,28},{5,29},{6,30},{7,31},{8,0},{9,1... | collective-permute-start | bytes 1327112 | tf_op jit(solution)/shard_map/ppermute | solution.py:698
  80.7 2.8 %collective-permute-start.4 = (f32[8,256]{1,0:T(8,128)S(1)}, f32[8,256]{1,0:T(8,128)S(1)}, u32[]{:S(2)}, u32[]{:S(2)}) collective-permute-start(f32[8,256]{1,0:T(8,128)S(1)} %get-tuple-element.43), channel_id=1, source_target_pairs={{0,7},{1,0},{2,1},{3,2},{4,3},{5,4},{6,5},{7,6},{8,15},{9,8},{10,9... | collective-permute-start | bytes 24584 | tf_op jit(solution)/shard_map/ppermute | solution.py:698
  82.6 5.2 %collective-permute-start.5 = (f32[8,256]{1,0:T(8,128)S(1)}, f32[8,256]{1,0:T(8,128)S(1)}, u32[]{:S(2)}, u32[]{:S(2)}) collective-permute-start(f32[8,256]{1,0:T(8,128)S(1)} %get-tuple-element.44), channel_id=1, source_target_pairs={{0,1},{1,2},{2,3},{3,4},{4,5},{5,6},{6,7},{7,0},{8,9},{9,10},{10,1... | collective-permute-start | bytes 24584 | tf_op jit(solution)/shard_map/ppermute | solution.py:698
  87.9 4.6 %collective-permute-start.6 = (f32[20,8,256]{2,1,0:T(8,128)S(1)}, f32[20,8,256]{2,1,0:T(8,128)S(1)}, u32[]{:S(2)}, u32[]{:S(2)}) collective-permute-start(f32[20,8,256]{2,1,0:T(8,128)S(1)} %get-tuple-element.45), channel_id=1, source_target_pairs={{0,8},{1,9},{2,10},{3,11},{4,12},{5,13},{6,14},{7,15},{8,16},{9,17... | collective-permute-start | bytes 491528 | tf_op jit(solution)/shard_map/ppermute | solution.py:698
  90.2 5.7 %collective-permute-start.7 = (f32[20,8,256]{2,1,0:T(8,128)S(1)}, f32[20,8,256]{2,1,0:T(8,128)S(1)}, u32[]{:S(2)}, u32[]{:S(2)}) collective-permute-start(f32[20,8,256]{2,1,0:T(8,128)S(1)} %get-tuple-element.46), channel_id=1, source_target_pairs={{0,24},{1,25},{2,26},{3,27},{4,28},{5,29},{6,30},{7,31},{8,0},{9,1... | collective-permute-start | bytes 491528 | tf_op jit(solution)/shard_map/ppermute | solution.py:698
  132.9 2.8 %collective-permute-start.8 = (f32[8,256]{1,0:T(8,128)S(1)}, f32[8,256]{1,0:T(8,128)S(1)}, u32[]{:S(2)}, u32[]{:S(2)}) collective-permute-start(f32[8,256]{1,0:T(8,128)S(1)} %get-tuple-element.55), channel_id=1, source_target_pairs={{0,7},{1,0},{2,1},{3,2},{4,3},{5,4},{6,5},{7,6},{8,15},{9,8},{10,9... | collective-permute-start | bytes 24584 | tf_op jit(solution)/shard_map/ppermute | solution.py:698
  134.9 5.2 %collective-permute-start.9 = (f32[8,256]{1,0:T(8,128)S(1)}, f32[8,256]{1,0:T(8,128)S(1)}, u32[]{:S(2)}, u32[]{:S(2)}) collective-permute-start(f32[8,256]{1,0:T(8,128)S(1)} %get-tuple-element.56), channel_id=1, source_target_pairs={{0,1},{1,2},{2,3},{3,4},{4,5},{5,6},{6,7},{7,0},{8,9},{9,10},{10,1... | collective-permute-start | bytes 24584 | tf_op jit(solution)/shard_map/ppermute | solution.py:698
  140.1 3.7 %collective-permute-start.10 = (f32[8,8,256]{2,1,0:T(8,128)S(1)}, f32[8,8,256]{2,1,0:T(8,128)S(1)}, u32[]{:S(2)}, u32[]{:S(2)}) collective-permute-start(f32[8,8,256]{2,1,0:T(8,128)S(1)} %get-tuple-element.57), channel_id=1, source_target_pairs={{0,8},{1,9},{2,10},{3,11},{4,12},{5,13},{6,14},{7,15},{8,16},{9,17... | collective-permute-start | bytes 196616 | tf_op jit(solution)/shard_map/ppermute | solution.py:698
  142.4 3.7 %collective-permute-start.11 = (f32[8,8,256]{2,1,0:T(8,128)S(1)}, f32[8,8,256]{2,1,0:T(8,128)S(1)}, u32[]{:S(2)}, u32[]{:S(2)}) collective-permute-start(f32[8,8,256]{2,1,0:T(8,128)S(1)} %get-tuple-element.58), channel_id=1, source_target_pairs={{0,24},{1,25},{2,26},{3,27},{4,28},{5,29},{6,30},{7,31},{8,0},{9,1... | collective-permute-start | bytes 196616 | tf_op jit(solution)/shard_map/ppermute | solution.py:698

commit v6 on v5

--- a/solution.py
+++ b/solution.py
@@ -607,7 +607,7 @@
             tangent(old, e, put_in(new, e))
             return carry
 
-        loop(REACH + step, rows - REACH - step, 11, body)
+        loop(REACH + step, rows - REACH - step, 14, body)
         now = 1 - now
         if step % STEP_WIN == 0:
             look(fields[now], step // STEP_WIN)

time: 152 us -> 150 us (0.987)
  no operation moved by 1% of the time
where the time goes in v6:
time: 150 us
  blocking collectives  59.5 us (40%)
  Pallas kernels  39.3 us (26%)
  waiting for transfers between devices  36.4 us (24%)
  starting transfers between devices  13 us (9%)
    all_to_all x5, blocking collectives, exchange(): x = lax.all_to_all(x, AXES, split_axis=0, concat_axis=0, tiled=True)  59.5 us
    pallas_call x12, Pallas kernels, call(): pl.pallas_call(kernel, out_shape=[jax.ShapeDtypeStruct(s, F32) if isinsta...  39.3 us
    ppermute x12, waiting for transfers between devices, send(): return lax.ppermute(x, AXES, pairs)  36.4 us
    ppermute x12, starting transfers between devices, send(): return lax.ppermute(x, AXES, pairs)  13 us
  transfers between devices with their start and end apart: 12, of which 12 were waited for; matrix products, arithmetic and copies ran while one was open for 0% of the time, Pallas kernels for 0%

profile of v6, /device:TPU:1, one launch (start us, length us, event | category | flops | bytes accessed | tf_op | source)
XLA Modules:
  0.0 150.2 jit_solution(1283852476546701084)
XLA Ops:
  0.7 3.6 %shard_map.122 = (f32[416,128]{1,0:T(8,128)}, f32[37,8,256]{2,1,0:T(8,128)}) custom-call(s32[32]{0:T(128)} %count_ref.5, s32[32]{0:T(128)} %type_ref.5, s32[32]{0:T(128)} %window_ref.5, s32[4,4096]{1,0:T(4,128)} %refs_1_.5, f32[4,4096]{1,0:T(4,128)} %refs_2_.3, f32[32,128]{1,0:T(8,128)} %bitcast.40, f32[32,128]{1,0:T(8,128)} %bitcast.47, ...), custom_call_target="tpu_custom_call" | custom-call | tf_op jit(solution)/shard_map/pallas_call | solution.py:641
  4.3 15.9 %all_to_all.25 = f32[416,1,128]{2,1,0:T(1,128)S(1)} all-to-all(f32[416,1,128]{2,1,0:T(1,128)} %bitcast.43), channel_id=1, replica_groups=mesh['lat'=4,'lon'=8] {'lat','lon'}, dimensions={0} | all-to-all | bytes 425984 | tf_op jit(solution)/shard_map/all_to_all | solution.py:689
  20.2 1.0 copy-done.2
  21.2 1.7 %shard_map.123 = (f32[56,8,256]{2,1,0:T(8,128)S(1)}, f32[8,512]{1,0:T(8,128)S(1)}, f32[8,512]{1,0:T(8,128)S(1)}, f32[8,128]{1,0:T(8,128)}) custom-call(f32[416,128]{1,0:T(8,128)S(1)} %bitcast.34, f32[37,8,256]{2,1,0:T(8,128)S(1)} %copy-done.2), custom_call_target="tpu_custom_call" | custom-call | tf_op jit(solution)/shard_map/pallas_call | solution.py:641
  22.9 1.9 %collective-permute-start = (f32[8,512]{1,0:T(8,128)S(1)}, f32[8,512]{1,0:T(8,128)S(1)}, u32[]{:S(2)}, u32[]{:S(2)}) collective-permute-start(f32[8,512]{1,0:T(8,128)S(1)} %get-tuple-element.36), channel_id=1, source_target_pairs={{0,7},{1,0},{2,1},{3,2},{4,3},{5,4},{6,5},{7,6},{8,15},{9,8},{10,9... | collective-permute-start | bytes 49160 | tf_op jit(solution)/shard_map/ppermute | solution.py:698
  24.8 0.9 collective-permute-done.east_ref.refs_3_
  25.7 4.4 %collective-permute-done.1.west_ref.refs_4_ = f32[8,512]{1,0:T(8,128)S(1)} collective-permute-done((f32[8,512]{1,0:T(8,128)S(1)}, f32[8,512]{1,0:T(8,128)S(1)}, u32[]{:S(2)}, u32[]{:S(2)}) %collective-permute-start.1) | collective-permute-done | bytes 16416 | tf_op jit(solution)/shard_map/ppermute | solution.py:698
  30.1 2.3 %collective-permute-start.2 = (f32[54,8,256]{2,1,0:T(8,128)S(1)}, f32[54,8,256]{2,1,0:T(8,128)S(1)}, u32[]{:S(2)}, u32[]{:S(2)}) collective-permute-start(f32[54,8,256]{2,1,0:T(8,128)S(1)} %get-tuple-element.38), channel_id=1, source_target_pairs={{0,8},{1,9},{2,10},{3,11},{4,12},{5,13},{6,14},{7,15},{8,16},{9,17... | collective-permute-start | bytes 1327112 | tf_op jit(solution)/shard_map/ppermute | solution.py:698
  32.7 7.9 %collective-permute-done.2.refs_0_ = f32[54,8,256]{2,1,0:T(8,128)S(1)} collective-permute-done((f32[54,8,256]{2,1,0:T(8,128)S(1)}, f32[54,8,256]{2,1,0:T(8,128)S(1)}, u32[]{:S(2)}, u32[]{:S(2)}) %collective-permute-start.2) | collective-permute-done | bytes 442400 | tf_op jit(solution)/shard_map/ppermute | solution.py:698
  40.6 3.6 %collective-permute-done.3.refs_2_ = f32[54,8,256]{2,1,0:T(8,128)S(1)} collective-permute-done((f32[54,8,256]{2,1,0:T(8,128)S(1)}, f32[54,8,256]{2,1,0:T(8,128)S(1)}, u32[]{:S(2)}, u32[]{:S(2)}) %collective-permute-start.3) | collective-permute-done | bytes 442400 | tf_op jit(solution)/shard_map/ppermute | solution.py:698
  44.2 9.7 %shard_map.125 = (f32[416,128]{1,0:T(8,128)S(1)}, f32[16,64,384]{2,1,0:T(8,128)S(1)}, f32[2,24,16,384]{3,2,1,0:T(8,128)S(1)}) custom-call(s32[2]{0:T(128)S(1)} %add_convert_fusion.edge_ref, f32[54,8,256]{2,1,0:T(8,128)S(1)} %collective-permute-done.2.refs_0_, f32[56,8,256]{2,1,0:T(8,128)S(1)} %get-tuple-element.35.main_ref.refs_1_, ...), custom_call_target="tpu_custom_call" | custom-call | tf_op jit(solution)/shard_map/pallas_call | solution.py:641
  53.8 10.2 %all_to_all.26 = f32[416,1,128]{2,1,0:T(1,128)S(1)} all-to-all(f32[416,1,128]{2,1,0:T(1,128)S(1)} %bitcast.36), channel_id=1, replica_groups=mesh['lat'=4,'lon'=8] {'lat','lon'}, dimensions={0} | all-to-all | bytes 425984 | tf_op jit(solution)/shard_map/all_to_all | solution.py:689
  64.0 3.4 %shard_map.126 = (f32[416,128]{1,0:T(8,128)S(1)}, f32[32,128]{1,0:T(8,128)S(1)}, f32[8,128]{1,0:T(8,128)S(1)}) custom-call(s32[32]{0:T(128)S(1)} %copy-done.5, s32[32]{0:T(128)S(1)} %copy-done.6, s32[32]{0:T(128)S(1)} %copy-done.7, f32[416,128]{1,0:T(8,128)S(1)} %bitcast.35, s32[4,4096]{1,0:T(4,128)S(1)} %copy-done, f32[4,4096]{1,0:T(4,128)S(1)} %copy-done.1, ...), custom_call_target="tpu_custom_call" | custom-call | tf_op jit(solution)/shard_map/pallas_call | solution.py:641
  67.4 11.6 %all_to_all.27 = f32[416,1,128]{2,1,0:T(1,128)S(1)} all-to-all(f32[416,1,128]{2,1,0:T(1,128)S(1)} %bitcast.39), channel_id=1, replica_groups=mesh['lat'=4,'lon'=8] {'lat','lon'}, dimensions={0} | all-to-all | bytes 425984 | tf_op jit(solution)/shard_map/all_to_all | solution.py:689
  79.0 1.1 shard_map.127
  80.2 2.0 %collective-permute-start.4 = (f32[8,256]{1,0:T(8,128)S(1)}, f32[8,256]{1,0:T(8,128)S(1)}, u32[]{:S(2)}, u32[]{:S(2)}) collective-permute-start(f32[8,256]{1,0:T(8,128)S(1)} %get-tuple-element.43), channel_id=1, source_target_pairs={{0,7},{1,0},{2,1},{3,2},{4,3},{5,4},{6,5},{7,6},{8,15},{9,8},{10,9... | collective-permute-start | bytes 24584 | tf_op jit(solution)/shard_map/ppermute | solution.py:698
  82.1 0.8 collective-permute-done.4.east_ref.refs_3_
  82.9 4.4 %collective-permute-done.5.west_ref.refs_4_ = f32[8,256]{1,0:T(8,128)S(1)} collective-permute-done((f32[8,256]{1,0:T(8,128)S(1)}, f32[8,256]{1,0:T(8,128)S(1)}, u32[]{:S(2)}, u32[]{:S(2)}) %collective-permute-start.5) | collective-permute-done | bytes 8224 | tf_op jit(solution)/shard_map/ppermute | solution.py:698
  87.3 2.3 %collective-permute-start.6 = (f32[20,8,256]{2,1,0:T(8,128)S(1)}, f32[20,8,256]{2,1,0:T(8,128)S(1)}, u32[]{:S(2)}, u32[]{:S(2)}) collective-permute-start(f32[20,8,256]{2,1,0:T(8,128)S(1)} %get-tuple-element.45), channel_id=1, source_target_pairs={{0,8},{1,9},{2,10},{3,11},{4,12},{5,13},{6,14},{7,15},{8,16},{9,17... | collective-permute-start | bytes 491528 | tf_op jit(solution)/shard_map/ppermute | solution.py:698
  89.8 2.1 %collective-permute-done.6.refs_0_ = f32[20,8,256]{2,1,0:T(8,128)S(1)} collective-permute-done((f32[20,8,256]{2,1,0:T(8,128)S(1)}, f32[20,8,256]{2,1,0:T(8,128)S(1)}, u32[]{:S(2)}, u32[]{:S(2)}) %collective-permute-start.6) | collective-permute-done | bytes 163872 | tf_op jit(solution)/shard_map/ppermute | solution.py:698
  91.9 3.5 %collective-permute-done.7.refs_2_ = f32[20,8,256]{2,1,0:T(8,128)S(1)} collective-permute-done((f32[20,8,256]{2,1,0:T(8,128)S(1)}, f32[20,8,256]{2,1,0:T(8,128)S(1)}, u32[]{:S(2)}, u32[]{:S(2)}) %collective-permute-start.7) | collective-permute-done | bytes 163872 | tf_op jit(solution)/shard_map/ppermute | solution.py:698
  95.4 9.8 %shard_map.129 = (f32[416,128]{1,0:T(8,128)S(1)}, f32[16,64,384]{2,1,0:T(8,128)S(1)}) custom-call(s32[2]{0:T(128)S(1)} %add_convert_fusion.edge_ref, f32[20,8,256]{2,1,0:T(8,128)S(1)} %collective-permute-done.6.refs_0_, f32[24,8,256]{2,1,0:T(8,128)S(1)} %get-tuple-element.42.main_ref.refs_1_, f32[20,8,256]{2,1,0:T(8,128)S(1)} %collective-permute-done.7.refs_2_, ...), custom_call_target="tpu_custom_call" | custom-call | tf_op jit(solution)/shard_map/pallas_call | solution.py:641
  105.2 10.1 %all_to_all.28 = f32[416,1,128]{2,1,0:T(1,128)S(1)} all-to-all(f32[416,1,128]{2,1,0:T(1,128)S(1)} %bitcast.37), channel_id=1, replica_groups=mesh['lat'=4,'lon'=8] {'lat','lon'}, dimensions={0} | all-to-all | bytes 425984 | tf_op jit(solution)/shard_map/all_to_all | solution.py:689
  115.3 3.8 %shard_map.130 = (f32[416,128]{1,0:T(8,128)S(1)}, f32[32,128]{1,0:T(8,128)}, f32[8,128]{1,0:T(8,128)S(1)}) custom-call(s32[32]{0:T(128)S(1)} %copy-done.5, s32[32]{0:T(128)S(1)} %copy-done.6, s32[32]{0:T(128)S(1)} %copy-done.7, f32[416,128]{1,0:T(8,128)S(1)} %bitcast.31, s32[4,4096]{1,0:T(4,128)S(1)} %copy-done, f32[4,4096]{1,0:T(4,128)S(1)} %copy-done.1, ...), custom_call_target="tpu_custom_call" | custom-call | tf_op jit(solution)/shard_map/pallas_call | solution.py:641
  119.2 11.6 %all_to_all.29 = f32[416,1,128]{2,1,0:T(1,128)S(1)} all-to-all(f32[416,1,128]{2,1,0:T(1,128)S(1)} %bitcast.38), channel_id=1, replica_groups=mesh['lat'=4,'lon'=8] {'lat','lon'}, dimensions={0} | all-to-all | bytes 425984 | tf_op jit(solution)/shard_map/all_to_all | solution.py:689
  130.8 1.1 shard_map.131
  131.9 2.0 %collective-permute-start.8 = (f32[8,256]{1,0:T(8,128)S(1)}, f32[8,256]{1,0:T(8,128)S(1)}, u32[]{:S(2)}, u32[]{:S(2)}) collective-permute-start(f32[8,256]{1,0:T(8,128)S(1)} %get-tuple-element.55), channel_id=1, source_target_pairs={{0,7},{1,0},{2,1},{3,2},{4,3},{5,4},{6,5},{7,6},{8,15},{9,8},{10,9... | collective-permute-start | bytes 24584 | tf_op jit(solution)/shard_map/ppermute | solution.py:698
  134.7 4.4 %collective-permute-done.9.west_ref.refs_4_ = f32[8,256]{1,0:T(8,128)S(1)} collective-permute-done((f32[8,256]{1,0:T(8,128)S(1)}, f32[8,256]{1,0:T(8,128)S(1)}, u32[]{:S(2)}, u32[]{:S(2)}) %collective-permute-start.9) | collective-permute-done | bytes 8224 | tf_op jit(solution)/shard_map/ppermute | solution.py:698
  139.1 2.3 %collective-permute-start.10 = (f32[8,8,256]{2,1,0:T(8,128)S(1)}, f32[8,8,256]{2,1,0:T(8,128)S(1)}, u32[]{:S(2)}, u32[]{:S(2)}) collective-permute-start(f32[8,8,256]{2,1,0:T(8,128)S(1)} %get-tuple-element.57), channel_id=1, source_target_pairs={{0,8},{1,9},{2,10},{3,11},{4,12},{5,13},{6,14},{7,15},{8,16},{9,17... | collective-permute-start | bytes 196616 | tf_op jit(solution)/shard_map/ppermute | solution.py:698
  141.4 1.3 collective-permute-done.10.refs_0_
  142.7 2.4 %collective-permute-done.11.refs_2_ = f32[8,8,256]{2,1,0:T(8,128)S(1)} collective-permute-done((f32[8,8,256]{2,1,0:T(8,128)S(1)}, f32[8,8,256]{2,1,0:T(8,128)S(1)}, u32[]{:S(2)}, u32[]{:S(2)}) %collective-permute-start.11) | collective-permute-done | bytes 65568 | tf_op jit(solution)/shard_map/ppermute | solution.py:698
  145.1 5.1 %shard_map.133 = (f32[512,256]{1,0:T(8,128)}, f32[512,256]{1,0:T(8,128)}) custom-call(s32[2]{0:T(128)S(1)} %add_convert_fusion.edge_ref, f32[8,8,256]{2,1,0:T(8,128)S(1)} %collective-permute-done.10.refs_0_, f32[24,8,256]{2,1,0:T(8,128)S(1)} %get-tuple-element.54.main_ref.refs_1_, f32[8,8,256]{2,1,0:T(8,128)S(1)} %collective-permute-done.11.refs_2_, ...), custom_call_target="tpu_custom_call" | custom-call | tf_op jit(solution)/shard_map/pallas_call | solution.py:641
  (32 shorter events, 1.3 us)
Async XLA Ops:
  0.6 43.5 %copy-start.3 = (s32[1,2048]{1,0:T(1,128)S(1)}, s32[1,2048]{1,0:T(1,128)}, u32[]{:S(2)}) copy-start(s32[1,2048]{1,0:T(1,128)} %send_ref.3) | copy-start | bytes 24580
  0.6 31.8 %copy-start.8 = (f32[8,64]{1,0:T(8,128)S(1)}, f32[8,64]{1,0:T(8,128)}, u32[]{:S(2)}) copy-start(f32[8,64]{1,0:T(8,128)} %param.13) | copy-start | bytes 6148
  4.3 59.7 %copy-start.4 = (f32[4096]{0:T(1024)S(1)}, f32[4096]{0:T(1024)}, u32[]{:S(2)}) copy-start(f32[4096]{0:T(1024)} %param.15) | copy-start | bytes 49156
  4.3 59.7 %copy-start.5 = (s32[32]{0:T(128)S(1)}, s32[32]{0:T(128)}, u32[]{:S(2)}) copy-start(s32[32]{0:T(128)} %count_ref.5) | copy-start | bytes 388
  4.3 59.7 %copy-start.6 = (s32[32]{0:T(128)S(1)}, s32[32]{0:T(128)}, u32[]{:S(2)}) copy-start(s32[32]{0:T(128)} %type_ref.5) | copy-start | bytes 388
  4.3 59.7 %copy-start.7 = (s32[32]{0:T(128)S(1)}, s32[32]{0:T(128)}, u32[]{:S(2)}) copy-start(s32[32]{0:T(128)} %window_ref.5) | copy-start | bytes 388
  20.2 43.8 %copy-start = (s32[4,4096]{1,0:T(4,128)S(1)}, s32[4,4096]{1,0:T(4,128)}, u32[]{:S(2)}) copy-start(s32[4,4096]{1,0:T(4,128)} %refs_1_.5) | copy-start | bytes 196612
  20.2 43.8 %copy-start.1 = (f32[4,4096]{1,0:T(4,128)S(1)}, f32[4,4096]{1,0:T(4,128)}, u32[]{:S(2)}) copy-start(f32[4,4096]{1,0:T(4,128)} %refs_2_.3) | copy-start | bytes 196612
  20.2 1.0 copy-start.2
  22.9 2.8 %collective-permute-start = (f32[8,512]{1,0:T(8,128)S(1)}, f32[8,512]{1,0:T(8,128)S(1)}, u32[]{:S(2)}, u32[]{:S(2)}) collective-permute-start(f32[8,512]{1,0:T(8,128)S(1)} %get-tuple-element.36), channel_id=1, source_target_pairs={{0,7},{1,0},{2,1},{3,2},{4,3},{5,4},{6,5},{7,6},{8,15},{9,8},{10,9... | collective-permute-start | bytes 49160 | tf_op jit(solution)/shard_map/ppermute | solution.py:698
  24.8 5.3 %collective-permute-start.1 = (f32[8,512]{1,0:T(8,128)S(1)}, f32[8,512]{1,0:T(8,128)S(1)}, u32[]{:S(2)}, u32[]{:S(2)}) collective-permute-start(f32[8,512]{1,0:T(8,128)S(1)} %get-tuple-element.37), channel_id=1, source_target_pairs={{0,1},{1,2},{2,3},{3,4},{4,5},{5,6},{6,7},{7,0},{8,9},{9,10},{10,1... | collective-permute-start | bytes 49160 | tf_op jit(solution)/shard_map/ppermute | solution.py:698
  30.1 10.4 %collective-permute-start.2 = (f32[54,8,256]{2,1,0:T(8,128)S(1)}, f32[54,8,256]{2,1,0:T(8,128)S(1)}, u32[]{:S(2)}, u32[]{:S(2)}) collective-permute-start(f32[54,8,256]{2,1,0:T(8,128)S(1)} %get-tuple-element.38), channel_id=1, source_target_pairs={{0,8},{1,9},{2,10},{3,11},{4,12},{5,13},{6,14},{7,15},{8,16},{9,17... | collective-permute-start | bytes 1327112 | tf_op jit(solution)/shard_map/ppermute | solution.py:698
  32.4 11.7 %collective-permute-start.3 = (f32[54,8,256]{2,1,0:T(8,128)S(1)}, f32[54,8,256]{2,1,0:T(8,128)S(1)}, u32[]{:S(2)}, u32[]{:S(2)}) collective-permute-start(f32[54,8,256]{2,1,0:T(8,128)S(1)} %get-tuple-element.39), channel_id=1, source_target_pairs={{0,24},{1,25},{2,26},{3,27},{4,28},{5,29},{6,30},{7,31},{8,0},{9,1... | collective-permute-start | bytes 1327112 | tf_op jit(solution)/shard_map/ppermute | solution.py:698
  80.2 2.8 %collective-permute-start.4 = (f32[8,256]{1,0:T(8,128)S(1)}, f32[8,256]{1,0:T(8,128)S(1)}, u32[]{:S(2)}, u32[]{:S(2)}) collective-permute-start(f32[8,256]{1,0:T(8,128)S(1)} %get-tuple-element.43), channel_id=1, source_target_pairs={{0,7},{1,0},{2,1},{3,2},{4,3},{5,4},{6,5},{7,6},{8,15},{9,8},{10,9... | collective-permute-start | bytes 24584 | tf_op jit(solution)/shard_map/ppermute | solution.py:698
  82.1 5.2 %collective-permute-start.5 = (f32[8,256]{1,0:T(8,128)S(1)}, f32[8,256]{1,0:T(8,128)S(1)}, u32[]{:S(2)}, u32[]{:S(2)}) collective-permute-start(f32[8,256]{1,0:T(8,128)S(1)} %get-tuple-element.44), channel_id=1, source_target_pairs={{0,1},{1,2},{2,3},{3,4},{4,5},{5,6},{6,7},{7,0},{8,9},{9,10},{10,1... | collective-permute-start | bytes 24584 | tf_op jit(solution)/shard_map/ppermute | solution.py:698
  87.3 4.6 %collective-permute-start.6 = (f32[20,8,256]{2,1,0:T(8,128)S(1)}, f32[20,8,256]{2,1,0:T(8,128)S(1)}, u32[]{:S(2)}, u32[]{:S(2)}) collective-permute-start(f32[20,8,256]{2,1,0:T(8,128)S(1)} %get-tuple-element.45), channel_id=1, source_target_pairs={{0,8},{1,9},{2,10},{3,11},{4,12},{5,13},{6,14},{7,15},{8,16},{9,17... | collective-permute-start | bytes 491528 | tf_op jit(solution)/shard_map/ppermute | solution.py:698
  89.7 5.7 %collective-permute-start.7 = (f32[20,8,256]{2,1,0:T(8,128)S(1)}, f32[20,8,256]{2,1,0:T(8,128)S(1)}, u32[]{:S(2)}, u32[]{:S(2)}) collective-permute-start(f32[20,8,256]{2,1,0:T(8,128)S(1)} %get-tuple-element.46), channel_id=1, source_target_pairs={{0,24},{1,25},{2,26},{3,27},{4,28},{5,29},{6,30},{7,31},{8,0},{9,1... | collective-permute-start | bytes 491528 | tf_op jit(solution)/shard_map/ppermute | solution.py:698
  131.9 2.8 %collective-permute-start.8 = (f32[8,256]{1,0:T(8,128)S(1)}, f32[8,256]{1,0:T(8,128)S(1)}, u32[]{:S(2)}, u32[]{:S(2)}) collective-permute-start(f32[8,256]{1,0:T(8,128)S(1)} %get-tuple-element.55), channel_id=1, source_target_pairs={{0,7},{1,0},{2,1},{3,2},{4,3},{5,4},{6,5},{7,6},{8,15},{9,8},{10,9... | collective-permute-start | bytes 24584 | tf_op jit(solution)/shard_map/ppermute | solution.py:698
  133.9 5.2 %collective-permute-start.9 = (f32[8,256]{1,0:T(8,128)S(1)}, f32[8,256]{1,0:T(8,128)S(1)}, u32[]{:S(2)}, u32[]{:S(2)}) collective-permute-start(f32[8,256]{1,0:T(8,128)S(1)} %get-tuple-element.56), channel_id=1, source_target_pairs={{0,1},{1,2},{2,3},{3,4},{4,5},{5,6},{6,7},{7,0},{8,9},{9,10},{10,1... | collective-permute-start | bytes 24584 | tf_op jit(solution)/shard_map/ppermute | solution.py:698
  139.1 3.6 %collective-permute-start.10 = (f32[8,8,256]{2,1,0:T(8,128)S(1)}, f32[8,8,256]{2,1,0:T(8,128)S(1)}, u32[]{:S(2)}, u32[]{:S(2)}) collective-permute-start(f32[8,8,256]{2,1,0:T(8,128)S(1)} %get-tuple-element.57), channel_id=1, source_target_pairs={{0,8},{1,9},{2,10},{3,11},{4,12},{5,13},{6,14},{7,15},{8,16},{9,17... | collective-permute-start | bytes 196616 | tf_op jit(solution)/shard_map/ppermute | solution.py:698
  141.4 3.7 %collective-permute-start.11 = (f32[8,8,256]{2,1,0:T(8,128)S(1)}, f32[8,8,256]{2,1,0:T(8,128)S(1)}, u32[]{:S(2)}, u32[]{:S(2)}) collective-permute-start(f32[8,8,256]{2,1,0:T(8,128)S(1)} %get-tuple-element.58), channel_id=1, source_target_pairs={{0,24},{1,25},{2,26},{3,27},{4,28},{5,29},{6,30},{7,31},{8,0},{9,1... | collective-permute-start | bytes 196616 | tf_op jit(solution)/shard_map/ppermute | solution.py:698
